TPU v7x, 128 devices: a whole 4x4x4 slice. The times are simulated.
128 devices in a mesh: data: 1, chip: 2 (over core), dap: 64 (over z, y, x).
Axes of the slice: x: 4, y: 4, z: 4, core: 2. Of those that a mesh axis runs over, the one named last changes fastest.
Arguments:
- m: bfloat16 [2048, 128, 256], P(('data', 'chip', 'dap'))
- z: bfloat16 [128, 128, 128], P(('data', 'chip', 'dap'))
- msa_mask: int32 [2048, 128], P('data')
- res_mask: int32 [128], P('data')
- w_row_in: bfloat16 [256, 1024], replicated
- w_row_bias: bfloat16 [128, 8], replicated
- w_row_out: bfloat16 [256, 256], replicated
- w_col_in: bfloat16 [256, 1024], replicated
- w_col_out: bfloat16 [256, 256], replicated
- w_opm_in: bfloat16 [256, 64], replicated
- w_opm_out: bfloat16 [1024, 128], replicated
- w_start_in: bfloat16 [128, 512], replicated
- w_start_bias: bfloat16 [128, 4], replicated
- w_start_out: bfloat16 [128, 128], replicated
- w_end_in: bfloat16 [128, 512], replicated
- w_end_bias: bfloat16 [128, 4], replicated
- w_end_out: bfloat16 [128, 128], replicated
Outputs:
- output 1: bfloat16 [2048, 128, 256], P(('data', 'chip', 'dap'))
- output 2: bfloat16 [128, 128, 128], P(('data', 'chip', 'dap'))
All inputs are finite; a program needn't handle non-finite values.
Results may differ from a plain program's by a relative error of at most 0.0148384.
Values are sent between devices in bfloat16 or wider.
A program may use at most 1 GiB of HBM per device.

v0:
```python
import jax
import jax.numpy as jnp
from jax import lax
from jax.sharding import PartitionSpec as P


def layer_norm(x):
    values = x.astype(jnp.float32)
    centred = values - jnp.mean(values, axis=-1, keepdims=True)
    variance = jnp.mean(centred * centred, axis=-1, keepdims=True)
    return (centred * lax.rsqrt(variance + 1e-5)).astype(jnp.bfloat16)


def add_residual(state, update):
    return (state.astype(jnp.float32) + update).astype(jnp.bfloat16)


def gated_attention(x_norm, w_in, w_out, heads, head_bias, key_ok, along_first):
    width = x_norm.shape[-1]
    head_dim = w_out.shape[0] // heads
    w_heads = jnp.transpose(w_in.reshape(width, 4, heads, head_dim), (2, 0, 1, 3))
    w_back = w_out.reshape(heads, head_dim, w_out.shape[1])
    if along_first:
        forms = ('nbc,cfd->nbfd', 'ibd,jbd->bij', 'bij,jbd->ibd', 'hibd,hdc->ibc')
    else:
        forms = ('bnc,cfd->bnfd', 'bid,bjd->bij', 'bij,bjd->bid', 'hbid,hdc->bic')
    key_keep = key_ok[:, None, :]
    scale = head_dim ** -0.5

    def one_head(head_in):
        projected = jnp.einsum(forms[0], x_norm, head_in[0], preferred_element_type=jnp.float32).astype(jnp.bfloat16)
        scores = jnp.einsum(forms[1], projected[:, :, 0], projected[:, :, 1], preferred_element_type=jnp.float32) * scale
        if len(head_in) > 1:
            scores = scores + head_in[1].astype(jnp.float32)[None]
        scores = jnp.where(key_keep, scores, -1e9)
        attn_prob = jax.nn.softmax(scores, axis=-1).astype(jnp.bfloat16)
        mixed = jnp.einsum(forms[2], attn_prob, projected[:, :, 2], preferred_element_type=jnp.float32)
        return (mixed * jax.nn.sigmoid(projected[:, :, 3].astype(jnp.float32))).astype(jnp.bfloat16)

    head_in = (w_heads,) if head_bias is None else (w_heads, head_bias)
    gated = lax.map(one_head, head_in)
    return jnp.einsum(forms[3], gated, w_back, preferred_element_type=jnp.float32)


def solution(mesh):
    dap_size = mesh.shape['dap']
    group = ('chip', 'dap')
    rows = P(('data', 'chip', 'dap'))
    in_specs = (rows, rows, P('data'), P('data')) + (P(),) * 13

    def per_device(m_blk, z_blk, value_a8, res_mask, w_row_in, w_row_bias, w_row_out, w_col_in, w_col_out,
                   w_opm_in, w_opm_out, w_start_in, w_start_bias, w_start_out, w_end_in, w_end_bias, w_end_out):
        group_idx = lax.axis_index('chip') * dap_size + lax.axis_index('dap')
        seq_loc = m_blk.shape[0]
        res_loc = z_blk.shape[0]
        heads_m = w_row_bias.shape[1]
        heads_t = w_start_bias.shape[1]
        opm = w_opm_in.shape[1] // 2
        value_a6 = value_a8 != 0
        res_ok = (res_mask != 0)[None, :]

        row_bias = jnp.einsum('ijc,ch->hij', layer_norm(z_blk), w_row_bias, preferred_element_type=jnp.float32).astype(jnp.bfloat16)
        row_bias = lax.all_gather(row_bias, group, axis=1, tiled=True)
        seq_ok = lax.dynamic_slice_in_dim(value_a6, group_idx * seq_loc, seq_loc, axis=0)
        m_blk = add_residual(m_blk, gated_attention(layer_norm(m_blk), w_row_in, w_row_out, heads_m, row_bias, seq_ok, False))

        m_cols = lax.all_to_all(m_blk, group, 1, 0, tiled=True)
        col_mask = lax.dynamic_slice_in_dim(value_a8, group_idx * res_loc, res_loc, axis=1)
        m_cols = add_residual(m_cols, gated_attention(layer_norm(m_cols), w_col_in, w_col_out, heads_m, None, (col_mask != 0).T, True))

        outer_proj = jnp.dot(layer_norm(m_cols), w_opm_in, preferred_element_type=jnp.float32).astype(jnp.bfloat16)
        col_w = col_mask.astype(jnp.bfloat16)
        left = outer_proj[:, :, :opm] * col_w[:, :, None]
        right = lax.all_gather(outer_proj[:, :, opm:] * col_w[:, :, None], group, axis=1, tiled=True)
        pair_norm = jnp.einsum('si,sj->ij', col_w, value_a8.astype(jnp.bfloat16), preferred_element_type=jnp.float32)
        outer = jnp.einsum('sia,sjc->ijac', left, right, preferred_element_type=jnp.float32).astype(jnp.bfloat16)
        outer = outer.reshape(res_loc, outer.shape[1], opm * opm)
        z_blk = add_residual(z_blk, jnp.dot(outer, w_opm_out, preferred_element_type=jnp.float32) / (1e-3 + pair_norm[:, :, None]))

        start_norm = layer_norm(z_blk)
        start_bias = jnp.einsum('jkc,ch->hjk', start_norm, w_start_bias, preferred_element_type=jnp.float32).astype(jnp.bfloat16)
        start_bias = lax.all_gather(start_bias, group, axis=1, tiled=True)
        z_blk = add_residual(z_blk, gated_attention(start_norm, w_start_in, w_start_out, heads_t, start_bias, res_ok, False))

        z_cols = lax.all_to_all(z_blk, group, 1, 0, tiled=True)
        end_norm = layer_norm(z_cols)
        end_bias = jnp.einsum('kjc,ch->hjk', end_norm, w_end_bias, preferred_element_type=jnp.float32).astype(jnp.bfloat16)
        end_bias = lax.all_gather(end_bias, group, axis=1, tiled=True)
        z_cols = add_residual(z_cols, gated_attention(end_norm, w_end_in, w_end_out, heads_t, end_bias, res_ok, True))

        z_out = lax.all_to_all(z_cols, group, 0, 1, tiled=True)
        m_out = lax.all_to_all(m_cols, group, 0, 1, tiled=True)
        return m_out, z_out

    return jax.shard_map(per_device, mesh=mesh, in_specs=in_specs, out_specs=(rows, rows), check_vma=False)
```

profile of v0, /device:TPU:1, one launch (start us, length us, event | category | flops | bytes accessed | tf_op | source)
XLA Modules:
  0.0 1315.2 jit_solution(5647166921693511071)
XLA Ops:
  9.6 321.0 %all-gather = bf16[8,16384]{1,0:T(8,128)(2,1)S(1)} all-gather(bf16[8,128]{1,0:T(8,128)(2,1)S(1)} %fusion.78), channel_id=2, replica_groups=mesh['data'=1,'chip'=2,'dap'=64] {'chip','dap'}, dimensions={1}, use_global_device_ids=true | all-gather | bytes 264192 | tf_op jit(solution)/shard_map/all_gather | solution.py:63
  335.5 40.0 %while.40 = (s32[]{:T(128)}, bf16[8,16,128,32]{2,3,1,0:T(8,128)(2,1)}, pred[16,1,128]{2,0,1:T(8,128)(4,1)S(1)}, bf16[8,256,4,32]{1,3,0,2:T(8,128)(2,1)S(1)}, bf1...) while((s32[]{:T(128)}, bf16[8,16,128,32]{2,3,1,0:T(8,128)(2,1)}, ...), condition=%wide.region_7.8_spmd, body=%wide.region_4.7_spmd.sunk | while | flops 170279040 | bytes 4573781 | solution.py:41
  385.5 15.4 %all-to-all-done = bf16[16,128,256]{2,0,1:T(8,128)(2,1)S(1)} async-done(((bf16[16,128,256]{2,0,1:T(8,128)(2,1)}), bf16[16,128,256]{2,0,1:T(8,128)(2,1)S(1)}, u32[]{:S(2)}, u32[]{:S(2)}) %all-to-all-start) | async-done | bytes 1048608 | tf_op jit(solution)/shard_map/all_to_all | solution.py:67
  403.4 135.1 %while.41 = (s32[]{:T(128)}, bf16[8,2048,1,32]{1,3,2,0:T(8,128)(2,1)}, bf16[8,256,4,32]{1,3,0,2:T(8,128)(2,1)}, bf16[2048,1,256]{2,0,1:T(8,128)(2,1)S(1)}, pred[...) while((s32[]{:T(128)}, bf16[8,2048,1,32]{1,3,2,0:T(8,128)(2,1)}, ...), condition=%wide.region_13.14_spmd, body=%wide.region_10.13_spmd.sunk | while | flops 722071552 | bytes 52677708 | solution.py:41
  409.7 4.9 fusion.163
  414.5 5.9 fusion.164
  426.5 4.9 fusion.163
  431.4 5.9 fusion.164
  443.4 4.9 fusion.163
  448.3 5.9 fusion.164
  460.3 4.9 fusion.163
  465.1 5.9 fusion.164
  477.1 4.9 fusion.163
  482.0 5.9 fusion.164
  498.9 5.9 fusion.164
  510.9 4.9 fusion.163
  515.8 5.9 fusion.164
  532.6 5.9 fusion.164
  544.7 76.9 %all-gather.5.cloned.1.call-done = bf16[2048,128,32]{0,2,1:T(8,128)(2,1)} async-done(((bf16[2048,1,32]{0,2,1:T(8,128)(2,1)}), bf16[2048,128,32]{0,2,1:T(8,128)(2,1)}) %all-gather.5.cloned.1.call-update) | async-done | bytes 16777232 | tf_op jit(solution)/shard_map/all_gather | solution.py:74
  621.6 8.2 fusion.68
  631.8 315.6 %all-gather.1 = bf16[4,16384]{1,0:T(4,128)(2,1)S(1)} all-gather(bf16[4,128]{1,0:T(4,128)(2,1)S(1)} %fusion.79), channel_id=3, replica_groups=mesh['data'=1,'chip'=2,'dap'=64] {'chip','dap'}, dimensions={1}, use_global_device_ids=true | all-gather | bytes 132096 | tf_op jit(solution)/shard_map/all_gather | solution.py:82
  958.7 6.1 all-to-all-done.2
  969.7 321.3 %all-gather.2 = bf16[4,16384]{1,0:T(4,128)(2,1)S(1)} all-gather(bf16[4,128]{1,0:T(4,128)(2,1)S(1)} %fusion.80), channel_id=4, replica_groups=mesh['data'=1,'chip'=2,'dap'=64] {'chip','dap'}, dimensions={1}, use_global_device_ids=true | all-gather | bytes 132096 | tf_op jit(solution)/shard_map/all_gather | solution.py:88
  1300.9 6.9 all-to-all-done.3
  (228 shorter events, 158.3 us)
Async XLA Ops:
  7.2 624.0 %copy-start = (bf16[1024,128]{1,0:T(8,128)(2,1)S(1)}, bf16[1024,128]{1,0:T(8,128)(2,1)}, u32[]{:S(2)}) copy-start(bf16[1024,128]{1,0:T(8,128)(2,1)} %param.35) | copy-start | bytes 786436
  7.2 326.0 %copy-start.3 = (bf16[16,128,256]{2,1,0:T(8,128)(2,1)S(1)}, bf16[16,128,256]{2,1,0:T(8,128)(2,1)}, u32[]{:S(2)}) copy-start(bf16[16,128,256]{2,1,0:T(8,128)(2,1)} %param.25) | copy-start | bytes 3145732
  331.5 3.0 copy-start.6
  377.2 5.3 copy-start.4
  378.8 4.4 copy-start.7
  378.8 22.1 %all-to-all-start = ((bf16[16,128,256]{2,0,1:T(8,128)(2,1)}), bf16[16,128,256]{2,0,1:T(8,128)(2,1)S(1)}, u32[]{:S(2)}, u32[]{:S(2)}) async-start(bf16[16,128,256]{2,0,1:T(8,128)(2,1)} %copy.90), calls=%async_computation | async-start | bytes 2097152 | tf_op jit(solution)/shard_map/all_to_all | solution.py:67
  382.5 239.1 %all-gather.5.cloned.1.call-start = ((), (), s32[]{:S(2)}) async-start(), calls=%async_computation.4 | async-start | bytes 16908288 | tf_op jit(solution)/shard_map/all_gather | solution.py:74
  401.8 1.6 copy-start.1
  403.4 135.1 %copy-start.2 = (f32[16,128,256]{2,0,1:T(8,128)S(1)}, f32[16,128,256]{2,0,1:T(8,128)}, u32[]{:S(2)}) copy-start(f32[16,128,256]{2,0,1:T(8,128)} %copy-done.1) | copy-start | bytes 6291460
  538.5 1.9 copy-start.10
  540.4 2.8 copy-start.17
  542.8 0.8 copy-start.13
  542.8 1.5 copy-start.11
  542.8 1.6 copy-start.19
  542.8 1.6 copy-start.5
  544.7 86.5 %copy-start.9 = (bf16[1,128,128]{1,2,0:T(8,128)(2,1)S(1)}, bf16[1,128,128]{1,2,0:T(8,128)(2,1)}, u32[]{:S(2)}) copy-start(bf16[1,128,128]{1,2,0:T(8,128)(2,1)} %copy-done.8) | copy-start | bytes 98308
  629.8 1.8 copy-start.16
  947.4 2.9 copy-start.14
  947.5 7.6 copy-start.12
  951.3 13.5 %all-to-all-start.2 = ((bf16[1,128,128]{2,0,1:T(2,128)(2,1)}), bf16[1,128,128]{2,0,1:T(2,128)(2,1)S(1)}, u32[]{:S(2)}, u32[]{:S(2)}) async-start(bf16[1,128,128]{2,0,1:T(2,128)(2,1)} %copy.103), calls=%async_computation.2 | async-start | bytes 131072 | tf_op jit(solution)/shard_map/all_to_all | solution.py:85
  957.6 11.9 copy-start.18
  964.9 329.9 %all-to-all-start.1 = ((bf16[128,2,2048]{2,1,0:T(2,128)(2,1)}), bf16[128,2,2048]{2,1,0:T(2,128)(2,1)S(1)}, u32[]{:S(2)}, u32[]{:S(2)}) async-start(bf16[128,2,2048]{2,1,0:T(2,128)(2,1)} %reshape.689), calls=%async_computation.1 | async-start | bytes 2097152 | tf_op jit(solution)/shard_map/all_to_all | solution.py:92
  1291.0 2.9 copy-start.15
  1294.8 13.0 all-to-all-start.3
  (1 other events, 0.6 us)
Sparse Core Ops, SparseCore 0:
  544.4 77.1 all-gather.4
where the time goes:
time: 1320 us
  blocking collectives  958 us (73%)
  matrix products  149 us (11%)
  waiting for transfers between devices  105 us (8%)
  other arithmetic  56.4 us (4%)
  local copies, waits for them, and re-layouts  17 us (1%)
  starting transfers between devices  15 us (1%)
  between operations  14.6 us (1%)
    all_gather x1, blocking collectives, per_device(): end_bias = lax.all_gather(end_bias, group, axis=1, tiled=True)  321 us
    all_gather x1, blocking collectives, per_device(): row_bias = lax.all_gather(row_bias, group, axis=1, tiled=True)  321 us
    all_gather x1, blocking collectives, per_device(): start_bias = lax.all_gather(start_bias, group, axis=1, tiled=True)  316 us
    all_gather x1, waiting for transfers between devices, per_device(): lax.all_gather(outer_proj[:, :, opm:] * col_w[:, :, None], group, axis=1,...  76.9 us
    dot_general x24, matrix products, one_head(): jnp.einsum(forms[2], attn_prob, projected[:, :, 2], preferred_element_typ...  65.4 us
    reduce_sum x16, other arithmetic, one_head(): attn_prob = jax.nn.softmax(scores, axis=-1).astype(jnp.bfloat16)  39.3 us
    dot_general x16, matrix products, one_head(): jnp.einsum(forms[1], projected[:, :, 0], projected[:, :, 1], preferred_el...  33.7 us
  transfers between devices with their start and end apart: 5, of which 4 were waited for; matrix products, arithmetic and copies ran while one was open for 1% of the time, Pallas kernels for 0%

commit v1 on v0

--- a/solution.py
+++ b/solution.py
@@ -42,9 +42,16 @@
     return jnp.einsum(forms[3], gated, w_back, preferred_element_type=jnp.float32)
 
 
+def gather_rows(block, group, size):
+    spread = jnp.broadcast_to(block[None], (size,) + block.shape)
+    spread = lax.all_to_all(spread, group, 0, 0, tiled=True)
+    return jnp.moveaxis(spread[:, :, 0], 0, 1)
+
+
 def solution(mesh):
     dap_size = mesh.shape['dap']
     group = ('chip', 'dap')
+    group_size = mesh.shape['chip'] * dap_size
     rows = P(('data', 'chip', 'dap'))
     in_specs = (rows, rows, P('data'), P('data')) + (P(),) * 13
 
@@ -60,7 +67,7 @@
         res_ok = (res_mask != 0)[None, :]
 
         row_bias = jnp.einsum('ijc,ch->hij', layer_norm(z_blk), w_row_bias, preferred_element_type=jnp.float32).astype(jnp.bfloat16)
-        row_bias = lax.all_gather(row_bias, group, axis=1, tiled=True)
+        row_bias = gather_rows(row_bias, group, group_size)
         seq_ok = lax.dynamic_slice_in_dim(value_a6, group_idx * seq_loc, seq_loc, axis=0)
         m_blk = add_residual(m_blk, gated_attention(layer_norm(m_blk), w_row_in, w_row_out, heads_m, row_bias, seq_ok, False))
 
@@ -79,13 +86,13 @@
 
         start_norm = layer_norm(z_blk)
         start_bias = jnp.einsum('jkc,ch->hjk', start_norm, w_start_bias, preferred_element_type=jnp.float32).astype(jnp.bfloat16)
-        start_bias = lax.all_gather(start_bias, group, axis=1, tiled=True)
+        start_bias = gather_rows(start_bias, group, group_size)
         z_blk = add_residual(z_blk, gated_attention(start_norm, w_start_in, w_start_out, heads_t, start_bias, res_ok, False))
 
         z_cols = lax.all_to_all(z_blk, group, 1, 0, tiled=True)
         end_norm = layer_norm(z_cols)
         end_bias = jnp.einsum('kjc,ch->hjk', end_norm, w_end_bias, preferred_element_type=jnp.float32).astype(jnp.bfloat16)
-        end_bias = lax.all_gather(end_bias, group, axis=1, tiled=True)
+        end_bias = gather_rows(end_bias, group, group_size)
         z_cols = add_residual(z_cols, gated_attention(end_norm, w_end_in, w_end_out, heads_t, end_bias, res_ok, True))
 
         z_out = lax.all_to_all(z_cols, group, 0, 1, tiled=True)

time: 1320 us -> 428 us (0.32)
  blocking collectives: 958 us -> 0 us
  waiting for transfers between devices: 105 us -> 147 us
  starting transfers between devices: 15 us -> 40.6 us
    all_gather x3 -> x0, blocking collectives: 958 us -> none  [the longest x1 321 us: per_device(): end_bias = lax.all_gather(end_bias, group, axis=1, tiled=True)]
    all_to_all x0 -> x3, waiting for transfers between devices: none -> 26.5 us  [gather_rows(): spread = lax.all_to_all(spread, group, 0, 0, tiled=True)]
    all_to_all x0 -> x3, starting transfers between devices: none -> 23 us  [gather_rows(): spread = lax.all_to_all(spread, group, 0, 0, tiled=True)]
    all_to_all x1, waiting for transfers between devices: 0.01 us -> 15 us  [per_device(): m_out = lax.all_to_all(m_cols, group, 0, 1, tiled=True)]
  transfers between devices with their start and end apart: 5 -> 8, of which waited for: 4 -> 8; matrix products, arithmetic and copies ran while one was open for 1% -> 4% of each run, Pallas kernels for 0% -> 0%
where the time goes in v1:
time: 428 us; the launch traced here: 425 us
  matrix products  149 us (35%)
  waiting for transfers between devices  147 us (34%)
  other arithmetic  56.3 us (13%)
  starting transfers between devices  40.6 us (9%)
  local copies, waits for them, and re-layouts  17.7 us (4%)
  between operations  14.7 us (3%)
    all_gather x1, waiting for transfers between devices, per_device(): lax.all_gather(outer_proj[:, :, opm:] * col_w[:, :, None], group, axis=1,...  76.9 us
    dot_general x24, matrix products, one_head(): jnp.einsum(forms[2], attn_prob, projected[:, :, 2], preferred_element_typ...  65.4 us
    reduce_sum x16, other arithmetic, one_head(): attn_prob = jax.nn.softmax(scores, axis=-1).astype(jnp.bfloat16)  39.3 us
    dot_general x16, matrix products, one_head(): jnp.einsum(forms[1], projected[:, :, 0], projected[:, :, 1], preferred_el...  33.9 us
    all_to_all x3, waiting for transfers between devices, gather_rows(): spread = lax.all_to_all(spread, group, 0, 0, tiled=True)  26.5 us
    all_to_all x3, starting transfers between devices, gather_rows(): spread = lax.all_to_all(spread, group, 0, 0, tiled=True)  23 us
    dot_general x24, matrix products, one_head(): jnp.einsum(forms[0], x_norm, head_in[0], preferred_element_type=jnp.float32)  21.8 us
    all_to_all x1, waiting for transfers between devices, per_device(): m_cols = lax.all_to_all(m_blk, group, 1, 0, tiled=True)  15.4 us
  transfers between devices with their start and end apart: 8, of which 8 were waited for; matrix products, arithmetic and copies ran while one was open for 4% of the time, Pallas kernels for 0%

profile of v1, /device:TPU:1, one launch (start us, length us, event | category | flops | bytes accessed | tf_op | source)
XLA Modules:
  0.0 425.5 jit_solution(55503343038843066)
XLA Ops:
  9.8 11.5 %all-to-all-start = ((bf16[128,8,1,128]{3,1,2,0:T(8,128)(2,1)}), bf16[128,8,1,128]{3,1,2,0:T(8,128)(2,1)S(1)}, u32[]{:S(2)}, u32[]{:S(2)}) async-start(bf16[128,8,1,128]{3,1,2,0:T(8,128)(2,1)} %broadcast_in_dim.129), calls=%async_computation | async-start | bytes 524288 | tf_op jit(solution)/shard_map/all_to_all | solution.py:47
  25.3 6.8 %all-to-all-done = bf16[128,8,1,128]{3,1,2,0:T(8,128)(2,1)S(1)} async-done(((bf16[128,8,1,128]{3,1,2,0:T(8,128)(2,1)}), bf16[128,8,1,128]{3,1,2,0:T(8,128)(2,1)S(1)}, u32[]{:S(2)}, u32[]{:S(2)}) %all-to-all-start) | async-done | bytes 262176 | tf_op jit(solution)/shard_map/all_to_all | solution.py:47
  32.9 40.0 %while.40 = (s32[]{:T(128)}, bf16[8,16,128,32]{2,3,1,0:T(8,128)(2,1)}, pred[16,1,128]{2,0,1:T(8,128)(4,1)S(1)}, bf16[8,256,4,32]{1,3,0,2:T(8,128)(2,1)S(1)}, bf1...) while((s32[]{:T(128)}, bf16[8,16,128,32]{2,3,1,0:T(8,128)(2,1)}, ...), condition=%wide.region_7.8_spmd, body=%wide.region_4.7_spmd.sunk | while | flops 170279040 | bytes 4573781 | solution.py:41
  83.5 15.4 %all-to-all-done.1 = bf16[16,128,256]{2,0,1:T(8,128)(2,1)S(1)} async-done(((bf16[16,128,256]{2,0,1:T(8,128)(2,1)}), bf16[16,128,256]{2,0,1:T(8,128)(2,1)S(1)}, u32[]{:S(2)}, u32[]{:S(2)}) %all-to-all-start.1) | async-done | bytes 1048608 | tf_op jit(solution)/shard_map/all_to_all | solution.py:74
  101.4 135.1 %while.41 = (s32[]{:T(128)}, bf16[8,2048,1,32]{1,3,2,0:T(8,128)(2,1)}, bf16[8,256,4,32]{1,3,0,2:T(8,128)(2,1)}, bf16[2048,1,256]{2,0,1:T(8,128)(2,1)S(1)}, pred[...) while((s32[]{:T(128)}, bf16[8,2048,1,32]{1,3,2,0:T(8,128)(2,1)}, ...), condition=%wide.region_13.14_spmd, body=%wide.region_10.13_spmd.sunk | while | flops 722071552 | bytes 52677708 | solution.py:41
  107.7 4.9 %fusion.163 = f32[2048]{0:T(1024)S(1)} fusion(f32[2048,2048]{0,1:T(8,128)S(1)} %get-tuple-element.418, f32[2048]{0:T(1024)S(1)} %get-tuple-element.419, pred[2048]{0:T(1024)(128)(4,1)S(1)} %reduce.36), kind=kLoop, calls=%fused_computation.68.clone.1 | loop fusion | flops 16775168 | bytes 16795648 | tf_op jit(solution)/shard_map/while/body/eval_jaxpr/reduce_sum | solution.py:36
  112.6 5.9 %fusion.164 = bf16[8,2048,1,32]{1,3,2,0:T(8,128)(2,1)} fusion(bf16[8,2048,1,32]{1,3,2,0:T(8,128)(2,1)} %get-tuple-element.465, s32[]{:T(128)} %get-tuple-element.464, f32[2048,2048]{0,1:T(8,128)S(1)} %get-tuple-element.418, f32[2048]{0:T(1024)S(1)} %fusion.163, f32[2048]{0:T(1024)S(1)} %get-tuple-element.419, pred[2048]{0:T(1024)(128)(4,1)S(1)} %reduce.36, ...), kind=kOutput, calls=%fused_computation.76.clone.1 | convolution fusion | flops 289800192 | bytes 17189376 | tf_op jit(solution)/shard_map/while/body/eval_jaxpr/bij,jbd->ibd/dot_general | solution.py:37
  129.5 5.9 %fusion.164 = bf16[8,2048,1,32]{1,3,2,0:T(8,128)(2,1)} fusion(bf16[8,2048,1,32]{1,3,2,0:T(8,128)(2,1)} %get-tuple-element.465, s32[]{:T(128)} %get-tuple-element.464, f32[2048,2048]{0,1:T(8,128)S(1)} %get-tuple-element.418, f32[2048]{0:T(1024)S(1)} %fusion.163, f32[2048]{0:T(1024)S(1)} %get-tuple-element.419, pred[2048]{0:T(1024)(128)(4,1)S(1)} %reduce.36, ...), kind=kOutput, calls=%fused_computation.76.clone.1 | convolution fusion | flops 289800192 | bytes 17189376 | tf_op jit(solution)/shard_map/while/body/eval_jaxpr/bij,jbd->ibd/dot_general | solution.py:37
  141.5 4.9 %fusion.163 = f32[2048]{0:T(1024)S(1)} fusion(f32[2048,2048]{0,1:T(8,128)S(1)} %get-tuple-element.418, f32[2048]{0:T(1024)S(1)} %get-tuple-element.419, pred[2048]{0:T(1024)(128)(4,1)S(1)} %reduce.36), kind=kLoop, calls=%fused_computation.68.clone.1 | loop fusion | flops 16775168 | bytes 16795648 | tf_op jit(solution)/shard_map/while/body/eval_jaxpr/reduce_sum | solution.py:36
  146.3 5.9 %fusion.164 = bf16[8,2048,1,32]{1,3,2,0:T(8,128)(2,1)} fusion(bf16[8,2048,1,32]{1,3,2,0:T(8,128)(2,1)} %get-tuple-element.465, s32[]{:T(128)} %get-tuple-element.464, f32[2048,2048]{0,1:T(8,128)S(1)} %get-tuple-element.418, f32[2048]{0:T(1024)S(1)} %fusion.163, f32[2048]{0:T(1024)S(1)} %get-tuple-element.419, pred[2048]{0:T(1024)(128)(4,1)S(1)} %reduce.36, ...), kind=kOutput, calls=%fused_computation.76.clone.1 | convolution fusion | flops 289800192 | bytes 17189376 | tf_op jit(solution)/shard_map/while/body/eval_jaxpr/bij,jbd->ibd/dot_general | solution.py:37
  163.2 5.9 %fusion.164 = bf16[8,2048,1,32]{1,3,2,0:T(8,128)(2,1)} fusion(bf16[8,2048,1,32]{1,3,2,0:T(8,128)(2,1)} %get-tuple-element.465, s32[]{:T(128)} %get-tuple-element.464, f32[2048,2048]{0,1:T(8,128)S(1)} %get-tuple-element.418, f32[2048]{0:T(1024)S(1)} %fusion.163, f32[2048]{0:T(1024)S(1)} %get-tuple-element.419, pred[2048]{0:T(1024)(128)(4,1)S(1)} %reduce.36, ...), kind=kOutput, calls=%fused_computation.76.clone.1 | convolution fusion | flops 289800192 | bytes 17189376 | tf_op jit(solution)/shard_map/while/body/eval_jaxpr/bij,jbd->ibd/dot_general | solution.py:37
  180.1 5.9 %fusion.164 = bf16[8,2048,1,32]{1,3,2,0:T(8,128)(2,1)} fusion(bf16[8,2048,1,32]{1,3,2,0:T(8,128)(2,1)} %get-tuple-element.465, s32[]{:T(128)} %get-tuple-element.464, f32[2048,2048]{0,1:T(8,128)S(1)} %get-tuple-element.418, f32[2048]{0:T(1024)S(1)} %fusion.163, f32[2048]{0:T(1024)S(1)} %get-tuple-element.419, pred[2048]{0:T(1024)(128)(4,1)S(1)} %reduce.36, ...), kind=kOutput, calls=%fused_computation.76.clone.1 | convolution fusion | flops 289800192 | bytes 17189376 | tf_op jit(solution)/shard_map/while/body/eval_jaxpr/bij,jbd->ibd/dot_general | solution.py:37
  197.0 5.9 %fusion.164 = bf16[8,2048,1,32]{1,3,2,0:T(8,128)(2,1)} fusion(bf16[8,2048,1,32]{1,3,2,0:T(8,128)(2,1)} %get-tuple-element.465, s32[]{:T(128)} %get-tuple-element.464, f32[2048,2048]{0,1:T(8,128)S(1)} %get-tuple-element.418, f32[2048]{0:T(1024)S(1)} %fusion.163, f32[2048]{0:T(1024)S(1)} %get-tuple-element.419, pred[2048]{0:T(1024)(128)(4,1)S(1)} %reduce.36, ...), kind=kOutput, calls=%fused_computation.76.clone.1 | convolution fusion | flops 289800192 | bytes 17189376 | tf_op jit(solution)/shard_map/while/body/eval_jaxpr/bij,jbd->ibd/dot_general | solution.py:37
  213.8 5.9 %fusion.164 = bf16[8,2048,1,32]{1,3,2,0:T(8,128)(2,1)} fusion(bf16[8,2048,1,32]{1,3,2,0:T(8,128)(2,1)} %get-tuple-element.465, s32[]{:T(128)} %get-tuple-element.464, f32[2048,2048]{0,1:T(8,128)S(1)} %get-tuple-element.418, f32[2048]{0:T(1024)S(1)} %fusion.163, f32[2048]{0:T(1024)S(1)} %get-tuple-element.419, pred[2048]{0:T(1024)(128)(4,1)S(1)} %reduce.36, ...), kind=kOutput, calls=%fused_computation.76.clone.1 | convolution fusion | flops 289800192 | bytes 17189376 | tf_op jit(solution)/shard_map/while/body/eval_jaxpr/bij,jbd->ibd/dot_general | solution.py:37
  230.7 5.9 %fusion.164 = bf16[8,2048,1,32]{1,3,2,0:T(8,128)(2,1)} fusion(bf16[8,2048,1,32]{1,3,2,0:T(8,128)(2,1)} %get-tuple-element.465, s32[]{:T(128)} %get-tuple-element.464, f32[2048,2048]{0,1:T(8,128)S(1)} %get-tuple-element.418, f32[2048]{0:T(1024)S(1)} %fusion.163, f32[2048]{0:T(1024)S(1)} %get-tuple-element.419, pred[2048]{0:T(1024)(128)(4,1)S(1)} %reduce.36, ...), kind=kOutput, calls=%fused_computation.76.clone.1 | convolution fusion | flops 289800192 | bytes 17189376 | tf_op jit(solution)/shard_map/while/body/eval_jaxpr/bij,jbd->ibd/dot_general | solution.py:37
  242.7 76.9 %all-gather.2.cloned.1.call-done = bf16[2048,128,32]{0,2,1:T(8,128)(2,1)} async-done(((bf16[2048,1,32]{0,2,1:T(8,128)(2,1)}), bf16[2048,128,32]{0,2,1:T(8,128)(2,1)}) %all-gather.2.cloned.1.call-update) | async-done | bytes 16777232 | tf_op jit(solution)/shard_map/all_gather | solution.py:81
  319.7 8.2 %fusion.68 = bf16[1,128,32,32]{2,3,1,0:T(8,128)(2,1)S(1)} fusion(bf16[2048,128,32]{0,2,1:T(8,128)(2,1)} %all-gather.2.cloned.1.call-done, bf16[2048,1,64]{0,2,1:T(8,128)(2,1)S(1)} %fusion.62, bf16[2048]{0:T(1024)(128)(2,1)S(1)} %copy-done.13), kind=kOutput, calls=%fused_computation.110 | convolution fusion | flops 537067520 | bytes 17174528 | tf_op jit(solution)/shard_map/sia,sjc->ijac/dot_general | solution.py:83
  330.5 7.4 %all-to-all-start.3 = ((bf16[128,4,1,128]{3,1,2,0:T(4,128)(2,1)}), bf16[128,4,1,128]{3,1,2,0:T(4,128)(2,1)S(1)}, u32[]{:S(2)}, u32[]{:S(2)}) async-start(bf16[128,4,1,128]{3,1,2,0:T(4,128)(2,1)} %broadcast_in_dim.132), calls=%async_computation.3 | async-start | bytes 262144 | tf_op jit(solution)/shard_map/all_to_all | solution.py:47
  338.0 9.8 %all-to-all-done.3 = bf16[128,4,1,128]{3,1,2,0:T(4,128)(2,1)S(1)} async-done(((bf16[128,4,1,128]{3,1,2,0:T(4,128)(2,1)}), bf16[128,4,1,128]{3,1,2,0:T(4,128)(2,1)S(1)}, u32[]{:S(2)}, u32[]{:S(2)}) %all-to-all-start.3) | async-done | bytes 131104 | tf_op jit(solution)/shard_map/all_to_all | solution.py:47
  358.9 6.1 %all-to-all-done.4 = bf16[1,128,128]{2,0,1:T(2,128)(2,1)S(1)} async-done(((bf16[1,128,128]{2,0,1:T(2,128)(2,1)}), bf16[1,128,128]{2,0,1:T(2,128)(2,1)S(1)}, u32[]{:S(2)}, u32[]{:S(2)}) %all-to-all-start.4) | async-done | bytes 32800 | tf_op jit(solution)/shard_map/all_to_all | solution.py:92
  370.5 10.0 %all-to-all-done.5 = bf16[128,4,1,128]{3,1,2,0:T(4,128)(2,1)S(1)} async-done(((bf16[128,4,1,128]{3,1,2,0:T(4,128)(2,1)}), bf16[128,4,1,128]{3,1,2,0:T(4,128)(2,1)S(1)}, u32[]{:S(2)}, u32[]{:S(2)}) %all-to-all-start.5) | async-done | bytes 131104 | tf_op jit(solution)/shard_map/all_to_all | solution.py:47
  387.9 15.0 %all-to-all-done.2 = bf16[128,2,2048]{2,1,0:T(2,128)(2,1)S(1)} async-done(((bf16[128,2,2048]{2,1,0:T(2,128)(2,1)}), bf16[128,2,2048]{2,1,0:T(2,128)(2,1)S(1)}, u32[]{:S(2)}, u32[]{:S(2)}) %all-to-all-start.2) | async-done | bytes 1048608 | tf_op jit(solution)/shard_map/all_to_all | solution.py:99
  402.9 5.4 %all-to-all-start.6 = ((bf16[128,1,128]{2,1,0:T(2,128)(2,1)}), bf16[128,1,128]{2,1,0:T(2,128)(2,1)S(1)}, u32[]{:S(2)}, u32[]{:S(2)}) async-start(bf16[128,1,128]{2,1,0:T(2,128)(2,1)} %copy.102), calls=%async_computation.6 | async-start | bytes 131072 | tf_op jit(solution)/shard_map/all_to_all | solution.py:98
  410.9 7.2 %all-to-all-done.6 = bf16[128,1,128]{2,1,0:T(2,128)(2,1)S(1)} async-done(((bf16[128,1,128]{2,1,0:T(2,128)(2,1)}), bf16[128,1,128]{2,1,0:T(2,128)(2,1)S(1)}, u32[]{:S(2)}, u32[]{:S(2)}) %all-to-all-start.6) | async-done | bytes 32800 | tf_op jit(solution)/shard_map/all_to_all | solution.py:98
  (218 shorter events, 178.9 us)
Async XLA Ops:
  7.2 322.1 %copy-start = (bf16[1024,128]{1,0:T(8,128)(2,1)S(1)}, bf16[1024,128]{1,0:T(8,128)(2,1)}, u32[]{:S(2)}) copy-start(bf16[1024,128]{1,0:T(8,128)(2,1)} %param.35) | copy-start | bytes 786436
  7.2 15.8 %copy-start.3 = (bf16[16,128,256]{2,1,0:T(8,128)(2,1)S(1)}, bf16[16,128,256]{2,1,0:T(8,128)(2,1)}, u32[]{:S(2)}) copy-start(bf16[16,128,256]{2,1,0:T(8,128)(2,1)} %param.25) | copy-start | bytes 3145732
  7.2 16.4 %copy-start.6 = (bf16[256,1024]{1,0:T(8,128)(2,1)S(1)}, bf16[256,1024]{1,0:T(8,128)(2,1)}, u32[]{:S(2)}) copy-start(bf16[256,1024]{1,0:T(8,128)(2,1)} %param.29) | copy-start | bytes 1572868
  8.2 15.4 %copy-start.8 = (bf16[1,128,128]{1,2,0:T(8,128)(2,1)}, bf16[1,128,128]{1,2,0:T(8,128)(2,1)S(1)}, u32[]{:S(2)}) copy-start(bf16[1,128,128]{1,2,0:T(8,128)(2,1)S(1)} %copy.81) | copy-start | bytes 98308
  9.8 22.2 %all-to-all-start = ((bf16[128,8,1,128]{3,1,2,0:T(8,128)(2,1)}), bf16[128,8,1,128]{3,1,2,0:T(8,128)(2,1)S(1)}, u32[]{:S(2)}, u32[]{:S(2)}) async-start(bf16[128,8,1,128]{3,1,2,0:T(8,128)(2,1)} %broadcast_in_dim.129), calls=%async_computation | async-start | bytes 524288 | tf_op jit(solution)/shard_map/all_to_all | solution.py:47
  74.7 5.9 %copy-start.4 = (s32[2048,128]{1,0:T(8,128)S(1)}, s32[2048,128]{1,0:T(8,128)}, u32[]{:S(2)}) copy-start(s32[2048,128]{1,0:T(8,128)} %param.27) | copy-start | bytes 3145732
  76.2 5.0 %copy-start.7 = (bf16[256,1024]{1,0:T(8,128)(2,1)S(1)}, bf16[256,1024]{1,0:T(8,128)(2,1)}, u32[]{:S(2)}) copy-start(bf16[256,1024]{1,0:T(8,128)(2,1)} %param.32) | copy-start | bytes 1572868
  76.2 22.7 %all-to-all-start.1 = ((bf16[16,128,256]{2,0,1:T(8,128)(2,1)}), bf16[16,128,256]{2,0,1:T(8,128)(2,1)S(1)}, u32[]{:S(2)}, u32[]{:S(2)}) async-start(bf16[16,128,256]{2,0,1:T(8,128)(2,1)} %copy.84), calls=%async_computation.1 | async-start | bytes 2097152 | tf_op jit(solution)/shard_map/all_to_all | solution.py:74
  80.5 239.1 %all-gather.2.cloned.1.call-start = ((), (), s32[]{:S(2)}) async-start(), calls=%async_computation.7 | async-start | bytes 16908288 | tf_op jit(solution)/shard_map/all_gather | solution.py:81
  101.4 135.1 %copy-start.2 = (f32[16,128,256]{2,0,1:T(8,128)S(1)}, f32[16,128,256]{2,0,1:T(8,128)}, u32[]{:S(2)}) copy-start(f32[16,128,256]{2,0,1:T(8,128)} %copy-done.1) | copy-start | bytes 6291460
  236.6 1.9 copy-start.10
  238.5 2.8 copy-start.17
  242.7 86.5 %copy-start.9 = (bf16[1,128,128]{1,2,0:T(8,128)(2,1)S(1)}, bf16[1,128,128]{1,2,0:T(8,128)(2,1)}, u32[]{:S(2)}) copy-start(bf16[1,128,128]{1,2,0:T(8,128)(2,1)} %copy-done.8) | copy-start | bytes 98308
  327.9 1.7 copy-start.16
  327.9 9.9 %copy-start.19 = (s32[128]{0:T(128)S(1)}, s32[128]{0:T(128)}, u32[]{:S(2)}) copy-start(s32[128]{0:T(128)} %param.28) | copy-start | bytes 1540
  329.6 20.7 %copy-start.14 = (bf16[128,128]{1,0:T(8,128)(2,1)S(1)}, bf16[128,128]{1,0:T(8,128)(2,1)}, u32[]{:S(2)}) copy-start(bf16[128,128]{1,0:T(8,128)(2,1)} %param.38) | copy-start | bytes 98308
  330.5 24.7 %copy-start.12 = (bf16[128,512]{1,0:T(8,128)(2,1)S(1)}, bf16[128,512]{1,0:T(8,128)(2,1)}, u32[]{:S(2)}) copy-start(bf16[128,512]{1,0:T(8,128)(2,1)} %param.39) | copy-start | bytes 393220
  330.5 17.3 %all-to-all-start.3 = ((bf16[128,4,1,128]{3,1,2,0:T(4,128)(2,1)}), bf16[128,4,1,128]{3,1,2,0:T(4,128)(2,1)S(1)}, u32[]{:S(2)}, u32[]{:S(2)}) async-start(bf16[128,4,1,128]{3,1,2,0:T(4,128)(2,1)} %broadcast_in_dim.132), calls=%async_computation.3 | async-start | bytes 262144 | tf_op jit(solution)/shard_map/all_to_all | solution.py:47
  351.2 13.8 %all-to-all-start.4 = ((bf16[1,128,128]{2,0,1:T(2,128)(2,1)}), bf16[1,128,128]{2,0,1:T(2,128)(2,1)S(1)}, u32[]{:S(2)}, u32[]{:S(2)}) async-start(bf16[1,128,128]{2,0,1:T(2,128)(2,1)} %copy.97), calls=%async_computation.4 | async-start | bytes 131072 | tf_op jit(solution)/shard_map/all_to_all | solution.py:92
  357.3 8.1 %copy-start.18 = (bf16[128,4]{0,1:T(4,128)(2,1)S(1)}, bf16[128,4]{0,1:T(4,128)(2,1)}, u32[]{:S(2)}) copy-start(bf16[128,4]{0,1:T(4,128)(2,1)} %param.40) | copy-start | bytes 3076
  366.3 14.2 %all-to-all-start.5 = ((bf16[128,4,1,128]{3,1,2,0:T(4,128)(2,1)}), bf16[128,4,1,128]{3,1,2,0:T(4,128)(2,1)S(1)}, u32[]{:S(2)}, u32[]{:S(2)}) async-start(bf16[128,4,1,128]{3,1,2,0:T(4,128)(2,1)} %broadcast_in_dim.134), calls=%async_computation.5 | async-start | bytes 262144 | tf_op jit(solution)/shard_map/all_to_all | solution.py:47
  380.5 22.4 %all-to-all-start.2 = ((bf16[128,2,2048]{2,1,0:T(2,128)(2,1)}), bf16[128,2,2048]{2,1,0:T(2,128)(2,1)S(1)}, u32[]{:S(2)}, u32[]{:S(2)}) async-start(bf16[128,2,2048]{2,1,0:T(2,128)(2,1)} %reshape.698), calls=%async_computation.2 | async-start | bytes 2097152 | tf_op jit(solution)/shard_map/all_to_all | solution.py:99
  384.5 2.5 copy-start.15
  402.9 15.2 %all-to-all-start.6 = ((bf16[128,1,128]{2,1,0:T(2,128)(2,1)}), bf16[128,1,128]{2,1,0:T(2,128)(2,1)S(1)}, u32[]{:S(2)}, u32[]{:S(2)}) async-start(bf16[128,1,128]{2,1,0:T(2,128)(2,1)} %copy.102), calls=%async_computation.6 | async-start | bytes 131072 | tf_op jit(solution)/shard_map/all_to_all | solution.py:98
  (4 other events, 5.5 us)
Sparse Core Ops, SparseCore 0:
  242.5 77.1 all-gather.1

commit v2 on v0

v2 whole, which is shorter than its diff:
```python
import functools

import jax
import jax.numpy as jnp
import numpy as np
from jax import lax
from jax.experimental import pallas as pl
from jax.experimental.pallas import tpu as pltpu
from jax.sharding import PartitionSpec as P

LOG2E = 1.4426950408889634
f32, bf16 = jnp.float32, jnp.bfloat16


def split3(value):
    parts = []
    rest = np.float64(value)
    for _ in range(3):
        part = np.float64(np.asarray(rest, dtype=jnp.bfloat16))
        parts.append(float(part))
        rest = rest - part
    return parts


def norm_rows(x):
    values = x.astype(f32)
    centred = values - jnp.mean(values, axis=-1, keepdims=True)
    variance = jnp.mean(centred * centred, axis=-1, keepdims=True)
    return (centred * lax.rsqrt(variance + 1e-5)).astype(bf16)


def dot_t(w, x):
    return lax.dot_general(w, x, (((0,), (1,)), ((), ())), preferred_element_type=f32)


def col_kernel(x_ref, mrow_ref, win_ref, wout_ref, wopm_ref, y_ref, ac_ref,
               kaug, qaug, vt, sig, gat, s0, s1, pr, wt, wka):
    seq, width = x_ref.shape
    heads, hd = vt.shape[0], vt.shape[1]
    fold = heads * hd
    bq = s0.shape[1]
    nq = seq // bq
    kc = 256
    nk = seq // kc
    c = hd ** -0.5 * LOG2E
    masked = split3(-1e9 * LOG2E)

    bp = 512
    lane = lax.broadcasted_iota(jnp.int32, (bp, 128), 1)
    row = lax.broadcasted_iota(jnp.int32, (128 - 3 * hd, bp), 0)
    fill = jnp.where(row == 0, masked[0], jnp.where(row == 1, masked[1], jnp.where(row == 2, masked[2], 0.0))).astype(bf16)
    flag = ((lane >= 3 * hd) & (lane < 3 * hd + 3)).astype(f32)
    flag2 = jnp.concatenate([flag, flag], axis=1)

    wt[...] = jnp.transpose(win_ref[...])
    for h in range(heads):
        wk = win_ref[:, fold + h * hd:fold + (h + 1) * hd]
        wka[:, h * 128:(h + 1) * 128] = jnp.concatenate([wk, wk, wk, jnp.zeros_like(wk)], axis=1)

    def project(b, carry):
        rows = pl.ds(pl.multiple_of(b * bp, bp), bp)
        xn = norm_rows(x_ref[rows, :])
        keep = jnp.transpose(jnp.broadcast_to(mrow_ref[:, rows], (128, bp)).astype(f32)) != 0
        keep2 = jnp.concatenate([keep, keep], axis=1)
        for h in range(0, heads, 2):
            k = jnp.dot(xn, wka[:, h * 128:(h + 2) * 128], preferred_element_type=f32)
            k = jnp.where(keep2, k, flag2).astype(bf16)
            kaug[h, rows, :] = k[:, :128]
            kaug[h + 1, rows, :] = k[:, 128:]

        def tdot(w):
            return lax.dot_general(w, xn, (((1,), (1,)), ((), ())), preferred_element_type=f32)

        qt = tdot(wt[:fold, :]).astype(bf16).astype(f32) * c
        hi = qt.astype(bf16)
        rest = qt - hi.astype(f32)
        mid = rest.astype(bf16)
        low = (rest - mid.astype(f32)).astype(bf16)
        vv = tdot(wt[2 * fold:3 * fold, :]).astype(bf16)
        gg = tdot(wt[3 * fold:, :]).astype(bf16).astype(f32)
        gg = 1.0 / (1.0 + jnp.exp(-gg))
        for h in range(heads):
            part = slice(h * hd, (h + 1) * hd)
            qaug[h, 0:hd, rows] = hi[part]
            qaug[h, hd:2 * hd, rows] = mid[part]
            qaug[h, 2 * hd:3 * hd, rows] = low[part]
            qaug[h, 3 * hd:, rows] = fill
            vt[h, :, rows] = vv[part]
            sig[h, :, rows] = gg[part]
        return carry

    lax.fori_loop(0, seq // bp, project, 0)

    def scores(h, q, k0):
        return jnp.dot(kaug[h, k0:k0 + kc, :], q, preferred_element_type=f32)

    def fold8(s):
        return s.reshape(kc // 8, 8, bq)

    def step(t, cur, nxt, m):
        qb, h = t // heads, t % heads
        tn = jnp.minimum(t + 1, nq * heads - 1)
        qbn, hn = tn // heads, tn % heads
        q = qaug[hn, :, pl.ds(pl.multiple_of(qbn * bq, bq), bq)]
        top = jnp.max(m, axis=0, keepdims=True)
        mn = None
        total = jnp.zeros((8, bq), f32)
        mixed = jnp.zeros((hd, bq), f32)
        for i in range(nk):
            s = scores(hn, q, i * kc)
            nxt[i * kc:(i + 1) * kc, :] = s
            sm = jnp.max(fold8(s), axis=0)
            mn = sm if mn is None else jnp.maximum(mn, sm)
            e = jnp.exp2(cur[i * kc:(i + 1) * kc, :] - top)
            total = total + jnp.sum(fold8(e), axis=0)
            mixed = mixed + jnp.dot(vt[h, :, i * kc:(i + 1) * kc], e.astype(bf16), preferred_element_type=f32)
        cols = pl.ds(pl.multiple_of(qb * bq, bq), bq)
        mixed = mixed / jnp.sum(total, axis=0, keepdims=True)
        gat[pl.ds(pl.multiple_of(h * hd, hd), hd), cols] = (mixed * sig[h, :, cols]).astype(bf16)
        return mn

    m = None
    q = qaug[0, :, 0:bq]
    for i in range(nk):
        s = scores(0, q, i * kc)
        s0[i * kc:(i + 1) * kc, :] = s
        sm = jnp.max(fold8(s), axis=0)
        m = sm if m is None else jnp.maximum(m, sm)

    def pair(u, m):
        m = step(2 * u, s0, s1, m)
        return step(2 * u + 1, s1, s0, m)

    lax.fori_loop(0, nq * heads // 2, pair, m)

    def finish(b, carry):
        rows = pl.ds(pl.multiple_of(b * bp, bp), bp)
        up = lax.dot_general(gat[:, rows], wout_ref[...], (((0,), (0,)), ((), ())), preferred_element_type=f32)
        y = (x_ref[rows, :].astype(f32) + up).astype(bf16)
        y_ref[rows, :] = y
        ac = lax.dot_general(jnp.transpose(wopm_ref[...]), norm_rows(y), (((1,), (1,)), ((), ())), preferred_element_type=f32).astype(bf16)
        ac_ref[:, rows] = (ac.astype(f32) * mrow_ref[:, rows].astype(f32)).astype(bf16)
        return carry

    lax.fori_loop(0, seq // bp, finish, 0)


def col_attention(x, mask, w_in, w_out, w_opm, heads, bq=512):
    seq, width = x.shape
    hd = w_out.shape[0] // heads
    vm = pl.BlockSpec(memory_space=pltpu.VMEM)
    return pl.pallas_call(
        col_kernel,
        out_shape=(jax.ShapeDtypeStruct((seq, width), bf16), jax.ShapeDtypeStruct((w_opm.shape[1], seq), bf16)),
        in_specs=[vm] * 5,
        out_specs=(vm, vm),
        scratch_shapes=[
            pltpu.VMEM((heads, seq, 128), bf16),
            pltpu.VMEM((heads, 128, seq), bf16),
            pltpu.VMEM((heads, hd, seq), bf16),
            pltpu.VMEM((heads, hd, seq), f32),
            pltpu.VMEM((heads * hd, seq), bf16),
            pltpu.VMEM((seq, bq), f32),
            pltpu.VMEM((seq, bq), f32),
            pltpu.VMEM((seq, bq), bf16),
            pltpu.VMEM(w_in.shape[::-1], bf16),
            pltpu.VMEM((width, heads * 128), bf16),
        ],
        compiler_params=pltpu.CompilerParams(vmem_limit_bytes=60 << 20),
        name="col_attention",
    )(x, mask[None, :], w_in, w_out, w_opm)


NT = (((1,), (1,)), ((), ()))
TN = (((0,), (0,)), ((), ()))
NEG = -1e9 * LOG2E


def mm(a, b, dims=(((1,), (0,)), ((), ()))):
    return lax.dot_general(a, b, dims, preferred_element_type=f32)


def attend_kernel(flip, per_row_mask, x_ref, b_ref, mask_ref, win_ref, wout_ref, y_ref,
                  kk, qt, vt, sig, gat, bias, wt, qd0, qd1):
    tokens, width = x_ref.shape
    size = bias.shape[0]
    seqs = tokens // size
    heads = bias.shape[1] // size
    fold = gat.shape[0]
    hd = fold // heads
    c = hd ** -0.5 * LOG2E
    bp = min(512, tokens)

    wt[...] = jnp.transpose(win_ref[...])
    qd0[...] = jnp.zeros_like(qd0)
    qd1[...] = jnp.zeros_like(qd1)
    for h in range(heads):
        block = b_ref[pl.ds(h, size, stride=heads), :] * LOG2E
        bias[:, h * size:(h + 1) * size] = jnp.transpose(block) if flip else block

    def project(b, carry):
        rows = pl.ds(pl.multiple_of(b * bp, bp), bp)
        xn = norm_rows(x_ref[rows, :])
        kk[rows, :] = mm(xn, win_ref[:, fold:2 * fold]).astype(bf16)
        qt[:, rows] = mm(wt[:fold, :], xn, NT).astype(bf16)
        vt[:, rows] = mm(wt[2 * fold:3 * fold, :], xn, NT).astype(bf16)
        gg = mm(wt[3 * fold:, :], xn, NT).astype(bf16).astype(f32)
        sig[:, rows] = 1.0 / (1.0 + jnp.exp(-gg))
        return carry

    if tokens == bp:
        project(0, 0)
    else:
        lax.fori_loop(0, tokens // bp, project, 0)

    def one(s, qd):
        cols = pl.ds(pl.multiple_of(s * size, size), size)
        for h in range(heads):
            qd[h * hd:(h + 1) * hd, h * size:(h + 1) * size] = qt[h * hd:(h + 1) * hd, cols]
        mrow = mask_ref[pl.ds(s if per_row_mask else 0, 1), :]
        keep = jnp.transpose(jnp.broadcast_to(mrow.astype(f32), (size, size))) != 0
        for h in range(0, heads, 2):
            two = slice(h * size, (h + 2) * size)
            t = mm(kk[cols, :], qd[:, two]) * c + bias[:, two]
            t = jnp.where(jnp.concatenate([keep, keep], axis=1), t, NEG)
            e = jnp.exp2(t - jnp.max(t, axis=0, keepdims=True))
            total = jnp.sum(e, axis=0, keepdims=True)
            mixed = mm(vt[h * hd:(h + 2) * hd, cols], e.astype(bf16)) / total
            gat[h * hd:(h + 1) * hd, cols] = (mixed[:hd, :size] * sig[h * hd:(h + 1) * hd, cols]).astype(bf16)
            gat[(h + 1) * hd:(h + 2) * hd, cols] = (mixed[hd:, size:] * sig[(h + 1) * hd:(h + 2) * hd, cols]).astype(bf16)

    if seqs == 1:
        one(0, qd0)
    else:
        def pair(u, carry):
            one(2 * u, qd0)
            one(2 * u + 1, qd1)
            return carry
        lax.fori_loop(0, seqs // 2, pair, 0)

    def finish(b, carry):
        rows = pl.ds(pl.multiple_of(b * bp, bp), bp)
        up = mm(gat[:, rows], wout_ref[...], TN)
        y_ref[rows, :] = (x_ref[rows, :].astype(f32) + up).astype(bf16)
        return carry

    if tokens == bp:
        finish(0, 0)
    else:
        lax.fori_loop(0, tokens // bp, finish, 0)


def attend(x, bias, mask, w_in, w_out, flip, per_row_mask, name):
    tokens, width = x.shape
    size = bias.shape[2]
    heads = bias.shape[1]
    fold = w_out.shape[0]
    vm = pl.BlockSpec(memory_space=pltpu.VMEM)
    return pl.pallas_call(
        functools.partial(attend_kernel, flip, per_row_mask),
        out_shape=jax.ShapeDtypeStruct((tokens, width), bf16),
        in_specs=[vm] * 5,
        out_specs=vm,
        scratch_shapes=[
            pltpu.VMEM((tokens, fold), bf16),
            pltpu.VMEM((fold, tokens), bf16),
            pltpu.VMEM((fold, tokens), bf16),
            pltpu.VMEM((fold, tokens), f32),
            pltpu.VMEM((fold, tokens), bf16),
            pltpu.VMEM((size, heads * size), f32),
            pltpu.VMEM(w_in.shape[::-1], bf16),
            pltpu.VMEM((fold, heads * size), bf16),
            pltpu.VMEM((fold, heads * size), bf16),
        ],
        compiler_params=pltpu.CompilerParams(vmem_limit_bytes=40 << 20),
        name=name,
    )(x, bias.reshape(size * heads, size), mask, w_in, w_out)


def gather_slots(block, group, size):
    spread = jnp.broadcast_to(block[None], (size,) + block.shape)
    return lax.all_to_all(spread, group, 0, 0, tiled=True)


def head_bias(x_norm, weight):
    return jnp.einsum('jc,ch->hj', x_norm, weight, preferred_element_type=f32).astype(bf16)


def solution(mesh):
    dap_size = mesh.shape['dap']
    group = ('chip', 'dap')
    group_size = mesh.shape['chip'] * dap_size
    rows = P(('data', 'chip', 'dap'))
    in_specs = (rows, rows, P('data'), P('data')) + (P(),) * 13

    def per_device(m_blk, z_blk, msa_mask, res_mask, w_row_in, w_row_bias, w_row_out, w_col_in, w_col_out,
                   w_opm_in, w_opm_out, w_start_in, w_start_bias, w_start_out, w_end_in, w_end_bias, w_end_out):
        me = lax.axis_index('chip') * dap_size + lax.axis_index('dap')
        seqs, res, width = m_blk.shape
        total = seqs * group_size
        heads_m = w_row_bias.shape[1]
        opm = w_opm_in.shape[1] // 2
        res_row = res_mask[None, :]

        row_bias = gather_slots(head_bias(norm_rows(z_blk[0]), w_row_bias), group, group_size).astype(f32)
        seq_mask = lax.dynamic_slice_in_dim(msa_mask, me * seqs, seqs, axis=0)
        m_blk = attend(m_blk.reshape(seqs * res, width), row_bias, seq_mask, w_row_in, w_row_out, True, True, 'row_attention')

        m_cols = lax.all_to_all(m_blk.reshape(seqs, res, width), group, 1, 0, tiled=True)
        col_mask = lax.dynamic_slice_in_dim(msa_mask, me, 1, axis=1)[:, 0]
        m_cols, pieces = col_attention(m_cols.reshape(total, width), col_mask, w_col_in, w_col_out, w_opm_in, heads_m)

        left = pieces[:opm]
        right = lax.all_gather(pieces[opm:], group, axis=0, tiled=True)
        weight = msa_mask.astype(bf16)
        pair_norm = jnp.einsum('s,sj->j', col_mask.astype(bf16), weight, preferred_element_type=f32)
        outer = lax.dot_general(right, left, NT, preferred_element_type=f32).astype(bf16)
        outer = jnp.swapaxes(outer.reshape(res, opm, opm), 1, 2).reshape(res, opm * opm)
        update = jnp.dot(outer, w_opm_out, preferred_element_type=f32) / (1e-3 + pair_norm[:, None])
        z_row = (z_blk[0].astype(f32) + update).astype(bf16)

        start_bias = gather_slots(head_bias(norm_rows(z_row), w_start_bias), group, group_size).astype(f32)
        z_row = attend(z_row, start_bias, res_row, w_start_in, w_start_out, True, False, 'start_attention')

        z_col = lax.all_to_all(z_row[None], group, 1, 0, tiled=True)[:, 0]
        end_bias = gather_slots(head_bias(norm_rows(z_col), w_end_bias), group, group_size).astype(f32)
        z_col = attend(z_col, end_bias, res_row, w_end_in, w_end_out, True, False, 'end_attention')

        z_out = lax.all_to_all(z_col[:, None], group, 0, 1, tiled=True)
        m_out = lax.all_to_all(m_cols[:, None], group, 0, 1, tiled=True)
        return m_out, z_out

    return jax.shard_map(per_device, mesh=mesh, in_specs=in_specs, out_specs=(rows, rows), check_vma=False)
```

time: 1320 us -> 307 us (0.23)
  blocking collectives: 958 us -> 30.9 us
  matrix products: 149 us -> 14 us
  Pallas kernels: 0 us -> 61.9 us
  other arithmetic: 56.4 us -> 5.72 us
  waiting for transfers between devices: 105 us -> 129 us
  starting transfers between devices: 15 us -> 29.3 us
    all_gather x3 -> x0, blocking collectives: 958 us -> none  [the longest x1 321 us: per_device(): end_bias = lax.all_gather(end_bias, group, axis=1, tiled=True)]
    dot_general x75 -> x6, matrix products: 136 us -> 14 us  [the longest x1 10.9 us: per_device(): lax.dot_general(right, left, NT, preferred_element_type=f32).astype(bf16)]
    pallas_call x0 -> x4, Pallas kernels: none -> 61.9 us  [the longest x1 44.5 us: col_attention(): pl.pallas_call(col_kernel, out_shape=(jax.ShapeDtypeStruct((seq, width),...]
    reduce_sum x26 -> x5, other arithmetic: 43.2 us -> 2.29 us  [the longest x3 1.29 us: norm_rows(): variance = jnp.mean(centred * centred, axis=-1, keepdims=True)]
    all_to_all x0 -> x2, blocking collectives: none -> 30.9 us  [the longest x1 17.4 us: gather_slots(): return lax.all_to_all(spread, group, 0, 0, tiled=True)]
    all_to_all x4 -> x5, waiting for transfers between devices: 28.4 us -> 55.2 us  [the longest x2 17 us: gather_slots(): return lax.all_to_all(spread, group, 0, 0, tiled=True)]
    all_to_all x4 -> x5, starting transfers between devices: 15 us -> 29.1 us  [the longest x2 15.6 us: gather_slots(): return lax.all_to_all(spread, group, 0, 0, tiled=True)]
  transfers between devices with their start and end apart: 5 -> 6, of which waited for: 4 -> 6; matrix products, arithmetic and copies ran while one was open for 1% -> 5% of each run, Pallas kernels for 0% -> 0%
where the time goes in v2:
time: 307 us; the launch traced here: 306 us
  waiting for transfers between devices  129 us (42%)
  Pallas kernels  61.9 us (20%)
  blocking collectives  30.9 us (10%)
  starting transfers between devices  29.3 us (10%)
  local copies, waits for them, and re-layouts  20.3 us (7%)
  between operations  14.3 us (5%)
  matrix products  14 us (5%)
  other arithmetic  5.72 us (2%)
    all_gather x1, waiting for transfers between devices, per_device(): right = lax.all_gather(pieces[opm:], group, axis=0, tiled=True)  74 us
    pallas_call x1, Pallas kernels, col_attention(): pl.pallas_call(col_kernel, out_shape=(jax.ShapeDtypeStruct((seq, width),...  44.5 us
    pallas_call x3, Pallas kernels, attend(): pl.pallas_call(functools.partial(attend_kernel, flip, per_row_mask), out_...  17.4 us
    all_to_all x1, blocking collectives, gather_slots(): return lax.all_to_all(spread, group, 0, 0, tiled=True)  17.4 us
    all_to_all x2, waiting for transfers between devices, gather_slots(): return lax.all_to_all(spread, group, 0, 0, tiled=True)  17 us
    all_to_all x1, waiting for transfers between devices, per_device(): m_out = lax.all_to_all(m_cols[:, None], group, 0, 1, tiled=True)  16.8 us
    all_to_all x2, starting transfers between devices, gather_slots(): return lax.all_to_all(spread, group, 0, 0, tiled=True)  15.6 us
    all_to_all x1, waiting for transfers between devices, per_device(): lax.all_to_all(m_blk.reshape(seqs, res, width), group, 1, 0, tiled=True)  14.2 us
  transfers between devices with their start and end apart: 6, of which 6 were waited for; matrix products, arithmetic and copies ran while one was open for 5% of the time, Pallas kernels for 0%

profile of v2, /device:TPU:1, one launch (start us, length us, event | category | flops | bytes accessed | tf_op | source)
XLA Modules:
  0.0 305.7 jit_solution(12073064200738846331)
XLA Ops:
  10.8 11.5 %all-to-all-start = ((bf16[128,8,128]{2,1,0:T(8,128)(2,1)}), bf16[128,8,128]{2,1,0:T(8,128)(2,1)S(1)}, u32[]{:S(2)}, u32[]{:S(2)}) async-start(bf16[128,8,128]{2,1,0:T(8,128)(2,1)} %broadcast_in_dim.14), calls=%async_computation | async-start | bytes 524288 | tf_op jit(solution)/shard_map/all_to_all | solution.py:282
  23.0 10.0 %all-to-all-done = bf16[128,8,128]{2,1,0:T(8,128)(2,1)S(1)} async-done(((bf16[128,8,128]{2,1,0:T(8,128)(2,1)}), bf16[128,8,128]{2,1,0:T(8,128)(2,1)S(1)}, u32[]{:S(2)}, u32[]{:S(2)}) %all-to-all-start) | async-done | bytes 262176 | tf_op jit(solution)/shard_map/all_to_all | solution.py:282
  36.2 15.7 %row_attention.1 = bf16[2048,256]{1,0:T(8,128)(2,1)S(1)} custom-call(bf16[2048,256]{1,0:T(8,128)(2,1)S(1)} %bitcast.67, f32[1024,128]{1,0:T(8,128)S(1)} %bitcast_convert_fusion.b_ref, s32[16,128]{1,0:T(8,128)S(1)} %constant_dynamic-slice_fusion.mask_ref, bf16[256,1024]{1,0:T(8,128)(2,1)S(1)} %copy-done.2, bf16[256,256]{1,0:T(8,128)(2,1)S(1)} %copy-done.3), custom_call_target="tpu_custom_call" | custom-call | tf_op jit(solution)/shard_map/row_attention/pallas_call | solution.py:259
  51.9 1.6 copy.36
  53.4 4.2 %all-to-all-start.1 = ((bf16[16,128,256]{2,0,1:T(8,128)(2,1)}), bf16[16,128,256]{2,0,1:T(8,128)(2,1)S(1)}, u32[]{:S(2)}, u32[]{:S(2)}) async-start(bf16[16,128,256]{2,0,1:T(8,128)(2,1)} %copy.36), calls=%async_computation.1 | async-start | bytes 2097152 | tf_op jit(solution)/shard_map/all_to_all | solution.py:309
  57.8 1.5 copy.37.wopm_ref
  59.3 2.5 dynamic-slice_reduce_fusion
  61.8 14.2 %all-to-all-done.1 = bf16[16,128,256]{2,0,1:T(8,128)(2,1)S(1)} async-done(((bf16[16,128,256]{2,0,1:T(8,128)(2,1)}), bf16[16,128,256]{2,0,1:T(8,128)(2,1)S(1)}, u32[]{:S(2)}, u32[]{:S(2)}) %all-to-all-start.1) | async-done | bytes 1048608 | tf_op jit(solution)/shard_map/all_to_all | solution.py:309
  77.0 44.5 %col_attention.1 = (bf16[2048,256]{1,0:T(8,128)(2,1)}, bf16[64,2048]{1,0:T(8,128)(2,1)}) custom-call(bf16[2048,256]{1,0:T(8,128)(2,1)} %bitcast.74, s32[1,2048]{1,0:T(1,128)} %bitcast.79, bf16[256,1024]{1,0:T(8,128)(2,1)} %win_ref.5, bf16[256,256]{1,0:T(8,128)(2,1)} %wout_ref.5, bf16[256,64]{1,0:T(8,128)(2,1)} %copy.37.wopm_ref), custom_call_target="tpu_custom_call" | custom-call | tf_op jit(solution)/shard_map/col_attention/pallas_call | solution.py:152
  121.5 1.7 slice.6
  123.2 1.9 fusion.6
  125.0 1.4 fusion.5
  126.5 74.0 %all-gather.2.cloned.1.call-done = bf16[4096,2048]{1,0:T(8,128)(2,1)} async-done(((bf16[32,2048]{1,0:T(8,128)(2,1)}), bf16[4096,2048]{1,0:T(8,128)(2,1)}) %all-gather.2.cloned.1.call-update) | async-done | bytes 16777232 | tf_op jit(solution)/shard_map/all_gather | solution.py:314
  200.5 10.9 %convolution_convert_fusion = bf16[4096,32]{0,1:T(8,128)(2,1)S(1)} fusion(bf16[4096,2048]{1,0:T(8,128)(2,1)} %all-gather.2.cloned.1.call-done, bf16[64,2048]{1,0:T(8,128)(2,1)} %get-tuple-element.5), kind=kOutput, calls=%fused_computation | convolution fusion | flops 537001984 | bytes 17170432 | tf_op jit(solution)/shard_map/dot_general | solution.py:317
  213.4 17.4 %all_to_all.69 = bf16[128,4,128]{2,1,0:T(4,128)(2,1)S(1)} all-to-all(bf16[128,4,128]{2,1,0:T(4,128)(2,1)S(1)} %broadcast_in_dim.16), channel_id=1, replica_groups=mesh['data'=1,'chip'=2,'dap'=64] {'chip','dap'}, dimensions={0} | all-to-all | bytes 262144 | tf_op jit(solution)/shard_map/all_to_all | solution.py:282
  231.8 13.6 %all_to_all.70 = bf16[1,128,128]{2,0,1:T(2,128)(2,1)S(1)} all-to-all(bf16[1,128,128]{2,0,1:T(2,128)(2,1)S(1)} %copy.41), channel_id=1, replica_groups=mesh['data'=1,'chip'=2,'dap'=64] {'chip','dap'}, dimensions={1} | all-to-all | bytes 65536 | tf_op jit(solution)/shard_map/all_to_all | solution.py:325
  246.6 4.1 %all-to-all-start.5 = ((bf16[128,4,128]{2,1,0:T(4,128)(2,1)}), bf16[128,4,128]{2,1,0:T(4,128)(2,1)S(1)}, u32[]{:S(2)}, u32[]{:S(2)}) async-start(bf16[128,4,128]{2,1,0:T(4,128)(2,1)} %broadcast_in_dim.19), calls=%async_computation.5 | async-start | bytes 262144 | tf_op jit(solution)/shard_map/all_to_all | solution.py:282
  251.2 1.4 reduce.5
  253.7 7.0 %all-to-all-done.5 = bf16[128,4,128]{2,1,0:T(4,128)(2,1)S(1)} async-done(((bf16[128,4,128]{2,1,0:T(4,128)(2,1)}), bf16[128,4,128]{2,1,0:T(4,128)(2,1)S(1)}, u32[]{:S(2)}, u32[]{:S(2)}) %all-to-all-start.5) | async-done | bytes 131104 | tf_op jit(solution)/shard_map/all_to_all | solution.py:282
  260.7 4.0 %all-to-all-start.2 = ((bf16[128,2,2048]{2,1,0:T(2,128)(2,1)}), bf16[128,2,2048]{2,1,0:T(2,128)(2,1)S(1)}, u32[]{:S(2)}, u32[]{:S(2)}) async-start(bf16[128,2,2048]{2,1,0:T(2,128)(2,1)} %reshape.107), calls=%async_computation.2 | async-start | bytes 2097152 | tf_op jit(solution)/shard_map/all_to_all | solution.py:330
  266.3 16.8 %all-to-all-done.2 = bf16[128,2,2048]{2,1,0:T(2,128)(2,1)S(1)} async-done(((bf16[128,2,2048]{2,1,0:T(2,128)(2,1)}), bf16[128,2,2048]{2,1,0:T(2,128)(2,1)S(1)}, u32[]{:S(2)}, u32[]{:S(2)}) %all-to-all-start.2) | async-done | bytes 1048608 | tf_op jit(solution)/shard_map/all_to_all | solution.py:330
  283.1 5.4 %all-to-all-start.6 = ((bf16[128,1,128]{2,1,0:T(2,128)(2,1)}), bf16[128,1,128]{2,1,0:T(2,128)(2,1)S(1)}, u32[]{:S(2)}, u32[]{:S(2)}) async-start(bf16[128,1,128]{2,1,0:T(2,128)(2,1)} %copy.42), calls=%async_computation.6 | async-start | bytes 131072 | tf_op jit(solution)/shard_map/all_to_all | solution.py:329
  289.8 1.3 copy.43
  291.1 7.1 %all-to-all-done.6 = bf16[128,1,128]{2,1,0:T(2,128)(2,1)S(1)} async-done(((bf16[128,1,128]{2,1,0:T(2,128)(2,1)}), bf16[128,1,128]{2,1,0:T(2,128)(2,1)S(1)}, u32[]{:S(2)}, u32[]{:S(2)}) %all-to-all-start.6) | async-done | bytes 32800 | tf_op jit(solution)/shard_map/all_to_all | solution.py:329
  (64 shorter events, 18.0 us)
Async XLA Ops:
  7.2 205.4 %copy-start = (bf16[1024,128]{1,0:T(8,128)(2,1)S(1)}, bf16[1024,128]{1,0:T(8,128)(2,1)}, u32[]{:S(2)}) copy-start(bf16[1024,128]{1,0:T(8,128)(2,1)} %param.27) | copy-start | bytes 786436
  10.8 22.2 %all-to-all-start = ((bf16[128,8,128]{2,1,0:T(8,128)(2,1)}), bf16[128,8,128]{2,1,0:T(8,128)(2,1)S(1)}, u32[]{:S(2)}, u32[]{:S(2)}) async-start(bf16[128,8,128]{2,1,0:T(8,128)(2,1)} %broadcast_in_dim.14), calls=%async_computation | async-start | bytes 524288 | tf_op jit(solution)/shard_map/all_to_all | solution.py:282
  33.0 1.2 copy-start.1
  34.2 1.0 copy-start.2
  35.3 0.9 copy-start.3
  36.2 176.4 %copy-start.11 = (bf16[1,128,128]{2,1,0:T(8,128)(2,1)S(1)}, bf16[1,128,128]{2,1,0:T(8,128)(2,1)}, u32[]{:S(2)}) copy-start(bf16[1,128,128]{2,1,0:T(8,128)(2,1)} %param.18) | copy-start | bytes 98308
  36.2 176.9 %copy-start.12 = (bf16[128,4]{0,1:T(4,128)(2,1)S(1)}, bf16[128,4]{0,1:T(4,128)(2,1)}, u32[]{:S(2)}) copy-start(bf16[128,4]{0,1:T(4,128)(2,1)} %param.29) | copy-start | bytes 3076
  36.2 194.6 %copy-start.4 = (bf16[128,512]{1,0:T(8,128)(2,1)S(1)}, bf16[128,512]{1,0:T(8,128)(2,1)}, u32[]{:S(2)}) copy-start(bf16[128,512]{1,0:T(8,128)(2,1)} %win_ref.6) | copy-start | bytes 393220
  36.2 194.6 %copy-start.6 = (bf16[128,128]{1,0:T(8,128)(2,1)S(1)}, bf16[128,128]{1,0:T(8,128)(2,1)}, u32[]{:S(2)}) copy-start(bf16[128,128]{1,0:T(8,128)(2,1)} %wout_ref.6) | copy-start | bytes 98308
  36.2 194.6 %copy-start.8 = (s32[128]{0:T(128)S(1)}, s32[128]{0:T(128)}, u32[]{:S(2)}) copy-start(s32[128]{0:T(128)} %param.20) | copy-start | bytes 1540
  51.9 193.8 %copy-start.13 = (bf16[128,4]{0,1:T(4,128)(2,1)S(1)}, bf16[128,4]{0,1:T(4,128)(2,1)}, u32[]{:S(2)}) copy-start(bf16[128,4]{0,1:T(4,128)(2,1)} %param.32) | copy-start | bytes 3076
  53.4 22.6 %all-to-all-start.1 = ((bf16[16,128,256]{2,0,1:T(8,128)(2,1)}), bf16[16,128,256]{2,0,1:T(8,128)(2,1)S(1)}, u32[]{:S(2)}, u32[]{:S(2)}) async-start(bf16[16,128,256]{2,0,1:T(8,128)(2,1)} %copy.36), calls=%async_computation.1 | async-start | bytes 2097152 | tf_op jit(solution)/shard_map/all_to_all | solution.py:309
  57.6 142.9 %all-gather.2.cloned.1.call-start = ((), (), s32[]{:S(2)}) async-start(), calls=%async_computation.7 | async-start | bytes 16908288 | tf_op jit(solution)/shard_map/all_gather | solution.py:314
  76.0 1.0 copy-start.9
  77.0 187.7 %copy-start.5 = (bf16[128,512]{1,0:T(8,128)(2,1)S(1)}, bf16[128,512]{1,0:T(8,128)(2,1)}, u32[]{:S(2)}) copy-start(bf16[128,512]{1,0:T(8,128)(2,1)} %win_ref.7) | copy-start | bytes 393220
  77.0 187.7 %copy-start.7 = (bf16[128,128]{1,0:T(8,128)(2,1)S(1)}, bf16[128,128]{1,0:T(8,128)(2,1)}, u32[]{:S(2)}) copy-start(bf16[128,128]{1,0:T(8,128)(2,1)} %wout_ref.7) | copy-start | bytes 98308
  121.5 129.7 %copy-start.10 = (bf16[2048,256]{1,0:T(8,128)(2,1)S(1)}, bf16[2048,256]{1,0:T(8,128)(2,1)}, u32[]{:S(2)}) copy-start(bf16[2048,256]{1,0:T(8,128)(2,1)} %get-tuple-element.4) | copy-start | bytes 3145732
  246.6 14.2 %all-to-all-start.5 = ((bf16[128,4,128]{2,1,0:T(4,128)(2,1)}), bf16[128,4,128]{2,1,0:T(4,128)(2,1)S(1)}, u32[]{:S(2)}, u32[]{:S(2)}) async-start(bf16[128,4,128]{2,1,0:T(4,128)(2,1)} %broadcast_in_dim.19), calls=%async_computation.5 | async-start | bytes 262144 | tf_op jit(solution)/shard_map/all_to_all | solution.py:282
  260.7 22.4 %all-to-all-start.2 = ((bf16[128,2,2048]{2,1,0:T(2,128)(2,1)}), bf16[128,2,2048]{2,1,0:T(2,128)(2,1)S(1)}, u32[]{:S(2)}, u32[]{:S(2)}) async-start(bf16[128,2,2048]{2,1,0:T(2,128)(2,1)} %reshape.107), calls=%async_computation.2 | async-start | bytes 2097152 | tf_op jit(solution)/shard_map/all_to_all | solution.py:330
  283.1 15.2 %all-to-all-start.6 = ((bf16[128,1,128]{2,1,0:T(2,128)(2,1)}), bf16[128,1,128]{2,1,0:T(2,128)(2,1)S(1)}, u32[]{:S(2)}, u32[]{:S(2)}) async-start(bf16[128,1,128]{2,1,0:T(2,128)(2,1)} %copy.42), calls=%async_computation.6 | async-start | bytes 131072 | tf_op jit(solution)/shard_map/all_to_all | solution.py:329
Sparse Core Ops, SparseCore 0:
  123.3 77.1 all-gather.1

commit v3 on v2

--- a/solution.py
+++ b/solution.py
@@ -277,6 +277,218 @@
     )(x, bias.reshape(size * heads, size), mask, w_in, w_out)
 
 
+NN = (((1,), (0,)), ((), ()))
+MESH = pl.DeviceIdType.MESH
+INNER = 8
+SLOT = 8
+
+
+def place(t, dap):
+    return (0, t // dap, t % dap)
+
+
+def pair_project(x, win_ref, fold):
+    xn = norm_rows(x)
+    k = mm(xn, win_ref[:, fold:2 * fold]).astype(bf16)
+    qt = dot_t(win_ref[:, :fold], xn).astype(bf16)
+    vt = dot_t(win_ref[:, 2 * fold:3 * fold], xn).astype(bf16)
+    gg = dot_t(win_ref[:, 3 * fold:], xn).astype(bf16).astype(f32)
+    return k, qt, vt, 1.0 / (1.0 + jnp.exp(-gg))
+
+
+def pair_attend(x, parts, biases, keep, wout_ref):
+    k, qt, vt, sig = parts
+    heads = len(biases)
+    hd = vt.shape[0] // heads
+    c = hd ** -0.5 * LOG2E
+    gated = []
+    for h in range(heads):
+        part = slice(h * hd, (h + 1) * hd)
+        t = mm(k[:, part], qt[part]) * c + biases[h] * LOG2E
+        t = jnp.where(keep, t, NEG)
+        e = jnp.exp2(t - jnp.max(t, axis=0, keepdims=True))
+        mixed = mm(vt[part], e.astype(bf16)) / jnp.sum(e, axis=0, keepdims=True)
+        gated.append((mixed * sig[part]).astype(bf16))
+    up = mm(jnp.concatenate(gated, axis=0), wout_ref[...], TN)
+    return (x.astype(f32) + up).astype(bf16)
+
+
+def pair_kernel(group, dap, ac_ref, mcol_ref, z_ref, norm_ref, mask_ref, wopm_ref, ws_in, ws_bias, ws_out,
+                we_in, we_bias, we_out, mout, zout,
+                abuf, cbuf, oscr, uscr, usend, ubuf, zrow, bsend, bbuf, bscr, esend, ebuf, zsend, zfin, send, recv):
+    me = lax.axis_index('chip') * dap + lax.axis_index('dap')
+    hi, lo = me // INNER, me % INNER
+    outer_n = group // INNER
+    opm = ac_ref.shape[0] // 2
+    heads = ws_bias.shape[1]
+    fold = ws_out.shape[0]
+    size = z_ref.shape[0]
+    piece = mcol_ref.shape[0] // group
+
+    barrier = pltpu.get_barrier_semaphore()
+
+    def greet(o, carry):
+        pl.semaphore_signal(barrier, inc=1, device_id=place((me + o) % group, dap), device_id_type=MESH)
+        return carry
+
+    lax.fori_loop(1, group, greet, 0)
+
+    def remote(src, dst, i, t):
+        return pltpu.make_async_remote_copy(src_ref=src, dst_ref=dst, send_sem=send.at[i], recv_sem=recv.at[i],
+                                            device_id=place(t, dap), device_id_type=MESH)
+
+    def settle(buf, i, n):
+        done = remote(buf.at[pl.ds(0, n)], buf.at[pl.ds(0, n)], i, me)
+        done.wait_send()
+        done.wait_recv()
+
+    abuf[lo] = ac_ref[:opm, :]
+    cbuf[hi] = ac_ref[opm:, :]
+    keep = jnp.transpose(jnp.broadcast_to(mask_ref[...].astype(f32), (size, size))) != 0
+    pl.semaphore_wait(barrier, group - 1)
+
+    def share_a(o, carry):
+        remote(ac_ref.at[pl.ds(0, opm)], abuf.at[lo], 0, hi * INNER + (lo + o) % INNER).start()
+        return carry
+
+    def share_c(o, carry):
+        remote(ac_ref.at[pl.ds(opm, opm)], cbuf.at[hi], 1, (hi + o) % outer_n * INNER + lo).start()
+        return carry
+
+    def share_m(o, carry):
+        t = (me + o) % group
+        remote(mcol_ref.at[pl.ds(pl.multiple_of(t * piece, piece), piece)], mout.at[me], 2, t).start()
+        return carry
+
+    lax.fori_loop(1, outer_n, share_c, 0)
+    lax.fori_loop(1, INNER, share_a, 0)
+    settle(abuf, 0, INNER - 1)
+    settle(cbuf, 1, outer_n - 1)
+    mout[me] = mcol_ref[pl.ds(pl.multiple_of(me * piece, piece), piece), :]
+    lax.fori_loop(1, group, share_m, 0)
+
+    per = 128 // opm
+    outer = mm(abuf[...].reshape(INNER * opm, -1), cbuf[...].reshape(outer_n * opm, -1), NT)
+    for g in range(outer_n // per):
+        oscr[g] = outer[:, g * 128:(g + 1) * 128]
+    lane = lax.broadcasted_iota(jnp.int32, (opm // per * INNER, 128), 1) // opm
+    tiles = []
+    for g in range(outer_n // per):
+        slabs = [jnp.concatenate([oscr[g, pl.ds(b * per + r, INNER, stride=opm), :] for b in range(opm // per)], axis=0)
+                 for r in range(per)]
+        turned = [[slabs[r] if s == 0 else pltpu.roll(slabs[r], s * opm, 1) for s in range(per)] for r in range(per)]
+        for q in range(per):
+            pick = turned[0][(0 - q) % per]
+            for r in range(1, per):
+                pick = jnp.where(lane == r, turned[r][(r - q) % per], pick)
+            tiles.append(pick)
+    up = None
+    for b in range(opm // per):
+        block = jnp.concatenate([t[b * INNER:(b + 1) * INNER] for t in tiles], axis=0).astype(bf16)
+        term = mm(block, wopm_ref[b * 128:(b + 1) * 128, :])
+        up = term if up is None else up + term
+    uscr[...] = up
+    for x in range(INNER):
+        usend[x] = uscr[pl.ds(x, outer_n, stride=INNER), :]
+    ubuf[lo] = usend[lo]
+
+    def share_u(o, carry):
+        x = (lo + o) % INNER
+        remote(usend.at[x], ubuf.at[lo], 3, hi * INNER + x).start()
+        return carry
+
+    lax.fori_loop(1, INNER, share_u, 0)
+    settle(ubuf, 3, INNER - 1)
+    for x in range(INNER):
+        zrow[pl.ds(x, outer_n, stride=INNER), :] = ubuf[x]
+    z1 = (z_ref[...].astype(f32) + zrow[...] / (1e-3 + norm_ref[...])).astype(bf16)
+
+    def bias_rows(z, weight):
+        rows = dot_t(weight[...], norm_rows(z)).astype(bf16)
+        return jnp.concatenate([rows, jnp.zeros((SLOT - heads, size), bf16)], axis=0)
+
+    bsend[...] = bias_rows(z1, ws_bias)
+    bbuf[me] = bsend[...]
+
+    def share_b(o, carry):
+        remote(bsend, bbuf.at[me], 4, (me + o) % group).start()
+        return carry
+
+    lax.fori_loop(1, group, share_b, 0)
+    parts = pair_project(z1, ws_in, fold)
+    settle(bbuf, 4, group - 1)
+    bscr[...] = bbuf[...].astype(f32).reshape(group * SLOT, size)
+    biases = [jnp.transpose(bscr[pl.ds(h, size, stride=SLOT), :]) for h in range(heads)]
+    z2 = pair_attend(z1, parts, biases, keep, ws_out)
+
+    end_rows = bias_rows(z2, we_bias).astype(f32)
+    for h in range(heads):
+        bscr[pl.ds(h, size, stride=SLOT), :] = jnp.broadcast_to(end_rows[h:h + 1], (size, size))
+    bscr[pl.ds(heads, size, stride=SLOT), :] = z2.astype(f32)
+    esend[...] = bscr[...].astype(bf16).reshape(group, SLOT, size)
+    ebuf[me] = esend[me]
+
+    def share_e(o, carry):
+        t = (me + o) % group
+        remote(esend.at[t], ebuf.at[me], 5, t).start()
+        return carry
+
+    lax.fori_loop(1, group, share_e, 0)
+    settle(ebuf, 5, group - 1)
+    bscr[...] = ebuf[...].astype(f32).reshape(group * SLOT, size)
+    zc = bscr[pl.ds(heads, size, stride=SLOT), :].astype(bf16)
+    biases = [bscr[pl.ds(h, size, stride=SLOT), :] for h in range(heads)]
+    z3 = pair_attend(zc, pair_project(zc, we_in, fold), biases, keep, we_out)
+
+    zsend[...] = z3.astype(f32)
+    zfin[pl.ds(me, 1), :] = zsend[pl.ds(me, 1), :]
+
+    def share_z(o, carry):
+        t = (me + o) % group
+        remote(zsend.at[pl.ds(t, 1)], zfin.at[pl.ds(me, 1)], 6, t).start()
+        return carry
+
+    lax.fori_loop(1, group, share_z, 0)
+    settle(zfin, 6, group - 1)
+    zout[...] = zfin[...].astype(bf16)
+    settle(mout, 2, group - 1)
+
+
+def pair_update(ac, mcols, z, norm, mask, weights, group, dap):
+    vm = pl.BlockSpec(memory_space=pltpu.VMEM)
+    seq = ac.shape[1]
+    opm = ac.shape[0] // 2
+    size, width = z.shape
+    outer_n = group // INNER
+    piece = mcols.shape[0] // group
+    return pl.pallas_call(
+        functools.partial(pair_kernel, group, dap),
+        out_shape=(jax.ShapeDtypeStruct((group, piece, mcols.shape[1]), bf16), jax.ShapeDtypeStruct((size, width), bf16)),
+        in_specs=[vm] * 12,
+        out_specs=(vm, vm),
+        scratch_shapes=[
+            pltpu.VMEM((INNER, opm, seq), bf16),
+            pltpu.VMEM((outer_n, opm, seq), bf16),
+            pltpu.VMEM((outer_n * opm // 128, INNER * opm, 128), f32),
+            pltpu.VMEM((size, width), f32),
+            pltpu.VMEM((INNER, outer_n, width), f32),
+            pltpu.VMEM((INNER, outer_n, width), f32),
+            pltpu.VMEM((size, width), f32),
+            pltpu.VMEM((SLOT, size), bf16),
+            pltpu.VMEM((group, SLOT, size), bf16),
+            pltpu.VMEM((group * SLOT, size), f32),
+            pltpu.VMEM((group, SLOT, size), bf16),
+            pltpu.VMEM((group, SLOT, size), bf16),
+            pltpu.VMEM((size, width), f32),
+            pltpu.VMEM((size, width), f32),
+            pltpu.SemaphoreType.DMA((7,)),
+            pltpu.SemaphoreType.DMA((7,)),
+        ],
+        compiler_params=pltpu.CompilerParams(collective_id=1, has_side_effects=True, vmem_limit_bytes=40 << 20),
+        name='pair_update',
+    )(ac, mcols, z, norm, mask, *weights)
+
+
 def gather_slots(block, group, size):
     spread = jnp.broadcast_to(block[None], (size,) + block.shape)
     return lax.all_to_all(spread, group, 0, 0, tiled=True)
@@ -299,7 +511,6 @@
         seqs, res, width = m_blk.shape
         total = seqs * group_size
         heads_m = w_row_bias.shape[1]
-        opm = w_opm_in.shape[1] // 2
         res_row = res_mask[None, :]
 
         row_bias = gather_slots(head_bias(norm_rows(z_blk[0]), w_row_bias), group, group_size).astype(f32)
@@ -310,24 +521,12 @@
         col_mask = lax.dynamic_slice_in_dim(msa_mask, me, 1, axis=1)[:, 0]
         m_cols, pieces = col_attention(m_cols.reshape(total, width), col_mask, w_col_in, w_col_out, w_opm_in, heads_m)
 
-        left = pieces[:opm]
-        right = lax.all_gather(pieces[opm:], group, axis=0, tiled=True)
         weight = msa_mask.astype(bf16)
         pair_norm = jnp.einsum('s,sj->j', col_mask.astype(bf16), weight, preferred_element_type=f32)
-        outer = lax.dot_general(right, left, NT, preferred_element_type=f32).astype(bf16)
-        outer = jnp.swapaxes(outer.reshape(res, opm, opm), 1, 2).reshape(res, opm * opm)
-        update = jnp.dot(outer, w_opm_out, preferred_element_type=f32) / (1e-3 + pair_norm[:, None])
-        z_row = (z_blk[0].astype(f32) + update).astype(bf16)
-
-        start_bias = gather_slots(head_bias(norm_rows(z_row), w_start_bias), group, group_size).astype(f32)
-        z_row = attend(z_row, start_bias, res_row, w_start_in, w_start_out, True, False, 'start_attention')
-
-        z_col = lax.all_to_all(z_row[None], group, 1, 0, tiled=True)[:, 0]
-        end_bias = gather_slots(head_bias(norm_rows(z_col), w_end_bias), group, group_size).astype(f32)
-        z_col = attend(z_col, end_bias, res_row, w_end_in, w_end_out, True, False, 'end_attention')
-
-        z_out = lax.all_to_all(z_col[:, None], group, 0, 1, tiled=True)
-        m_out = lax.all_to_all(m_cols[:, None], group, 0, 1, tiled=True)
+        pair_norm = jnp.broadcast_to(pair_norm[:, None], (res, z_blk.shape[2]))
+        weights = (w_opm_out, w_start_in, w_start_bias, w_start_out, w_end_in, w_end_bias, w_end_out)
+        m_slots, z_out = pair_update(pieces, m_cols, z_blk[0], pair_norm, res_row, weights, group_size, dap_size)
+        m_out, z_out = jnp.swapaxes(m_slots, 0, 1), z_out[None]
         return m_out, z_out
 
     return jax.shard_map(per_device, mesh=mesh, in_specs=in_specs, out_specs=(rows, rows), check_vma=False)

time: 307 us -> 201 us (0.65)
  waiting for transfers between devices: 129 us -> 24 us
  Pallas kernels: 61.9 us -> 146 us
  blocking collectives: 30.9 us -> 0 us
  matrix products: 14 us -> 0.4 us
  starting transfers between devices: 29.3 us -> 15.8 us
  between operations: 14.3 us -> 0.84 us
  local copies, waits for them, and re-layouts: 20.3 us -> 12.4 us
  other arithmetic: 5.72 us -> 1.81 us
    pallas_call x0 -> x1, Pallas kernels: none -> 85.4 us  [pair_update(): pl.pallas_call(functools.partial(pair_kernel, group, dap), out_shape=(jax...]
    all_gather x1 -> x0, waiting for transfers between devices: 74 us -> none  [per_device(): right = lax.all_gather(pieces[opm:], group, axis=0, tiled=True)]
    all_to_all x2 -> x0, blocking collectives: 30.9 us -> none  [the longest x1 17.4 us: gather_slots(): return lax.all_to_all(spread, group, 0, 0, tiled=True)]
    all_to_all x2 -> x0, waiting for transfers between devices: 24 us -> none  [the longest x1 16.8 us: per_device(): m_out = lax.all_to_all(m_cols[:, None], group, 0, 1, tiled=True)]
    dot_general x2 -> x0, matrix products: 11.2 us -> none  [the longest x1 10.9 us: per_device(): lax.dot_general(right, left, NT, preferred_element_type=f32).astype(bf16)]
    all_to_all x2 -> x0, starting transfers between devices: 9.35 us -> none  [the longest x1 5.4 us: per_device(): z_out = lax.all_to_all(z_col[:, None], group, 0, 1, tiled=True)]
    all_to_all x2 -> x1, waiting for transfers between devices: 17 us -> 9.89 us  [gather_slots(): return lax.all_to_all(spread, group, 0, 0, tiled=True)]
    all_to_all x2 -> x1, starting transfers between devices: 15.6 us -> 11.5 us  [gather_slots(): return lax.all_to_all(spread, group, 0, 0, tiled=True)]
  transfers between devices with their start and end apart: 6 -> 2, of which waited for: 6 -> 2; matrix products, arithmetic and copies ran while one was open for 5% -> 2% of each run, Pallas kernels for 0% -> 0%
where the time goes in v3:
time: 201 us
  Pallas kernels  146 us (73%)
  waiting for transfers between devices  24 us (12%)
  starting transfers between devices  15.8 us (8%)
  local copies, waits for them, and re-layouts  12.4 us (6%)
    pallas_call x1, Pallas kernels, pair_update(): pl.pallas_call(functools.partial(pair_kernel, group, dap), out_shape=(jax...  85.4 us
    pallas_call x1, Pallas kernels, col_attention(): pl.pallas_call(col_kernel, out_shape=(jax.ShapeDtypeStruct((seq, width),...  44.5 us
    pallas_call x1, Pallas kernels, attend(): pl.pallas_call(functools.partial(attend_kernel, flip, per_row_mask), out_...  15.7 us
    all_to_all x1, waiting for transfers between devices, per_device(): lax.all_to_all(m_blk.reshape(seqs, res, width), group, 1, 0, tiled=True)  14.1 us
    all_to_all x1, starting transfers between devices, gather_slots(): return lax.all_to_all(spread, group, 0, 0, tiled=True)  11.5 us
    all_to_all x1, waiting for transfers between devices, gather_slots(): return lax.all_to_all(spread, group, 0, 0, tiled=True)  9.89 us
    unnamed x41, local copies, waits for them, and re-layouts  8 us
    all_to_all x1, starting transfers between devices, per_device(): lax.all_to_all(m_blk.reshape(seqs, res, width), group, 1, 0, tiled=True)  4.3 us
  transfers between devices with their start and end apart: 2, of which 2 were waited for; matrix products, arithmetic and copies ran while one was open for 2% of the time, Pallas kernels for 0%

profile of v3, /device:TPU:1, one launch (start us, length us, event | category | flops | bytes accessed | tf_op | source)
XLA Modules:
  0.0 200.8 jit_solution(15887393698859444990)
XLA Ops:
  0.7 0.9 convert_reduce_fusion
  1.8 0.2 fusion
  2.1 0.7 broadcast_in_dim.8
  2.8 11.5 %all-to-all-start = ((bf16[128,8,128]{2,1,0:T(8,128)(2,1)}), bf16[128,8,128]{2,1,0:T(8,128)(2,1)S(1)}, u32[]{:S(2)}, u32[]{:S(2)}) async-start(bf16[128,8,128]{2,1,0:T(8,128)(2,1)} %broadcast_in_dim.8), calls=%async_computation | async-start | bytes 524288 | tf_op jit(solution)/shard_map/all_to_all | solution.py:494
  14.3 0.8 constant_dynamic-slice_fusion.mask_ref
  15.1 9.9 %all-to-all-done = bf16[128,8,128]{2,1,0:T(8,128)(2,1)S(1)} async-done(((bf16[128,8,128]{2,1,0:T(8,128)(2,1)}), bf16[128,8,128]{2,1,0:T(8,128)(2,1)S(1)}, u32[]{:S(2)}, u32[]{:S(2)}) %all-to-all-start) | async-done | bytes 262176 | tf_op jit(solution)/shard_map/all_to_all | solution.py:494
  25.1 15.7 %row_attention.1 = bf16[2048,256]{1,0:T(8,128)(2,1)S(1)} custom-call(bf16[2048,256]{1,0:T(8,128)(2,1)S(1)} %bitcast.28, f32[1024,128]{1,0:T(8,128)S(1)} %bitcast_convert_fusion.b_ref, s32[16,128]{1,0:T(8,128)S(1)} %constant_dynamic-slice_fusion.mask_ref, bf16[256,1024]{1,0:T(8,128)(2,1)S(1)} %copy-done.3, bf16[256,256]{1,0:T(8,128)(2,1)S(1)} %copy-done.7), custom_call_target="tpu_custom_call" | custom-call | tf_op jit(solution)/shard_map/row_attention/pallas_call | solution.py:259
  40.7 1.6 copy.24
  42.3 4.3 %all-to-all-start.1 = ((bf16[16,128,256]{2,0,1:T(8,128)(2,1)}), bf16[16,128,256]{2,0,1:T(8,128)(2,1)S(1)}, u32[]{:S(2)}, u32[]{:S(2)}) async-start(bf16[16,128,256]{2,0,1:T(8,128)(2,1)} %copy.24), calls=%async_computation.1 | async-start | bytes 2097152 | tf_op jit(solution)/shard_map/all_to_all | solution.py:520
  46.6 0.7 copy.25.wopm_ref
  47.3 0.6 fusion.1
  48.0 0.7 copy-done.16
  48.8 0.5 copy-done.17
  49.5 1.2 dynamic-slice_reduce_fusion
  50.7 0.2 convolution_bitcast_fusion
  50.9 14.1 %all-to-all-done.1 = bf16[16,128,256]{2,0,1:T(8,128)(2,1)S(1)} async-done(((bf16[16,128,256]{2,0,1:T(8,128)(2,1)}), bf16[16,128,256]{2,0,1:T(8,128)(2,1)S(1)}, u32[]{:S(2)}, u32[]{:S(2)}) %all-to-all-start.1) | async-done | bytes 1048608 | tf_op jit(solution)/shard_map/all_to_all | solution.py:520
  65.0 1.0 copy-done.14
  66.0 44.5 %col_attention.1 = (bf16[2048,256]{1,0:T(8,128)(2,1)}, bf16[64,2048]{1,0:T(8,128)(2,1)}) custom-call(bf16[2048,256]{1,0:T(8,128)(2,1)} %bitcast.33, s32[1,2048]{1,0:T(1,128)} %bitcast.34, bf16[256,1024]{1,0:T(8,128)(2,1)} %win_ref.3, bf16[256,256]{1,0:T(8,128)(2,1)} %wout_ref.3, bf16[256,64]{1,0:T(8,128)(2,1)} %copy.25.wopm_ref), custom_call_target="tpu_custom_call" | custom-call | tf_op jit(solution)/shard_map/col_attention/pallas_call | solution.py:152
  110.6 0.6 copy-done.10
  111.3 1.2 copy-done.2
  112.5 0.9 copy-done.6
  113.4 85.4 %pair_update.1 = (bf16[128,16,256]{2,1,0:T(8,128)(2,1)S(1)}, bf16[128,128]{1,0:T(8,128)(2,1)S(1)}) custom-call(bf16[64,2048]{1,0:T(8,128)(2,1)S(1)} %copy-done.6, bf16[2048,256]{1,0:T(8,128)(2,1)S(1)} %copy-done.2, bf16[128,128]{1,0:T(8,128)(2,1)S(1)} %bitcast.30, f32[128,128]{1,0:T(8,128)S(1)} %broadcast_in_dim.9.norm_ref, s32[1,128]{1,0:T(1,128)S(1)} %bitcast.32, ...), custom_call_target="tpu_custom_call" | custom-call | tf_op jit(solution)/shard_map/pair_update/pallas_call | solution.py:464
  198.8 1.3 copy.28
  200.2 0.6 copy.30
  (38 shorter events, 0.6 us)
Async XLA Ops:
  0.6 1.2 copy-start
  0.6 1.0 copy-start.4
  0.7 24.4 %copy-start.1 = (bf16[16,128,256]{2,1,0:T(8,128)(2,1)S(1)}, bf16[16,128,256]{2,1,0:T(8,128)(2,1)}, u32[]{:S(2)}) copy-start(bf16[16,128,256]{2,1,0:T(8,128)(2,1)} %param.17) | copy-start | bytes 3145732
  2.8 22.2 %all-to-all-start = ((bf16[128,8,128]{2,1,0:T(8,128)(2,1)}), bf16[128,8,128]{2,1,0:T(8,128)(2,1)S(1)}, u32[]{:S(2)}, u32[]{:S(2)}) async-start(bf16[128,8,128]{2,1,0:T(8,128)(2,1)} %broadcast_in_dim.8), calls=%async_computation | async-start | bytes 524288 | tf_op jit(solution)/shard_map/all_to_all | solution.py:494
  14.3 10.7 %copy-start.3 = (bf16[256,1024]{1,0:T(8,128)(2,1)S(1)}, bf16[256,1024]{1,0:T(8,128)(2,1)}, u32[]{:S(2)}) copy-start(bf16[256,1024]{1,0:T(8,128)(2,1)} %win_ref.2) | copy-start | bytes 1572868
  15.1 10.0 %copy-start.7 = (bf16[256,256]{1,0:T(8,128)(2,1)S(1)}, bf16[256,256]{1,0:T(8,128)(2,1)}, u32[]{:S(2)}) copy-start(bf16[256,256]{1,0:T(8,128)(2,1)} %wout_ref.2) | copy-start | bytes 393220
  42.3 4.3 %copy-start.15 = (bf16[256,64]{0,1:T(8,128)(2,1)S(1)}, bf16[256,64]{0,1:T(8,128)(2,1)}, u32[]{:S(2)}) copy-start(bf16[256,64]{0,1:T(8,128)(2,1)} %param.26) | copy-start | bytes 98308
  42.3 5.1 %copy-start.13 = (s32[2048,128]{1,0:T(8,128)S(1)}, s32[2048,128]{1,0:T(8,128)}, u32[]{:S(2)}) copy-start(s32[2048,128]{1,0:T(8,128)} %param.19) | copy-start | bytes 3145732
  42.3 22.7 %all-to-all-start.1 = ((bf16[16,128,256]{2,0,1:T(8,128)(2,1)}), bf16[16,128,256]{2,0,1:T(8,128)(2,1)S(1)}, u32[]{:S(2)}, u32[]{:S(2)}) async-start(bf16[16,128,256]{2,0,1:T(8,128)(2,1)} %copy.24), calls=%async_computation.1 | async-start | bytes 2097152 | tf_op jit(solution)/shard_map/all_to_all | solution.py:520
  48.0 0.7 copy-start.16
  48.7 0.7 copy-start.17
  65.0 1.0 copy-start.14
  66.0 44.6 %copy-start.5 = (bf16[1024,128]{1,0:T(8,128)(2,1)S(1)}, bf16[1024,128]{1,0:T(8,128)(2,1)}, u32[]{:S(2)}) copy-start(bf16[1024,128]{1,0:T(8,128)(2,1)} %wopm_ref.2) | copy-start | bytes 786436
  66.0 44.6 %copy-start.8 = (bf16[128,512]{1,0:T(8,128)(2,1)S(1)}, bf16[128,512]{1,0:T(8,128)(2,1)}, u32[]{:S(2)}) copy-start(bf16[128,512]{1,0:T(8,128)(2,1)} %ws_in.1) | copy-start | bytes 393220
  66.0 44.6 %copy-start.9 = (bf16[128,512]{1,0:T(8,128)(2,1)S(1)}, bf16[128,512]{1,0:T(8,128)(2,1)}, u32[]{:S(2)}) copy-start(bf16[128,512]{1,0:T(8,128)(2,1)} %we_in.1) | copy-start | bytes 393220
  110.5 0.8 copy-start.10
  110.5 0.8 copy-start.11
  110.6 0.7 copy-start.12
  111.3 1.2 copy-start.2
  112.5 0.9 copy-start.6

commit v4 on v3

v4 whole, which is shorter than its diff:
```python
import functools

import jax
import jax.numpy as jnp
import numpy as np
from jax import lax
from jax.experimental import pallas as pl
from jax.experimental.pallas import tpu as pltpu
from jax.sharding import PartitionSpec as P

LOG2E = 1.4426950408889634
f32, bf16 = jnp.float32, jnp.bfloat16


def split3(value):
    parts = []
    rest = np.float64(value)
    for _ in range(3):
        part = np.float64(np.asarray(rest, dtype=jnp.bfloat16))
        parts.append(float(part))
        rest = rest - part
    return parts


def norm_rows(x):
    values = x.astype(f32)
    centred = values - jnp.mean(values, axis=-1, keepdims=True)
    variance = jnp.mean(centred * centred, axis=-1, keepdims=True)
    return (centred * lax.rsqrt(variance + 1e-5)).astype(bf16)


def dot_t(w, x):
    return lax.dot_general(w, x, (((0,), (1,)), ((), ())), preferred_element_type=f32)


NT = (((1,), (1,)), ((), ()))
TN = (((0,), (0,)), ((), ()))
NEG = -1e9 * LOG2E


def mm(a, b, dims=(((1,), (0,)), ((), ()))):
    return lax.dot_general(a, b, dims, preferred_element_type=f32)


def attend_kernel(flip, per_row_mask, x_ref, b_ref, mask_ref, win_ref, wout_ref, y_ref,
                  kk, qt, vt, sig, gat, bias, wt, qd0, qd1):
    tokens, width = x_ref.shape
    size = bias.shape[0]
    seqs = tokens // size
    heads = bias.shape[1] // size
    fold = gat.shape[0]
    hd = fold // heads
    c = hd ** -0.5 * LOG2E
    bp = min(512, tokens)

    wt[...] = jnp.transpose(win_ref[...])
    qd0[...] = jnp.zeros_like(qd0)
    qd1[...] = jnp.zeros_like(qd1)
    for h in range(heads):
        block = b_ref[pl.ds(h, size, stride=heads), :] * LOG2E
        bias[:, h * size:(h + 1) * size] = jnp.transpose(block) if flip else block

    def project(b, carry):
        rows = pl.ds(pl.multiple_of(b * bp, bp), bp)
        xn = norm_rows(x_ref[rows, :])
        kk[rows, :] = mm(xn, win_ref[:, fold:2 * fold]).astype(bf16)
        qt[:, rows] = mm(wt[:fold, :], xn, NT).astype(bf16)
        vt[:, rows] = mm(wt[2 * fold:3 * fold, :], xn, NT).astype(bf16)
        gg = mm(wt[3 * fold:, :], xn, NT).astype(bf16).astype(f32)
        sig[:, rows] = 1.0 / (1.0 + jnp.exp(-gg))
        return carry

    if tokens == bp:
        project(0, 0)
    else:
        lax.fori_loop(0, tokens // bp, project, 0)

    def one(s, qd):
        cols = pl.ds(pl.multiple_of(s * size, size), size)
        for h in range(heads):
            qd[h * hd:(h + 1) * hd, h * size:(h + 1) * size] = qt[h * hd:(h + 1) * hd, cols]
        mrow = mask_ref[pl.ds(s if per_row_mask else 0, 1), :]
        keep = jnp.transpose(jnp.broadcast_to(mrow.astype(f32), (size, size))) != 0
        for h in range(0, heads, 2):
            two = slice(h * size, (h + 2) * size)
            t = mm(kk[cols, :], qd[:, two]) * c + bias[:, two]
            t = jnp.where(jnp.concatenate([keep, keep], axis=1), t, NEG)
            e = jnp.exp2(t - jnp.max(t, axis=0, keepdims=True))
            total = jnp.sum(e, axis=0, keepdims=True)
            mixed = mm(vt[h * hd:(h + 2) * hd, cols], e.astype(bf16)) / total
            gat[h * hd:(h + 1) * hd, cols] = (mixed[:hd, :size] * sig[h * hd:(h + 1) * hd, cols]).astype(bf16)
            gat[(h + 1) * hd:(h + 2) * hd, cols] = (mixed[hd:, size:] * sig[(h + 1) * hd:(h + 2) * hd, cols]).astype(bf16)

    if seqs == 1:
        one(0, qd0)
    else:
        def pair(u, carry):
            one(2 * u, qd0)
            one(2 * u + 1, qd1)
            return carry
        lax.fori_loop(0, seqs // 2, pair, 0)

    def finish(b, carry):
        rows = pl.ds(pl.multiple_of(b * bp, bp), bp)
        up = mm(gat[:, rows], wout_ref[...], TN)
        y_ref[rows, :] = (x_ref[rows, :].astype(f32) + up).astype(bf16)
        return carry

    if tokens == bp:
        finish(0, 0)
    else:
        lax.fori_loop(0, tokens // bp, finish, 0)


def attend(x, bias, mask, w_in, w_out, flip, per_row_mask, name):
    tokens, width = x.shape
    size = bias.shape[2]
    heads = bias.shape[1]
    fold = w_out.shape[0]
    vm = pl.BlockSpec(memory_space=pltpu.VMEM)
    return pl.pallas_call(
        functools.partial(attend_kernel, flip, per_row_mask),
        out_shape=jax.ShapeDtypeStruct((tokens, width), bf16),
        in_specs=[vm] * 5,
        out_specs=vm,
        scratch_shapes=[
            pltpu.VMEM((tokens, fold), bf16),
            pltpu.VMEM((fold, tokens), bf16),
            pltpu.VMEM((fold, tokens), bf16),
            pltpu.VMEM((fold, tokens), f32),
            pltpu.VMEM((fold, tokens), bf16),
            pltpu.VMEM((size, heads * size), f32),
            pltpu.VMEM(w_in.shape[::-1], bf16),
            pltpu.VMEM((fold, heads * size), bf16),
            pltpu.VMEM((fold, heads * size), bf16),
        ],
        compiler_params=pltpu.CompilerParams(vmem_limit_bytes=40 << 20),
        name=name,
    )(x, bias.reshape(size * heads, size), mask, w_in, w_out)


NN = (((1,), (0,)), ((), ()))
MESH = pl.DeviceIdType.MESH
INNER = 8
SLOT = 8


def place(t, dap):
    return (0, t // dap, t % dap)


def pair_project(x, win_ref, fold):
    xn = norm_rows(x)
    k = mm(xn, win_ref[:, fold:2 * fold]).astype(bf16)
    qt = dot_t(win_ref[:, :fold], xn).astype(bf16)
    vt = dot_t(win_ref[:, 2 * fold:3 * fold], xn).astype(bf16)
    gg = dot_t(win_ref[:, 3 * fold:], xn).astype(bf16).astype(f32)
    return k, qt, vt, 1.0 / (1.0 + jnp.exp(-gg))


def pair_attend(x, parts, biases, keep, wout_ref):
    k, qt, vt, sig = parts
    heads = len(biases)
    hd = vt.shape[0] // heads
    c = hd ** -0.5 * LOG2E
    gated = []
    for h in range(heads):
        part = slice(h * hd, (h + 1) * hd)
        t = mm(k[:, part], qt[part]) * c + biases[h] * LOG2E
        t = jnp.where(keep, t, NEG)
        e = jnp.exp2(t - jnp.max(t, axis=0, keepdims=True))
        mixed = mm(vt[part], e.astype(bf16)) / jnp.sum(e, axis=0, keepdims=True)
        gated.append((mixed * sig[part]).astype(bf16))
    up = mm(jnp.concatenate(gated, axis=0), wout_ref[...], TN)
    return (x.astype(f32) + up).astype(bf16)


def col_stage(x_ref, mrow_ref, win_ref, wout_ref, wopm_ref, emit,
              kaug, qaug, vt, sig, gat, s0, s1, wt, wka):
    seq, width = x_ref.shape
    heads, hd = vt.shape[0], vt.shape[1]
    fold = heads * hd
    bq = s0.shape[1]
    nq = seq // bq
    kc = 256
    nk = seq // kc
    c = hd ** -0.5 * LOG2E
    masked = split3(-1e9 * LOG2E)

    lane = lax.broadcasted_iota(jnp.int32, (bq, 128), 1)
    row = lax.broadcasted_iota(jnp.int32, (128 - 3 * hd, bq), 0)
    fill = jnp.where(row == 0, masked[0], jnp.where(row == 1, masked[1], jnp.where(row == 2, masked[2], 0.0))).astype(bf16)
    flag = ((lane >= 3 * hd) & (lane < 3 * hd + 3)).astype(f32)
    flag2 = jnp.concatenate([flag, flag], axis=1)

    wt[...] = jnp.transpose(win_ref[...])
    for h in range(heads):
        wk = win_ref[:, fold + h * hd:fold + (h + 1) * hd]
        wka[:, h * 128:(h + 1) * 128] = jnp.concatenate([wk, wk, wk, jnp.zeros_like(wk)], axis=1)
    wopm_t = jnp.transpose(wopm_ref[...])

    def project(b, carry):
        rows = pl.ds(pl.multiple_of(b * bq, bq), bq)
        xn = norm_rows(x_ref[rows, :])
        keep = jnp.transpose(jnp.broadcast_to(mrow_ref[:, rows], (128, bq)).astype(f32)) != 0
        keep2 = jnp.concatenate([keep, keep], axis=1)
        for h in range(0, heads, 2):
            k = mm(xn, wka[:, h * 128:(h + 2) * 128])
            k = jnp.where(keep2, k, flag2).astype(bf16)
            kaug[h, rows, :] = k[:, :128]
            kaug[h + 1, rows, :] = k[:, 128:]
        qt = mm(wt[:fold, :], xn, NT).astype(bf16).astype(f32) * c
        hi = qt.astype(bf16)
        rest = qt - hi.astype(f32)
        mid = rest.astype(bf16)
        low = (rest - mid.astype(f32)).astype(bf16)
        vv = mm(wt[2 * fold:3 * fold, :], xn, NT).astype(bf16)
        gg = mm(wt[3 * fold:, :], xn, NT).astype(bf16).astype(f32)
        gg = 1.0 / (1.0 + jnp.exp(-gg))
        for h in range(heads):
            part = slice(h * hd, (h + 1) * hd)
            qaug[h, 0:hd, rows] = hi[part]
            qaug[h, hd:2 * hd, rows] = mid[part]
            qaug[h, 2 * hd:3 * hd, rows] = low[part]
            qaug[h, 3 * hd:, rows] = fill
            vt[h, :, rows] = vv[part]
            sig[h, :, rows] = gg[part]
        return carry

    lax.fori_loop(0, nq, project, 0)

    def fold8(s):
        return s.reshape(kc // 8, 8, bq)

    def chunk_scores(h, q, i, buf, m):
        s = mm(kaug[h, i * kc:(i + 1) * kc, :], q)
        buf[i * kc:(i + 1) * kc, :] = s
        top = jnp.max(fold8(s), axis=0)
        return top if m is None else jnp.maximum(m, top)

    def step(qb, h, cur, nxt, m):
        t = jnp.minimum(qb * heads + h + 1, nq * heads - 1)
        hn = t % heads
        q = qaug[hn, :, pl.ds(pl.multiple_of(t // heads * bq, bq), bq)]
        top = jnp.max(m, axis=0, keepdims=True)
        mn = None
        total = jnp.zeros((8, bq), f32)
        mixed = jnp.zeros((hd, bq), f32)
        for i in range(nk):
            mn = chunk_scores(hn, q, i, nxt, mn)
            e = jnp.exp2(cur[i * kc:(i + 1) * kc, :] - top)
            total = total + jnp.sum(fold8(e), axis=0)
            mixed = mixed + mm(vt[h, :, i * kc:(i + 1) * kc], e.astype(bf16))
        cols = pl.ds(pl.multiple_of(qb * bq, bq), bq)
        mixed = mixed / jnp.sum(total, axis=0, keepdims=True)
        gat[pl.ds(pl.multiple_of(h * hd, hd), hd), :] = (mixed * sig[h, :, cols]).astype(bf16)
        return mn

    m = None
    for i in range(nk):
        m = chunk_scores(0, qaug[0, :, 0:bq], i, s0, m)

    def block(qb, m):
        def pair(u, m):
            m = step(qb, 2 * u, s0, s1, m)
            return step(qb, 2 * u + 1, s1, s0, m)

        m = lax.fori_loop(0, heads // 2, pair, m)
        rows = pl.ds(pl.multiple_of(qb * bq, bq), bq)
        y = (x_ref[rows, :].astype(f32) + mm(gat[...], wout_ref[...], TN)).astype(bf16)
        ac = mm(wopm_t, norm_rows(y), NT).astype(bf16)
        emit(qb, y, (ac.astype(f32) * mrow_ref[:, rows].astype(f32)).astype(bf16))
        return m

    lax.fori_loop(0, nq, block, m)


class Links:
    def __init__(self, group, dap, send, recv):
        self.group, self.dap, self.send, self.recv = group, dap, send, recv
        self.me = lax.axis_index('chip') * dap + lax.axis_index('dap')
        self.hi, self.lo = self.me // INNER, self.me % INNER
        self.outer_n = group // INNER

    def greet(self):
        barrier = pltpu.get_barrier_semaphore()

        def one(o, carry):
            pl.semaphore_signal(barrier, inc=1, device_id=place((self.me + o) % self.group, self.dap), device_id_type=MESH)
            return carry

        lax.fori_loop(1, self.group, one, 0)

    def ready(self):
        pl.semaphore_wait(pltpu.get_barrier_semaphore(), self.group - 1)

    def copy(self, src, dst, i, t):
        return pltpu.make_async_remote_copy(src_ref=src, dst_ref=dst, send_sem=self.send.at[i], recv_sem=self.recv.at[i],
                                            device_id=place(t, self.dap), device_id_type=MESH)

    def settle(self, part, i):
        done = self.copy(part, part, i, self.me)
        done.wait_send()
        done.wait_recv()

    def to_all(self, make, i):
        def one(o, carry):
            t = (self.me + o) % self.group
            src, dst = make(t)
            self.copy(src, dst, i, t).start()
            return carry

        lax.fori_loop(1, self.group, one, 0)

    def to_inner(self, make, i):
        def one(o, carry):
            x = (self.lo + o) % INNER
            src, dst = make(x)
            self.copy(src, dst, i, self.hi * INNER + x).start()
            return carry

        lax.fori_loop(1, INNER, one, 0)

    def to_outer(self, make, i):
        def one(o, carry):
            src, dst = make()
            self.copy(src, dst, i, (self.hi + o) % self.outer_n * INNER + self.lo).start()
            return carry

        lax.fori_loop(1, self.outer_n, one, 0)


def pair_stage(net, z_ref, norm_ref, mask_ref, wopm_ref, ws_in, ws_bias, ws_out, we_in, we_bias, we_out, zout,
               abuf, cbuf, oscr, uscr, usend, ubuf, zrow, bsend, bbuf, bscr, esend, ebuf, zsend, zfin):
    me, lo, group, outer_n = net.me, net.lo, net.group, net.outer_n
    blocks, opm = abuf.shape[0], abuf.shape[2]
    heads = ws_bias.shape[1]
    fold = ws_out.shape[0]
    size = z_ref.shape[0]
    keep = jnp.transpose(jnp.broadcast_to(mask_ref[...].astype(f32), (size, size))) != 0

    per = 128 // opm
    outer = None
    for q in range(blocks):
        term = mm(abuf[q].reshape(INNER * opm, -1), cbuf[q].reshape(outer_n * opm, -1), NT)
        outer = term if outer is None else outer + term
    for g in range(outer_n // per):
        oscr[g] = outer[:, g * 128:(g + 1) * 128]
    lane = lax.broadcasted_iota(jnp.int32, (opm // per * INNER, 128), 1) // opm
    tiles = []
    for g in range(outer_n // per):
        slabs = [jnp.concatenate([oscr[g, pl.ds(b * per + r, INNER, stride=opm), :] for b in range(opm // per)], axis=0)
                 for r in range(per)]
        turned = [[slabs[r] if s == 0 else pltpu.roll(slabs[r], s * opm, 1) for s in range(per)] for r in range(per)]
        for q in range(per):
            pick = turned[0][(0 - q) % per]
            for r in range(1, per):
                pick = jnp.where(lane == r, turned[r][(r - q) % per], pick)
            tiles.append(pick)
    up = None
    for b in range(opm // per):
        block = jnp.concatenate([t[b * INNER:(b + 1) * INNER] for t in tiles], axis=0).astype(bf16)
        term = mm(block, wopm_ref[b * 128:(b + 1) * 128, :])
        up = term if up is None else up + term
    uscr[...] = up
    for x in range(INNER):
        usend[x] = uscr[pl.ds(x, outer_n, stride=INNER), :]
    ubuf[lo] = usend[lo]
    net.to_inner(lambda x: (usend.at[x], ubuf.at[lo]), 3)
    net.settle(ubuf.at[pl.ds(0, INNER - 1)], 3)
    for x in range(INNER):
        zrow[pl.ds(x, outer_n, stride=INNER), :] = ubuf[x]
    z1 = (z_ref[...].astype(f32) + zrow[...] / (1e-3 + norm_ref[...])).astype(bf16)

    def bias_rows(z, weight):
        rows = dot_t(weight[...], norm_rows(z)).astype(bf16)
        return jnp.concatenate([rows, jnp.zeros((SLOT - heads, size), bf16)], axis=0)

    bsend[...] = bias_rows(z1, ws_bias)
    bbuf[me] = bsend[...]
    net.to_all(lambda t: (bsend, bbuf.at[me]), 4)
    parts = pair_project(z1, ws_in, fold)
    net.settle(bbuf.at[pl.ds(0, group - 1)], 4)
    bscr[...] = bbuf[...].astype(f32).reshape(group * SLOT, size)
    biases = [jnp.transpose(bscr[pl.ds(h, size, stride=SLOT), :]) for h in range(heads)]
    z2 = pair_attend(z1, parts, biases, keep, ws_out)

    end_rows = bias_rows(z2, we_bias).astype(f32)
    for h in range(heads):
        bscr[pl.ds(h, size, stride=SLOT), :] = jnp.broadcast_to(end_rows[h:h + 1], (size, size))
    bscr[pl.ds(heads, size, stride=SLOT), :] = z2.astype(f32)
    esend[...] = bscr[...].astype(bf16).reshape(group, SLOT, size)
    ebuf[me] = esend[me]
    net.to_all(lambda t: (esend.at[t], ebuf.at[me]), 5)
    net.settle(ebuf.at[pl.ds(0, group - 1)], 5)
    bscr[...] = ebuf[...].astype(f32).reshape(group * SLOT, size)
    zc = bscr[pl.ds(heads, size, stride=SLOT), :].astype(bf16)
    biases = [bscr[pl.ds(h, size, stride=SLOT), :] for h in range(heads)]
    z3 = pair_attend(zc, pair_project(zc, we_in, fold), biases, keep, we_out)

    zsend[...] = z3.astype(f32)
    zfin[pl.ds(me, 1), :] = zsend[pl.ds(me, 1), :]
    net.to_all(lambda t: (zsend.at[pl.ds(t, 1)], zfin.at[pl.ds(me, 1)]), 6)
    net.settle(zfin.at[pl.ds(0, group - 1)], 6)
    zout[...] = zfin[...].astype(bf16)


def tail_kernel(group, dap, x_ref, mrow_ref, wc_in, wc_out, wopm_in, z_ref, norm_ref, mask_ref, wopm_out,
                ws_in, ws_bias, ws_out, we_in, we_bias, we_out, mout, zout,
                kaug, qaug, vt, sig, gat, s0, s1, wt, wka, ycol, acs, abuf, cbuf,
                oscr, uscr, usend, ubuf, zrow, bsend, bbuf, bscr, esend, ebuf, zsend, zfin, send, recv):
    net = Links(group, dap, send, recv)
    me, lo, hi = net.me, net.lo, net.hi
    blocks, opm = abuf.shape[0], abuf.shape[2]
    bq = s0.shape[1]
    piece = mout.shape[1]
    per = bq // piece
    net.greet()

    def emit(qb, y, ac):
        ycol[pl.ds(pl.multiple_of(qb * bq, bq), bq), :] = y
        acs[qb] = ac
        abuf[qb, lo] = ac[:opm]
        cbuf[qb, hi] = ac[opm:]

        @pl.when(qb == 0)
        def _():
            net.ready()

        net.to_outer(lambda: (acs.at[qb, pl.ds(opm, opm)], cbuf.at[qb, hi]), 1)
        net.to_inner(lambda x: (acs.at[qb, pl.ds(0, opm)], abuf.at[qb, lo]), 0)

        def share_m(o, carry):
            t = qb * per + (me + o) % per

            @pl.when(t != me)
            def _():
                net.copy(ycol.at[pl.ds(pl.multiple_of(t * piece, piece), piece)], mout.at[me], 2, t).start()

            return carry

        lax.fori_loop(0, per, share_m, 0)

    col_stage(x_ref, mrow_ref, wc_in, wc_out, wopm_in, emit, kaug, qaug, vt, sig, gat, s0, s1, wt, wka)
    mout[me] = ycol[pl.ds(pl.multiple_of(me * piece, piece), piece), :]
    net.settle(cbuf.at[:, pl.ds(0, net.outer_n - 1)], 1)
    net.settle(abuf.at[:, pl.ds(0, INNER - 1)], 0)
    pair_stage(net, z_ref, norm_ref, mask_ref, wopm_out, ws_in, ws_bias, ws_out, we_in, we_bias, we_out, zout,
               abuf, cbuf, oscr, uscr, usend, ubuf, zrow, bsend, bbuf, bscr, esend, ebuf, zsend, zfin)
    net.settle(mout.at[pl.ds(0, group - 1)], 2)


def col_scratch(seq, width, heads, hd, bq):
    return [
        pltpu.VMEM((heads, seq, 128), bf16),
        pltpu.VMEM((heads, 128, seq), bf16),
        pltpu.VMEM((heads, hd, seq), bf16),
        pltpu.VMEM((heads, hd, seq), f32),
        pltpu.VMEM((heads * hd, bq), bf16),
        pltpu.VMEM((seq, bq), f32),
        pltpu.VMEM((seq, bq), f32),
        pltpu.VMEM((4 * heads * hd, width), bf16),
        pltpu.VMEM((width, heads * 128), bf16),
        pltpu.VMEM((seq, width), bf16),
    ]


def pair_scratch(seq, size, width, opm, group, bq):
    outer_n = group // INNER
    return [
        pltpu.VMEM((seq // bq, 2 * opm, bq), bf16),
        pltpu.VMEM((seq // bq, INNER, opm, bq), bf16),
        pltpu.VMEM((seq // bq, outer_n, opm, bq), bf16),
        pltpu.VMEM((outer_n * opm // 128, INNER * opm, 128), f32),
        pltpu.VMEM((size, width), f32),
        pltpu.VMEM((INNER, outer_n, width), f32),
        pltpu.VMEM((INNER, outer_n, width), f32),
        pltpu.VMEM((size, width), f32),
        pltpu.VMEM((SLOT, size), bf16),
        pltpu.VMEM((group, SLOT, size), bf16),
        pltpu.VMEM((group * SLOT, size), f32),
        pltpu.VMEM((group, SLOT, size), bf16),
        pltpu.VMEM((group, SLOT, size), bf16),
        pltpu.VMEM((size, width), f32),
        pltpu.VMEM((size, width), f32),
    ]


def tail_update(mcols, col_mask, col_weights, z, norm, mask, weights, heads, group, dap, bq=512):
    vm = pl.BlockSpec(memory_space=pltpu.VMEM)
    seq, m_width = mcols.shape
    wc_in, wc_out, wopm_in = col_weights
    opm = wopm_in.shape[1] // 2
    size, width = z.shape
    return pl.pallas_call(
        functools.partial(tail_kernel, group, dap),
        out_shape=(jax.ShapeDtypeStruct((group, seq // group, m_width), bf16), jax.ShapeDtypeStruct((size, width), bf16)),
        in_specs=[vm] * 15,
        out_specs=(vm, vm),
        scratch_shapes=col_scratch(seq, m_width, heads, wc_out.shape[0] // heads, bq)
        + pair_scratch(seq, size, width, opm, group, bq)
        + [pltpu.SemaphoreType.DMA((7,)), pltpu.SemaphoreType.DMA((7,))],
        compiler_params=pltpu.CompilerParams(collective_id=1, has_side_effects=True, vmem_limit_bytes=56 << 20),
        name='tail_update',
    )(mcols, col_mask[None, :], *col_weights, z, norm, mask, *weights)


def gather_slots(block, group, size):
    spread = jnp.broadcast_to(block[None], (size,) + block.shape)
    return lax.all_to_all(spread, group, 0, 0, tiled=True)


def head_bias(x_norm, weight):
    return jnp.einsum('jc,ch->hj', x_norm, weight, preferred_element_type=f32).astype(bf16)


def solution(mesh):
    dap_size = mesh.shape['dap']
    group = ('chip', 'dap')
    group_size = mesh.shape['chip'] * dap_size
    rows = P(('data', 'chip', 'dap'))
    in_specs = (rows, rows, P('data'), P('data')) + (P(),) * 13

    def per_device(m_blk, z_blk, msa_mask, res_mask, w_row_in, w_row_bias, w_row_out, w_col_in, w_col_out,
                   w_opm_in, w_opm_out, w_start_in, w_start_bias, w_start_out, w_end_in, w_end_bias, w_end_out):
        me = lax.axis_index('chip') * dap_size + lax.axis_index('dap')
        seqs, res, width = m_blk.shape
        total = seqs * group_size
        heads_m = w_row_bias.shape[1]
        res_row = res_mask[None, :]

        row_bias = gather_slots(head_bias(norm_rows(z_blk[0]), w_row_bias), group, group_size).astype(f32)
        seq_mask = lax.dynamic_slice_in_dim(msa_mask, me * seqs, seqs, axis=0)
        m_blk = attend(m_blk.reshape(seqs * res, width), row_bias, seq_mask, w_row_in, w_row_out, True, True, 'row_attention')

        m_cols = lax.all_to_all(m_blk.reshape(seqs, res, width), group, 1, 0, tiled=True)
        col_mask = lax.dynamic_slice_in_dim(msa_mask, me, 1, axis=1)[:, 0]
        weight = msa_mask.astype(bf16)
        pair_norm = jnp.einsum('s,sj->j', col_mask.astype(bf16), weight, preferred_element_type=f32)
        pair_norm = jnp.broadcast_to(pair_norm[:, None], (res, z_blk.shape[2]))
        weights = (w_opm_out, w_start_in, w_start_bias, w_start_out, w_end_in, w_end_bias, w_end_out)
        m_slots, z_out = tail_update(m_cols.reshape(total, width), col_mask, (w_col_in, w_col_out, w_opm_in), z_blk[0],
                                     pair_norm, res_row, weights, heads_m, group_size, dap_size)
        m_out, z_out = jnp.swapaxes(m_slots, 0, 1), z_out[None]
        return m_out, z_out

    return jax.shard_map(per_device, mesh=mesh, in_specs=in_specs, out_specs=(rows, rows), check_vma=False)
```

time: 201 us -> 169 us (0.84)
  Pallas kernels: 146 us -> 115 us
    pallas_call x2 -> x1, Pallas kernels: 130 us -> 99.6 us  [tail_update(): pl.pallas_call(functools.partial(tail_kernel, group, dap), out_shape=(jax...]
    unnamed x41 -> x27, local copies, waits for them, and re-layouts: 8 us -> 6.18 us
  transfers between devices with their start and end apart: 2 -> 2, of which waited for: 2 -> 2; matrix products, arithmetic and copies ran while one was open for 2% -> 3% of each run, Pallas kernels for 0% -> 0%
where the time goes in v4:
time: 169 us
  Pallas kernels  115 us (68%)
  waiting for transfers between devices  23.4 us (14%)
  starting transfers between devices  15.8 us (9%)
  local copies, waits for them, and re-layouts  11.3 us (7%)
  other arithmetic  1.81 us (1%)
    pallas_call x1, Pallas kernels, tail_update(): pl.pallas_call(functools.partial(tail_kernel, group, dap), out_shape=(jax...  99.6 us
    pallas_call x1, Pallas kernels, attend(): pl.pallas_call(functools.partial(attend_kernel, flip, per_row_mask), out_...  15.6 us
    all_to_all x1, waiting for transfers between devices, per_device(): lax.all_to_all(m_blk.reshape(seqs, res, width), group, 1, 0, tiled=True)  13.5 us
    all_to_all x1, starting transfers between devices, gather_slots(): return lax.all_to_all(spread, group, 0, 0, tiled=True)  11.5 us
    all_to_all x1, waiting for transfers between devices, gather_slots(): return lax.all_to_all(spread, group, 0, 0, tiled=True)  9.89 us
    unnamed x27, local copies, waits for them, and re-layouts  6.18 us
    all_to_all x1, starting transfers between devices, per_device(): lax.all_to_all(m_blk.reshape(seqs, res, width), group, 1, 0, tiled=True)  4.29 us
  transfers between devices with their start and end apart: 2, of which 2 were waited for; matrix products, arithmetic and copies ran while one was open for 3% of the time, Pallas kernels for 0%

profile of v4, /device:TPU:1, one launch (start us, length us, event | category | flops | bytes accessed | tf_op | source)
XLA Modules:
  0.0 168.7 jit_solution(6473183682243170165)
XLA Ops:
  0.6 0.0 copy-start
  0.7 0.9 convert_reduce_fusion
  1.6 0.2 fusion.5
  1.8 0.2 fusion
  2.1 0.7 broadcast_in_dim.8
  2.8 11.5 %all-to-all-start = ((bf16[128,8,128]{2,1,0:T(8,128)(2,1)}), bf16[128,8,128]{2,1,0:T(8,128)(2,1)S(1)}, u32[]{:S(2)}, u32[]{:S(2)}) async-start(bf16[128,8,128]{2,1,0:T(8,128)(2,1)} %broadcast_in_dim.8), calls=%async_computation | async-start | bytes 524288 | tf_op jit(solution)/shard_map/all_to_all | solution.py:510
  14.3 0.8 constant_dynamic-slice_fusion.mask_ref
  15.1 9.9 %all-to-all-done = bf16[128,8,128]{2,1,0:T(8,128)(2,1)S(1)} async-done(((bf16[128,8,128]{2,1,0:T(8,128)(2,1)}), bf16[128,8,128]{2,1,0:T(8,128)(2,1)S(1)}, u32[]{:S(2)}, u32[]{:S(2)}) %all-to-all-start) | async-done | bytes 262176 | tf_op jit(solution)/shard_map/all_to_all | solution.py:510
  25.1 15.6 %row_attention.1 = bf16[2048,256]{1,0:T(8,128)(2,1)S(1)} custom-call(bf16[2048,256]{1,0:T(8,128)(2,1)S(1)} %bitcast.28, f32[1024,128]{1,0:T(8,128)S(1)} %bitcast_convert_fusion.b_ref, s32[16,128]{1,0:T(8,128)S(1)} %constant_dynamic-slice_fusion.mask_ref, bf16[256,1024]{1,0:T(8,128)(2,1)S(1)} %copy-done.2, bf16[256,256]{1,0:T(8,128)(2,1)S(1)} %copy-done.3), custom_call_target="tpu_custom_call" | custom-call | tf_op jit(solution)/shard_map/row_attention/pallas_call | solution.py:121
  40.7 1.6 copy.24
  42.2 4.3 %all-to-all-start.1 = ((bf16[16,128,256]{2,0,1:T(8,128)(2,1)}), bf16[16,128,256]{2,0,1:T(8,128)(2,1)S(1)}, u32[]{:S(2)}, u32[]{:S(2)}) async-start(bf16[16,128,256]{2,0,1:T(8,128)(2,1)} %copy.24), calls=%async_computation.1 | async-start | bytes 2097152 | tf_op jit(solution)/shard_map/all_to_all | solution.py:536
  46.6 0.6 fusion.1
  47.2 0.7 copy-done.9
  47.9 0.7 copy.26.ws_bias
  48.6 0.7 copy.27.we_bias
  49.4 0.7 copy.25.wopm_in
  50.1 1.2 dynamic-slice_reduce_fusion
  51.3 0.2 convolution_bitcast_fusion
  51.5 13.5 %all-to-all-done.1 = bf16[16,128,256]{2,0,1:T(8,128)(2,1)S(1)} async-done(((bf16[16,128,256]{2,0,1:T(8,128)(2,1)}), bf16[16,128,256]{2,0,1:T(8,128)(2,1)S(1)}, u32[]{:S(2)}, u32[]{:S(2)}) %all-to-all-start.1) | async-done | bytes 1048608 | tf_op jit(solution)/shard_map/all_to_all | solution.py:536
  65.0 0.9 broadcast_in_dim.9.norm_ref
  65.8 0.1 copy-done.5
  65.9 99.6 %tail_update.1 = (bf16[128,16,256]{2,1,0:T(8,128)(2,1)}, bf16[128,128]{1,0:T(8,128)(2,1)}) custom-call(bf16[2048,256]{1,0:T(8,128)(2,1)} %bitcast.29, s32[1,2048]{1,0:T(1,128)} %bitcast.32, bf16[256,1024]{1,0:T(8,128)(2,1)} %wc_in.1, bf16[256,256]{1,0:T(8,128)(2,1)} %wc_out.1, bf16[256,64]{1,0:T(8,128)(2,1)} %copy.25.wopm_in, bf16[128,128]{1,0:T(8,128)(2,1)} %bitcast.31, ...), custom_call_target="tpu_custom_call" | custom-call | tf_op jit(solution)/shard_map/tail_update/pallas_call | solution.py:495
  165.5 2.5 %copy.28 = bf16[16,128,256]{2,1,0:T(8,128)(2,1)} copy(bf16[16,128,256]{2,0,1:T(8,128)(2,1)} %bitcast.30) | data formatting | bytes 2097152
  168.1 0.6 copy.30
  (23 shorter events, 0.1 us)
Async XLA Ops:
  0.6 1.2 copy-start
  0.6 1.0 copy-start.6
  0.7 24.4 %copy-start.1 = (bf16[16,128,256]{2,1,0:T(8,128)(2,1)S(1)}, bf16[16,128,256]{2,1,0:T(8,128)(2,1)}, u32[]{:S(2)}) copy-start(bf16[16,128,256]{2,1,0:T(8,128)(2,1)} %param.17) | copy-start | bytes 3145732
  2.8 22.2 %all-to-all-start = ((bf16[128,8,128]{2,1,0:T(8,128)(2,1)}), bf16[128,8,128]{2,1,0:T(8,128)(2,1)S(1)}, u32[]{:S(2)}, u32[]{:S(2)}) async-start(bf16[128,8,128]{2,1,0:T(8,128)(2,1)} %broadcast_in_dim.8), calls=%async_computation | async-start | bytes 524288 | tf_op jit(solution)/shard_map/all_to_all | solution.py:510
  14.3 10.7 %copy-start.2 = (bf16[256,1024]{1,0:T(8,128)(2,1)S(1)}, bf16[256,1024]{1,0:T(8,128)(2,1)}, u32[]{:S(2)}) copy-start(bf16[256,1024]{1,0:T(8,128)(2,1)} %win_ref.1) | copy-start | bytes 1572868
  15.1 10.0 %copy-start.3 = (bf16[256,256]{1,0:T(8,128)(2,1)S(1)}, bf16[256,256]{1,0:T(8,128)(2,1)}, u32[]{:S(2)}) copy-start(bf16[256,256]{1,0:T(8,128)(2,1)} %wout_ref.1) | copy-start | bytes 393220
  42.2 4.3 %copy-start.4 = (s32[2048,128]{1,0:T(8,128)S(1)}, s32[2048,128]{1,0:T(8,128)}, u32[]{:S(2)}) copy-start(s32[2048,128]{1,0:T(8,128)} %param.19) | copy-start | bytes 3145732
  42.2 22.7 %all-to-all-start.1 = ((bf16[16,128,256]{2,0,1:T(8,128)(2,1)}), bf16[16,128,256]{2,0,1:T(8,128)(2,1)S(1)}, u32[]{:S(2)}, u32[]{:S(2)}) async-start(bf16[16,128,256]{2,0,1:T(8,128)(2,1)} %copy.24), calls=%async_computation.1 | async-start | bytes 2097152 | tf_op jit(solution)/shard_map/all_to_all | solution.py:536
  47.2 0.7 copy-start.9
  47.9 0.7 copy-start.10
  47.9 1.5 copy-start.7
  65.0 1.0 copy-start.5
  165.5 2.5 %copy-start.8 = (bf16[128,128]{1,0:T(8,128)(2,1)S(1)}, bf16[128,128]{1,0:T(8,128)(2,1)}, u32[]{:S(2)}) copy-start(bf16[128,128]{1,0:T(8,128)(2,1)} %get-tuple-element.5) | copy-start | bytes 98308

commit v5 on v4

--- a/solution.py
+++ b/solution.py
@@ -40,103 +40,6 @@
 
 def mm(a, b, dims=(((1,), (0,)), ((), ()))):
     return lax.dot_general(a, b, dims, preferred_element_type=f32)
-
-
-def attend_kernel(flip, per_row_mask, x_ref, b_ref, mask_ref, win_ref, wout_ref, y_ref,
-                  kk, qt, vt, sig, gat, bias, wt, qd0, qd1):
-    tokens, width = x_ref.shape
-    size = bias.shape[0]
-    seqs = tokens // size
-    heads = bias.shape[1] // size
-    fold = gat.shape[0]
-    hd = fold // heads
-    c = hd ** -0.5 * LOG2E
-    bp = min(512, tokens)
-
-    wt[...] = jnp.transpose(win_ref[...])
-    qd0[...] = jnp.zeros_like(qd0)
-    qd1[...] = jnp.zeros_like(qd1)
-    for h in range(heads):
-        block = b_ref[pl.ds(h, size, stride=heads), :] * LOG2E
-        bias[:, h * size:(h + 1) * size] = jnp.transpose(block) if flip else block
-
-    def project(b, carry):
-        rows = pl.ds(pl.multiple_of(b * bp, bp), bp)
-        xn = norm_rows(x_ref[rows, :])
-        kk[rows, :] = mm(xn, win_ref[:, fold:2 * fold]).astype(bf16)
-        qt[:, rows] = mm(wt[:fold, :], xn, NT).astype(bf16)
-        vt[:, rows] = mm(wt[2 * fold:3 * fold, :], xn, NT).astype(bf16)
-        gg = mm(wt[3 * fold:, :], xn, NT).astype(bf16).astype(f32)
-        sig[:, rows] = 1.0 / (1.0 + jnp.exp(-gg))
-        return carry
-
-    if tokens == bp:
-        project(0, 0)
-    else:
-        lax.fori_loop(0, tokens // bp, project, 0)
-
-    def one(s, qd):
-        cols = pl.ds(pl.multiple_of(s * size, size), size)
-        for h in range(heads):
-            qd[h * hd:(h + 1) * hd, h * size:(h + 1) * size] = qt[h * hd:(h + 1) * hd, cols]
-        mrow = mask_ref[pl.ds(s if per_row_mask else 0, 1), :]
-        keep = jnp.transpose(jnp.broadcast_to(mrow.astype(f32), (size, size))) != 0
-        for h in range(0, heads, 2):
-            two = slice(h * size, (h + 2) * size)
-            t = mm(kk[cols, :], qd[:, two]) * c + bias[:, two]
-            t = jnp.where(jnp.concatenate([keep, keep], axis=1), t, NEG)
-            e = jnp.exp2(t - jnp.max(t, axis=0, keepdims=True))
-            total = jnp.sum(e, axis=0, keepdims=True)
-            mixed = mm(vt[h * hd:(h + 2) * hd, cols], e.astype(bf16)) / total
-            gat[h * hd:(h + 1) * hd, cols] = (mixed[:hd, :size] * sig[h * hd:(h + 1) * hd, cols]).astype(bf16)
-            gat[(h + 1) * hd:(h + 2) * hd, cols] = (mixed[hd:, size:] * sig[(h + 1) * hd:(h + 2) * hd, cols]).astype(bf16)
-
-    if seqs == 1:
-        one(0, qd0)
-    else:
-        def pair(u, carry):
-            one(2 * u, qd0)
-            one(2 * u + 1, qd1)
-            return carry
-        lax.fori_loop(0, seqs // 2, pair, 0)
-
-    def finish(b, carry):
-        rows = pl.ds(pl.multiple_of(b * bp, bp), bp)
-        up = mm(gat[:, rows], wout_ref[...], TN)
-        y_ref[rows, :] = (x_ref[rows, :].astype(f32) + up).astype(bf16)
-        return carry
-
-    if tokens == bp:
-        finish(0, 0)
-    else:
-        lax.fori_loop(0, tokens // bp, finish, 0)
-
-
-def attend(x, bias, mask, w_in, w_out, flip, per_row_mask, name):
-    tokens, width = x.shape
-    size = bias.shape[2]
-    heads = bias.shape[1]
-    fold = w_out.shape[0]
-    vm = pl.BlockSpec(memory_space=pltpu.VMEM)
-    return pl.pallas_call(
-        functools.partial(attend_kernel, flip, per_row_mask),
-        out_shape=jax.ShapeDtypeStruct((tokens, width), bf16),
-        in_specs=[vm] * 5,
-        out_specs=vm,
-        scratch_shapes=[
-            pltpu.VMEM((tokens, fold), bf16),
-            pltpu.VMEM((fold, tokens), bf16),
-            pltpu.VMEM((fold, tokens), bf16),
-            pltpu.VMEM((fold, tokens), f32),
-            pltpu.VMEM((fold, tokens), bf16),
-            pltpu.VMEM((size, heads * size), f32),
-            pltpu.VMEM(w_in.shape[::-1], bf16),
-            pltpu.VMEM((fold, heads * size), bf16),
-            pltpu.VMEM((fold, heads * size), bf16),
-        ],
-        compiler_params=pltpu.CompilerParams(vmem_limit_bytes=40 << 20),
-        name=name,
-    )(x, bias.reshape(size * heads, size), mask, w_in, w_out)
 
 
 NN = (((1,), (0,)), ((), ()))
@@ -175,9 +78,8 @@
     return (x.astype(f32) + up).astype(bf16)
 
 
-def col_stage(x_ref, mrow_ref, win_ref, wout_ref, wopm_ref, emit,
+def col_stage(load, seq, mrow_ref, win_ref, wout_ref, wopm_ref, emit,
               kaug, qaug, vt, sig, gat, s0, s1, wt, wka):
-    seq, width = x_ref.shape
     heads, hd = vt.shape[0], vt.shape[1]
     fold = heads * hd
     bq = s0.shape[1]
@@ -197,12 +99,11 @@
     for h in range(heads):
         wk = win_ref[:, fold + h * hd:fold + (h + 1) * hd]
         wka[:, h * 128:(h + 1) * 128] = jnp.concatenate([wk, wk, wk, jnp.zeros_like(wk)], axis=1)
-    wopm_t = jnp.transpose(wopm_ref[...])
 
     def project(b, carry):
         rows = pl.ds(pl.multiple_of(b * bq, bq), bq)
-        xn = norm_rows(x_ref[rows, :])
-        keep = jnp.transpose(jnp.broadcast_to(mrow_ref[:, rows], (128, bq)).astype(f32)) != 0
+        xn = norm_rows(load(b))
+        keep = jnp.transpose(jnp.broadcast_to(mrow_ref[0:1, rows], (128, bq))) != 0
         keep2 = jnp.concatenate([keep, keep], axis=1)
         for h in range(0, heads, 2):
             k = mm(xn, wka[:, h * 128:(h + 2) * 128])
@@ -267,9 +168,9 @@
 
         m = lax.fori_loop(0, heads // 2, pair, m)
         rows = pl.ds(pl.multiple_of(qb * bq, bq), bq)
-        y = (x_ref[rows, :].astype(f32) + mm(gat[...], wout_ref[...], TN)).astype(bf16)
-        ac = mm(wopm_t, norm_rows(y), NT).astype(bf16)
-        emit(qb, y, (ac.astype(f32) * mrow_ref[:, rows].astype(f32)).astype(bf16))
+        y = (load(qb).astype(f32) + mm(gat[...], wout_ref[...], TN)).astype(bf16)
+        ac = mm(wopm_ref[...], norm_rows(y), NT).astype(bf16)
+        emit(qb, y, (ac.astype(f32) * mrow_ref[0:1, rows]).astype(bf16))
         return m
 
     lax.fori_loop(0, nq, block, m)
@@ -330,11 +231,17 @@
         lax.fori_loop(1, self.outer_n, one, 0)
 
 
-def pair_stage(net, z_ref, norm_ref, mask_ref, wopm_ref, ws_in, ws_bias, ws_out, we_in, we_bias, we_out, zout,
+def bias_rows(z, weight):
+    rows = mm(weight[...], norm_rows(z), NT).astype(bf16)
+    spare = SLOT - rows.shape[0]
+    return jnp.concatenate([rows, jnp.zeros((spare, rows.shape[1]), bf16)], axis=0) if spare else rows
+
+
+def pair_stage(net, z_ref, norm, mask_ref, wopm_ref, ws_in, ws_bias, ws_out, we_in, we_bias, we_out, zout,
                abuf, cbuf, oscr, uscr, usend, ubuf, zrow, bsend, bbuf, bscr, esend, ebuf, zsend, zfin):
     me, lo, group, outer_n = net.me, net.lo, net.group, net.outer_n
     blocks, opm = abuf.shape[0], abuf.shape[2]
-    heads = ws_bias.shape[1]
+    heads = ws_bias.shape[0]
     fold = ws_out.shape[0]
     size = z_ref.shape[0]
     keep = jnp.transpose(jnp.broadcast_to(mask_ref[...].astype(f32), (size, size))) != 0
@@ -370,11 +277,7 @@
     net.settle(ubuf.at[pl.ds(0, INNER - 1)], 3)
     for x in range(INNER):
         zrow[pl.ds(x, outer_n, stride=INNER), :] = ubuf[x]
-    z1 = (z_ref[...].astype(f32) + zrow[...] / (1e-3 + norm_ref[...])).astype(bf16)
-
-    def bias_rows(z, weight):
-        rows = dot_t(weight[...], norm_rows(z)).astype(bf16)
-        return jnp.concatenate([rows, jnp.zeros((SLOT - heads, size), bf16)], axis=0)
+    z1 = (z_ref[...].astype(f32) + zrow[...] / (1e-3 + norm[...])).astype(bf16)
 
     bsend[...] = bias_rows(z1, ws_bias)
     bbuf[me] = bsend[...]
@@ -405,49 +308,173 @@
     zout[...] = zfin[...].astype(bf16)
 
 
-def tail_kernel(group, dap, x_ref, mrow_ref, wc_in, wc_out, wopm_in, z_ref, norm_ref, mask_ref, wopm_out,
-                ws_in, ws_bias, ws_out, we_in, we_bias, we_out, mout, zout,
-                kaug, qaug, vt, sig, gat, s0, s1, wt, wka, ycol, acs, abuf, cbuf,
-                oscr, uscr, usend, ubuf, zrow, bsend, bbuf, bscr, esend, ebuf, zsend, zfin, send, recv):
+def row_stage(net, x_ref, z_ref, mask_ref, wb_ref, win_ref, wout_ref, ship, side,
+              kk, qt, vt, sig, gat, bias, wt, qd0, qd1, bsend, bbuf, bscr, ytr):
+    tokens, width = x_ref.shape
+    size = bias.shape[0]
+    seqs = tokens // size
+    heads = bias.shape[1] // size
+    fold = gat.shape[0]
+    hd = fold // heads
+    c = hd ** -0.5 * LOG2E
+    bp = 512
+    me, group = net.me, net.group
+
+    net.greet()
+    bsend[...] = bias_rows(z_ref[...], wb_ref)
+    bbuf[me] = bsend[...]
+    wt[...] = jnp.transpose(win_ref[...])
+    qd0[...] = jnp.zeros_like(qd0)
+    qd1[...] = jnp.zeros_like(qd1)
+
+    def project(b, carry):
+        rows = pl.ds(pl.multiple_of(b * bp, bp), bp)
+        xn = norm_rows(x_ref[rows, :])
+        kk[rows, :] = mm(xn, win_ref[:, fold:2 * fold]).astype(bf16)
+        qt[:, rows] = mm(wt[:fold, :], xn, NT).astype(bf16)
+        vt[:, rows] = mm(wt[2 * fold:3 * fold, :], xn, NT).astype(bf16)
+        gg = mm(wt[3 * fold:, :], xn, NT).astype(bf16).astype(f32)
+        sig[:, rows] = 1.0 / (1.0 + jnp.exp(-gg))
+
+        @pl.when(b == 1)
+        def _():
+            net.ready()
+            net.to_all(lambda t: (bsend, bbuf.at[me]), 7)
+
+        return carry
+
+    lax.fori_loop(0, tokens // bp, project, 0)
+    side()
+    net.settle(bbuf.at[pl.ds(0, group - 1)], 7)
+    bscr[...] = bbuf[...].astype(f32).reshape(group * SLOT, size)
+    for h in range(heads):
+        bias[:, h * size:(h + 1) * size] = jnp.transpose(bscr[pl.ds(h, size, stride=SLOT), :] * LOG2E)
+
+    def one(s, qd):
+        cols = pl.ds(pl.multiple_of(s * size, size), size)
+        for h in range(heads):
+            qd[h * hd:(h + 1) * hd, h * size:(h + 1) * size] = qt[h * hd:(h + 1) * hd, cols]
+        mrow = mask_ref[pl.ds(me * seqs + s, 1), :]
+        keep = jnp.transpose(jnp.broadcast_to(mrow.astype(f32), (size, size))) != 0
+        keep2 = jnp.concatenate([keep, keep], axis=1)
+        for h in range(0, heads, 2):
+            two = slice(h * size, (h + 2) * size)
+            t = mm(kk[cols, :], qd[:, two]) * c + bias[:, two]
+            t = jnp.where(keep2, t, NEG)
+            e = jnp.exp2(t - jnp.max(t, axis=0, keepdims=True))
+            total = jnp.sum(e, axis=0, keepdims=True)
+            mixed = mm(vt[h * hd:(h + 2) * hd, cols], e.astype(bf16)) / total
+            gat[h * hd:(h + 1) * hd, cols] = (mixed[:hd, :size] * sig[h * hd:(h + 1) * hd, cols]).astype(bf16)
+            gat[(h + 1) * hd:(h + 2) * hd, cols] = (mixed[hd:, size:] * sig[(h + 1) * hd:(h + 2) * hd, cols]).astype(bf16)
+
+    def chunk(k, carry):
+        def pair(u, carry):
+            one(k * SLOT + 2 * u, qd0)
+            one(k * SLOT + 2 * u + 1, qd1)
+            return carry
+
+        lax.fori_loop(0, SLOT // 2, pair, 0)
+        for b in range(SLOT * size // bp):
+            rows = pl.ds(pl.multiple_of((k * SLOT * size // bp + b) * bp, bp), bp)
+            y = (x_ref[rows, :].astype(f32) + mm(gat[:, rows], wout_ref[...], TN)).astype(bf16).astype(f32)
+            for i in range(bp // size):
+                for half in range(width // 128):
+                    ytr[half, pl.ds(b * (bp // size) + i, size, stride=SLOT), :] = (
+                        y[i * size:(i + 1) * size, half * 128:(half + 1) * 128])
+        ship(k, jnp.concatenate([ytr[half] for half in range(width // 128)], axis=1).astype(bf16))
+        return carry
+
+    lax.fori_loop(0, seqs // SLOT, chunk, 0)
+
+
+def block_kernel(group, dap, m_ref, z_ref, mask_ref, res_ref, wr_in, wr_bias, wr_out, wc_in, wc_out, wopm_in, wopm_out,
+                 ws_in, ws_bias, ws_out, we_in, we_bias, we_out, mout, zout,
+                 kk, qt, rvt, rsig, rgat, bias, rwt, qd0, qd1, rsend, rbuf, rscr, ytr, msend, xbuf, mrow, norm,
+                 kaug, qaug, vt, sig, gat, s0, s1, wt, wka, ycol, acs, abuf, cbuf,
+                 oscr, uscr, usend, ubuf, zrow, bsend, bbuf, bscr, esend, ebuf, zsend, zfin, send, recv):
     net = Links(group, dap, send, recv)
     me, lo, hi = net.me, net.lo, net.hi
-    blocks, opm = abuf.shape[0], abuf.shape[2]
+    opm = abuf.shape[2]
+    seq, size = mask_ref.shape
+    chunks = xbuf.shape[0]
     bq = s0.shape[1]
-    piece = mout.shape[1]
-    per = bq // piece
-    net.greet()
+    per = bq // SLOT
+    turns = group // per
+
+    def side():
+        flags = mask_ref[...].astype(bf16)
+        pick = (lax.broadcasted_iota(jnp.int32, (size, size), 0) == me).astype(bf16)
+        norm[...] = mm(flags, mm(flags, pick).astype(bf16), TN)
+        row = (lax.broadcasted_iota(jnp.int32, (SLOT, size), 1) == me).astype(bf16)
+        split = mask_ref[...].reshape(group, chunks, SLOT, size)
+        for k in range(chunks):
+            mrow[:, k * group * SLOT:(k + 1) * group * SLOT] = mm(
+                row, split[:, k].astype(f32).reshape(group * SLOT, size).astype(bf16), NT)
+
+    def ship(k, y):
+        msend[k] = y.astype(f32).reshape(group, SLOT, -1).astype(bf16)
+        xbuf[k, me] = msend[k, me]
+        net.to_all(lambda t: (msend.at[k, t], xbuf.at[k, me]), 8)
+
+    row_stage(net, m_ref, z_ref, mask_ref, wr_bias, wr_in, wr_out, ship, side,
+              kk, qt, rvt, rsig, rgat, bias, rwt, qd0, qd1, rsend, rbuf, rscr, ytr)
+    net.settle(xbuf.at[:, pl.ds(0, group - 1)], 8)
+
+    def load(b):
+        part = xbuf[b // turns, pl.ds(pl.multiple_of(b % turns * per, per), per)]
+        return part.astype(f32).reshape(bq, -1)
 
     def emit(qb, y, ac):
-        ycol[pl.ds(pl.multiple_of(qb * bq, bq), bq), :] = y
+        ycol[qb] = y.astype(f32).reshape(per, SLOT, -1).astype(bf16)
         acs[qb] = ac
         abuf[qb, lo] = ac[:opm]
         cbuf[qb, hi] = ac[opm:]
-
-        @pl.when(qb == 0)
-        def _():
-            net.ready()
-
         net.to_outer(lambda: (acs.at[qb, pl.ds(opm, opm)], cbuf.at[qb, hi]), 1)
         net.to_inner(lambda x: (acs.at[qb, pl.ds(0, opm)], abuf.at[qb, lo]), 0)
 
         def share_m(o, carry):
-            t = qb * per + (me + o) % per
+            i = (me + o) % per
+            t = qb % turns * per + i
 
             @pl.when(t != me)
             def _():
-                net.copy(ycol.at[pl.ds(pl.multiple_of(t * piece, piece), piece)], mout.at[me], 2, t).start()
+                net.copy(ycol.at[qb, i], mout.at[qb // turns, me], 2, t).start()
 
             return carry
 
         lax.fori_loop(0, per, share_m, 0)
 
-    col_stage(x_ref, mrow_ref, wc_in, wc_out, wopm_in, emit, kaug, qaug, vt, sig, gat, s0, s1, wt, wka)
-    mout[me] = ycol[pl.ds(pl.multiple_of(me * piece, piece), piece), :]
+    col_stage(load, seq, mrow, wc_in, wc_out, wopm_in, emit, kaug, qaug, vt, sig, gat, s0, s1, wt, wka)
+    for k in range(chunks):
+        mout[k, me] = ycol[k * turns + me // per, me % per]
     net.settle(cbuf.at[:, pl.ds(0, net.outer_n - 1)], 1)
     net.settle(abuf.at[:, pl.ds(0, INNER - 1)], 0)
-    pair_stage(net, z_ref, norm_ref, mask_ref, wopm_out, ws_in, ws_bias, ws_out, we_in, we_bias, we_out, zout,
+    pair_stage(net, z_ref, norm, res_ref, wopm_out, ws_in, ws_bias, ws_out, we_in, we_bias, we_out, zout,
                abuf, cbuf, oscr, uscr, usend, ubuf, zrow, bsend, bbuf, bscr, esend, ebuf, zsend, zfin)
-    net.settle(mout.at[pl.ds(0, group - 1)], 2)
+    net.settle(mout.at[:, pl.ds(0, group - 1)], 2)
+
+
+def row_scratch(tokens, size, width, heads, fold, group):
+    seqs = tokens // size
+    return [
+        pltpu.VMEM((tokens, fold), bf16),
+        pltpu.VMEM((fold, tokens), bf16),
+        pltpu.VMEM((fold, tokens), bf16),
+        pltpu.VMEM((fold, tokens), f32),
+        pltpu.VMEM((fold, tokens), bf16),
+        pltpu.VMEM((size, heads * size), f32),
+        pltpu.VMEM((4 * fold, width), bf16),
+        pltpu.VMEM((fold, heads * size), bf16),
+        pltpu.VMEM((fold, heads * size), bf16),
+        pltpu.VMEM((SLOT, size), bf16),
+        pltpu.VMEM((group, SLOT, size), bf16),
+        pltpu.VMEM((group * SLOT, size), f32),
+        pltpu.VMEM((width // 128, SLOT * size, 128), f32),
+        pltpu.VMEM((seqs // SLOT, group, SLOT, width), bf16),
+        pltpu.VMEM((seqs // SLOT, group, SLOT, width), bf16),
+        pltpu.VMEM((SLOT, seqs * group), f32),
+        pltpu.VMEM((size, size), f32),
+    ]
 
 
 def col_scratch(seq, width, heads, hd, bq):
@@ -461,7 +488,7 @@
         pltpu.VMEM((seq, bq), f32),
         pltpu.VMEM((4 * heads * hd, width), bf16),
         pltpu.VMEM((width, heads * 128), bf16),
-        pltpu.VMEM((seq, width), bf16),
+        pltpu.VMEM((seq // bq, bq // SLOT, SLOT, width), bf16),
     ]
 
 
@@ -486,62 +513,42 @@
     ]
 
 
-def tail_update(mcols, col_mask, col_weights, z, norm, mask, weights, heads, group, dap, bq=512):
+def block_update(m, z, msa_mask, res_mask, weights, heads, group, dap, bq=512):
     vm = pl.BlockSpec(memory_space=pltpu.VMEM)
-    seq, m_width = mcols.shape
-    wc_in, wc_out, wopm_in = col_weights
-    opm = wopm_in.shape[1] // 2
+    tokens, m_width = m.shape
     size, width = z.shape
+    seqs = tokens // size
+    seq = seqs * group
+    fold = weights[2].shape[0]
+    opm = weights[5].shape[0] // 2
     return pl.pallas_call(
-        functools.partial(tail_kernel, group, dap),
-        out_shape=(jax.ShapeDtypeStruct((group, seq // group, m_width), bf16), jax.ShapeDtypeStruct((size, width), bf16)),
-        in_specs=[vm] * 15,
+        functools.partial(block_kernel, group, dap),
+        out_shape=(jax.ShapeDtypeStruct((seqs // SLOT, group, SLOT, m_width), bf16), jax.ShapeDtypeStruct((size, width), bf16)),
+        in_specs=[vm] * (4 + len(weights)),
         out_specs=(vm, vm),
-        scratch_shapes=col_scratch(seq, m_width, heads, wc_out.shape[0] // heads, bq)
+        scratch_shapes=row_scratch(tokens, size, m_width, heads, fold, group)
+        + col_scratch(seq, m_width, heads, fold // heads, bq)
         + pair_scratch(seq, size, width, opm, group, bq)
-        + [pltpu.SemaphoreType.DMA((7,)), pltpu.SemaphoreType.DMA((7,))],
-        compiler_params=pltpu.CompilerParams(collective_id=1, has_side_effects=True, vmem_limit_bytes=56 << 20),
-        name='tail_update',
-    )(mcols, col_mask[None, :], *col_weights, z, norm, mask, *weights)
-
-
-def gather_slots(block, group, size):
-    spread = jnp.broadcast_to(block[None], (size,) + block.shape)
-    return lax.all_to_all(spread, group, 0, 0, tiled=True)
-
-
-def head_bias(x_norm, weight):
-    return jnp.einsum('jc,ch->hj', x_norm, weight, preferred_element_type=f32).astype(bf16)
+        + [pltpu.SemaphoreType.DMA((9,)), pltpu.SemaphoreType.DMA((9,))],
+        compiler_params=pltpu.CompilerParams(collective_id=1, has_side_effects=True, vmem_limit_bytes=63 << 20),
+        name='block_update',
+    )(m, z, msa_mask, res_mask, *weights)
 
 
 def solution(mesh):
     dap_size = mesh.shape['dap']
-    group = ('chip', 'dap')
     group_size = mesh.shape['chip'] * dap_size
     rows = P(('data', 'chip', 'dap'))
     in_specs = (rows, rows, P('data'), P('data')) + (P(),) * 13
 
     def per_device(m_blk, z_blk, msa_mask, res_mask, w_row_in, w_row_bias, w_row_out, w_col_in, w_col_out,
                    w_opm_in, w_opm_out, w_start_in, w_start_bias, w_start_out, w_end_in, w_end_bias, w_end_out):
-        me = lax.axis_index('chip') * dap_size + lax.axis_index('dap')
         seqs, res, width = m_blk.shape
-        total = seqs * group_size
-        heads_m = w_row_bias.shape[1]
-        res_row = res_mask[None, :]
-
-        row_bias = gather_slots(head_bias(norm_rows(z_blk[0]), w_row_bias), group, group_size).astype(f32)
-        seq_mask = lax.dynamic_slice_in_dim(msa_mask, me * seqs, seqs, axis=0)
-        m_blk = attend(m_blk.reshape(seqs * res, width), row_bias, seq_mask, w_row_in, w_row_out, True, True, 'row_attention')
-
-        m_cols = lax.all_to_all(m_blk.reshape(seqs, res, width), group, 1, 0, tiled=True)
-        col_mask = lax.dynamic_slice_in_dim(msa_mask, me, 1, axis=1)[:, 0]
-        weight = msa_mask.astype(bf16)
-        pair_norm = jnp.einsum('s,sj->j', col_mask.astype(bf16), weight, preferred_element_type=f32)
-        pair_norm = jnp.broadcast_to(pair_norm[:, None], (res, z_blk.shape[2]))
-        weights = (w_opm_out, w_start_in, w_start_bias, w_start_out, w_end_in, w_end_bias, w_end_out)
-        m_slots, z_out = tail_update(m_cols.reshape(total, width), col_mask, (w_col_in, w_col_out, w_opm_in), z_blk[0],
-                                     pair_norm, res_row, weights, heads_m, group_size, dap_size)
-        m_out, z_out = jnp.swapaxes(m_slots, 0, 1), z_out[None]
-        return m_out, z_out
+        weights = (w_row_in, w_row_bias.T, w_row_out, w_col_in, w_col_out, w_opm_in.T, w_opm_out,
+                   w_start_in, w_start_bias.T, w_start_out, w_end_in, w_end_bias.T, w_end_out)
+        slots, z_out = block_update(m_blk.reshape(seqs * res, width), z_blk[0], msa_mask, res_mask[None, :], weights,
+                                    w_row_bias.shape[1], group_size, dap_size)
+        m_out = jnp.swapaxes(slots, 1, 2).reshape(seqs, res, width)
+        return m_out, z_out[None]
 
     return jax.shard_map(per_device, mesh=mesh, in_specs=in_specs, out_specs=(rows, rows), check_vma=False)

time: 169 us -> 144 us (0.85)
  Pallas kernels: 115 us -> 140 us
  waiting for transfers between devices: 23.4 us -> 0 us
  starting transfers between devices: 15.8 us -> 0 us
  local copies, waits for them, and re-layouts: 11.3 us -> 3.05 us
  other arithmetic: 1.81 us -> 0 us
    pallas_call x2 -> x1, Pallas kernels: 115 us -> 140 us  [block_update(): pl.pallas_call(functools.partial(block_kernel, group, dap), out_shape=(ja...]
    all_to_all x2 -> x0, waiting for transfers between devices: 23.4 us -> none  [the longest x1 13.5 us: per_device(): lax.all_to_all(m_blk.reshape(seqs, res, width), group, 1, 0, tiled=True)]
    all_to_all x2 -> x0, starting transfers between devices: 15.8 us -> none  [the longest x1 11.5 us: gather_slots(): return lax.all_to_all(spread, group, 0, 0, tiled=True)]
    unnamed x27 -> x3, local copies, waits for them, and re-layouts: 6.18 us -> 0.62 us
    transpose x0 -> x1, local copies, waits for them, and re-layouts: none -> 2.43 us  [per_device(): m_out = jnp.swapaxes(slots, 1, 2).reshape(seqs, res, width)]
    dynamic_slice x2 -> x0, local copies, waits for them, and re-layouts: 1.99 us -> none  [the longest x1 1.23 us: per_device(): col_mask = lax.dynamic_slice_in_dim(msa_mask, me, 1, axis=1)[:, 0]]
  transfers between devices with their start and end apart: 2 -> 0, of which waited for: 2 -> 0; matrix products, arithmetic and copies ran while one was open for 3% -> 0% of each run, Pallas kernels for 0% -> 0%
where the time goes in v5:
time: 144 us
  Pallas kernels  140 us (97%)
  local copies, waits for them, and re-layouts  3.05 us (2%)
    pallas_call x1, Pallas kernels, block_update(): pl.pallas_call(functools.partial(block_kernel, group, dap), out_shape=(ja...  140 us

profile of v5, /device:TPU:1, one launch (start us, length us, event | category | flops | bytes accessed | tf_op | source)
XLA Modules:
  0.0 143.8 jit_solution(49577252984185227)
XLA Ops:
  0.6 140.1 %block_update.1 = (bf16[2,128,8,256]{3,2,1,0:T(8,128)(2,1)}, bf16[128,128]{1,0:T(8,128)(2,1)}) custom-call(bf16[2048,256]{1,0:T(8,128)(2,1)} %bitcast.10, bf16[128,128]{1,0:T(8,128)(2,1)} %bitcast.13, s32[2048,128]{1,0:T(8,128)} %mask_ref.1, s32[1,128]{1,0:T(1,128)} %bitcast.19, bf16[256,1024]{1,0:T(8,128)(2,1)} %wr_in.1, bf16[8,128]{1,0:T(8,128)(2,1)} %bitcast.16, ...), custom_call_target="tpu_custom_call" | custom-call | tf_op jit(solution)/shard_map/block_update/pallas_call | solution.py:524
  140.8 0.0 copy-start
  140.8 2.4 %copy.19 = bf16[2,8,128,256]{3,2,1,0:T(8,128)(2,1)} copy(bf16[2,8,128,256]{3,1,2,0:T(8,128)(2,1)} %bitcast.12) | data formatting | bytes 2097152 | tf_op jit(solution)/shard_map/transpose | solution.py:551
  143.2 0.0 copy-done
  143.2 0.6 copy.21
Async XLA Ops:
  140.8 2.4 %copy-start = (bf16[128,128]{1,0:T(8,128)(2,1)S(1)}, bf16[128,128]{1,0:T(8,128)(2,1)}, u32[]{:S(2)}) copy-start(bf16[128,128]{1,0:T(8,128)(2,1)} %get-tuple-element.5) | copy-start | bytes 98308

commit v6 on v5

--- a/solution.py
+++ b/solution.py
@@ -49,7 +49,7 @@
 
 
 def place(t, dap):
-    return (0, t // dap, t % dap)
+    return (0, lax.div(t, dap), lax.rem(t, dap))
 
 
 def pair_project(x, win_ref, fold):
@@ -78,7 +78,7 @@
     return (x.astype(f32) + up).astype(bf16)
 
 
-def col_stage(load, seq, mrow_ref, win_ref, wout_ref, wopm_ref, emit,
+def col_stage(arrive, load, seq, mrow_ref, win_ref, wout_ref, wopm_ref, emit,
               kaug, qaug, vt, sig, gat, s0, s1, wt, wka):
     heads, hd = vt.shape[0], vt.shape[1]
     fold = heads * hd
@@ -102,6 +102,7 @@
 
     def project(b, carry):
         rows = pl.ds(pl.multiple_of(b * bq, bq), bq)
+        arrive(b)
         xn = norm_rows(load(b))
         keep = jnp.transpose(jnp.broadcast_to(mrow_ref[0:1, rows], (128, bq))) != 0
         keep2 = jnp.concatenate([keep, keep], axis=1)
@@ -176,21 +177,34 @@
     lax.fori_loop(0, nq, block, m)
 
 
+def each(start, stop, one, step=8):
+    whole = (stop - start) // step
+
+    def some(i, carry):
+        for j in range(step):
+            one(start + i * step + j)
+        return carry
+
+    lax.fori_loop(0, whole, some, 0)
+    for o in range(start + whole * step, stop):
+        one(o)
+
+
 class Links:
     def __init__(self, group, dap, send, recv):
         self.group, self.dap, self.send, self.recv = group, dap, send, recv
         self.me = lax.axis_index('chip') * dap + lax.axis_index('dap')
-        self.hi, self.lo = self.me // INNER, self.me % INNER
+        self.hi, self.lo = lax.div(self.me, INNER), lax.rem(self.me, INNER)
         self.outer_n = group // INNER
 
     def greet(self):
         barrier = pltpu.get_barrier_semaphore()
 
-        def one(o, carry):
-            pl.semaphore_signal(barrier, inc=1, device_id=place((self.me + o) % self.group, self.dap), device_id_type=MESH)
-            return carry
-
-        lax.fori_loop(1, self.group, one, 0)
+        def one(o):
+            t = lax.rem(self.me + o, self.group)
+            pl.semaphore_signal(barrier, inc=1, device_id=place(t, self.dap), device_id_type=MESH)
+
+        each(1, self.group, one)
 
     def ready(self):
         pl.semaphore_wait(pltpu.get_barrier_semaphore(), self.group - 1)
@@ -205,30 +219,28 @@
         done.wait_recv()
 
     def to_all(self, make, i):
-        def one(o, carry):
-            t = (self.me + o) % self.group
+        def one(o):
+            t = lax.rem(self.me + o, self.group)
             src, dst = make(t)
             self.copy(src, dst, i, t).start()
-            return carry
-
-        lax.fori_loop(1, self.group, one, 0)
+
+        each(1, self.group, one)
 
     def to_inner(self, make, i):
-        def one(o, carry):
-            x = (self.lo + o) % INNER
+        for o in range(1, INNER):
+            x = lax.rem(self.lo + o, INNER)
             src, dst = make(x)
             self.copy(src, dst, i, self.hi * INNER + x).start()
-            return carry
-
-        lax.fori_loop(1, INNER, one, 0)
-
-    def to_outer(self, make, i):
-        def one(o, carry):
-            src, dst = make()
-            self.copy(src, dst, i, (self.hi + o) % self.outer_n * INNER + self.lo).start()
-            return carry
-
-        lax.fori_loop(1, self.outer_n, one, 0)
+
+    def to_half(self, src, dst, i):
+        half = self.outer_n // 2
+        base = lax.div(self.hi, half) * half
+        for o in range(1, half):
+            y = base + lax.rem(lax.rem(self.hi, half) + o, half)
+            self.copy(src, dst, i, y * INNER + self.lo).start()
+
+    def to_partner(self, part, i):
+        self.copy(part, part, i, lax.rem(self.me + self.group // 2, self.group)).start()
 
 
 def bias_rows(z, weight):
@@ -336,7 +348,7 @@
         gg = mm(wt[3 * fold:, :], xn, NT).astype(bf16).astype(f32)
         sig[:, rows] = 1.0 / (1.0 + jnp.exp(-gg))
 
-        @pl.when(b == 1)
+        @pl.when(b == 0)
         def _():
             net.ready()
             net.to_all(lambda t: (bsend, bbuf.at[me]), 7)
@@ -414,40 +426,54 @@
     def ship(k, y):
         msend[k] = y.astype(f32).reshape(group, SLOT, -1).astype(bf16)
         xbuf[k, me] = msend[k, me]
-        net.to_all(lambda t: (msend.at[k, t], xbuf.at[k, me]), 8)
+        net.to_all(lambda t: (msend.at[k, t], xbuf.at[k, me]), 8 + k)
 
     row_stage(net, m_ref, z_ref, mask_ref, wr_bias, wr_in, wr_out, ship, side,
               kk, qt, rvt, rsig, rgat, bias, rwt, qd0, qd1, rsend, rbuf, rscr, ytr)
-    net.settle(xbuf.at[:, pl.ds(0, group - 1)], 8)
+
+    def arrive(b):
+        @pl.when(lax.rem(b, turns) == 0)
+        def _():
+            k = lax.div(b, turns)
+            net.settle(xbuf.at[k, pl.ds(0, group - 1)], 8 + k)
 
     def load(b):
         part = xbuf[b // turns, pl.ds(pl.multiple_of(b % turns * per, per), per)]
         return part.astype(f32).reshape(bq, -1)
+
+    half = pl.ds(pl.multiple_of(lax.div(hi, net.outer_n // 2) * (net.outer_n // 2), net.outer_n // 2), net.outer_n // 2)
+
+    def pass_on(qb):
+        net.settle(cbuf.at[qb, pl.ds(0, net.outer_n // 2 - 1)], 10 + qb)
+        net.to_partner(cbuf.at[qb, half], 1)
 
     def emit(qb, y, ac):
         ycol[qb] = y.astype(f32).reshape(per, SLOT, -1).astype(bf16)
         acs[qb] = ac
         abuf[qb, lo] = ac[:opm]
         cbuf[qb, hi] = ac[opm:]
-        net.to_outer(lambda: (acs.at[qb, pl.ds(opm, opm)], cbuf.at[qb, hi]), 1)
+        net.to_half(acs.at[qb, pl.ds(opm, opm)], cbuf.at[qb, hi], 10 + qb)
         net.to_inner(lambda x: (acs.at[qb, pl.ds(0, opm)], abuf.at[qb, lo]), 0)
 
-        def share_m(o, carry):
-            i = (me + o) % per
-            t = qb % turns * per + i
+        @pl.when(qb > 0)
+        def _():
+            pass_on(qb - 1)
+
+        def share_m(o):
+            i = lax.rem(me + o, per)
+            t = lax.rem(qb, turns) * per + i
 
             @pl.when(t != me)
             def _():
-                net.copy(ycol.at[qb, i], mout.at[qb // turns, me], 2, t).start()
-
-            return carry
-
-        lax.fori_loop(0, per, share_m, 0)
-
-    col_stage(load, seq, mrow, wc_in, wc_out, wopm_in, emit, kaug, qaug, vt, sig, gat, s0, s1, wt, wka)
+                net.copy(ycol.at[qb, i], mout.at[lax.div(qb, turns), me], 2, t).start()
+
+        each(0, per, share_m)
+
+    col_stage(arrive, load, seq, mrow, wc_in, wc_out, wopm_in, emit, kaug, qaug, vt, sig, gat, s0, s1, wt, wka)
     for k in range(chunks):
-        mout[k, me] = ycol[k * turns + me // per, me % per]
-    net.settle(cbuf.at[:, pl.ds(0, net.outer_n - 1)], 1)
+        mout[k, me] = ycol[k * turns + lax.div(me, per), lax.rem(me, per)]
+    pass_on(cbuf.shape[0] - 1)
+    net.settle(cbuf.at[:, pl.ds(0, net.outer_n // 2)], 1)
     net.settle(abuf.at[:, pl.ds(0, INNER - 1)], 0)
     pair_stage(net, z_ref, norm, res_ref, wopm_out, ws_in, ws_bias, ws_out, we_in, we_bias, we_out, zout,
                abuf, cbuf, oscr, uscr, usend, ubuf, zrow, bsend, bbuf, bscr, esend, ebuf, zsend, zfin)
@@ -529,7 +555,7 @@
         scratch_shapes=row_scratch(tokens, size, m_width, heads, fold, group)
         + col_scratch(seq, m_width, heads, fold // heads, bq)
         + pair_scratch(seq, size, width, opm, group, bq)
-        + [pltpu.SemaphoreType.DMA((9,)), pltpu.SemaphoreType.DMA((9,))],
+        + [pltpu.SemaphoreType.DMA((14,)), pltpu.SemaphoreType.DMA((14,))],
         compiler_params=pltpu.CompilerParams(collective_id=1, has_side_effects=True, vmem_limit_bytes=63 << 20),
         name='block_update',
     )(m, z, msa_mask, res_mask, *weights)

time: 144 us -> 130 us (0.903)
  Pallas kernels: 140 us -> 126 us
    pallas_call x1, Pallas kernels: 140 us -> 126 us  [block_update(): pl.pallas_call(functools.partial(block_kernel, group, dap), out_shape=(ja...]
where the time goes in v6:
time: 130 us
  Pallas kernels  126 us (97%)
  local copies, waits for them, and re-layouts  3.05 us (2%)
    pallas_call x1, Pallas kernels, block_update(): pl.pallas_call(functools.partial(block_kernel, group, dap), out_shape=(ja...  126 us

profile of v6, /device:TPU:1, one launch (start us, length us, event | category | flops | bytes accessed | tf_op | source)
XLA Modules:
  0.0 130.2 jit_solution(14331442240472362931)
XLA Ops:
  0.6 126.5 %block_update.1 = (bf16[2,128,8,256]{3,2,1,0:T(8,128)(2,1)}, bf16[128,128]{1,0:T(8,128)(2,1)}) custom-call(bf16[2048,256]{1,0:T(8,128)(2,1)} %bitcast.10, bf16[128,128]{1,0:T(8,128)(2,1)} %bitcast.13, s32[2048,128]{1,0:T(8,128)} %mask_ref.1, s32[1,128]{1,0:T(1,128)} %bitcast.19, bf16[256,1024]{1,0:T(8,128)(2,1)} %wr_in.1, bf16[8,128]{1,0:T(8,128)(2,1)} %bitcast.16, ...), custom_call_target="tpu_custom_call" | custom-call | tf_op jit(solution)/shard_map/block_update/pallas_call | solution.py:550
  127.1 0.0 copy-start
  127.2 2.4 %copy.19 = bf16[2,8,128,256]{3,2,1,0:T(8,128)(2,1)} copy(bf16[2,8,128,256]{3,1,2,0:T(8,128)(2,1)} %bitcast.12) | data formatting | bytes 2097152 | tf_op jit(solution)/shard_map/transpose | solution.py:577
  129.6 0.0 copy-done
  129.6 0.6 copy.21
Async XLA Ops:
  127.1 2.4 %copy-start = (bf16[128,128]{1,0:T(8,128)(2,1)S(1)}, bf16[128,128]{1,0:T(8,128)(2,1)}, u32[]{:S(2)}) copy-start(bf16[128,128]{1,0:T(8,128)(2,1)} %get-tuple-element.5) | copy-start | bytes 98308

commit v7 on v6

--- a/solution.py
+++ b/solution.py
@@ -148,11 +148,15 @@
         mn = None
         total = jnp.zeros((8, bq), f32)
         mixed = jnp.zeros((hd, bq), f32)
+        held = None
         for i in range(nk):
             mn = chunk_scores(hn, q, i, nxt, mn)
+            if held is not None:
+                mixed = mixed + mm(vt[h, :, (i - 1) * kc:i * kc], held)
             e = jnp.exp2(cur[i * kc:(i + 1) * kc, :] - top)
             total = total + jnp.sum(fold8(e), axis=0)
-            mixed = mixed + mm(vt[h, :, i * kc:(i + 1) * kc], e.astype(bf16))
+            held = e.astype(bf16)
+        mixed = mixed + mm(vt[h, :, (nk - 1) * kc:], held)
         cols = pl.ds(pl.multiple_of(qb * bq, bq), bq)
         mixed = mixed / jnp.sum(total, axis=0, keepdims=True)
         gat[pl.ds(pl.multiple_of(h * hd, hd), hd), :] = (mixed * sig[h, :, cols]).astype(bf16)
@@ -320,7 +324,7 @@
     zout[...] = zfin[...].astype(bf16)
 
 
-def row_stage(net, x_ref, z_ref, mask_ref, wb_ref, win_ref, wout_ref, ship, side,
+def row_stage(net, x_ref, z_ref, mask_ref, wb_ref, win_ref, wout_ref, ship, side, stash,
               kk, qt, vt, sig, gat, bias, wt, qd0, qd1, bsend, bbuf, bscr, ytr):
     tokens, width = x_ref.shape
     size = bias.shape[0]
@@ -356,22 +360,38 @@
         return carry
 
     lax.fori_loop(0, tokens // bp, project, 0)
+    slab = heads // 2
+
+    def prescore(s, u, buf, qd):
+        cols = pl.ds(pl.multiple_of(s * size, size), size)
+        for h in range(heads):
+            qd[h * hd:(h + 1) * hd, h * size:(h + 1) * size] = qt[h * hd:(h + 1) * hd, cols]
+        for g in range(2):
+            out = pl.ds(pl.multiple_of((2 * u + g) * size, size), size)
+            buf[out, :] = mm(kk[cols, :], qd[:, g * slab * size:(g + 1) * slab * size]) * c
+
+    for k, buf in enumerate(stash):
+        def ahead(u, carry):
+            prescore(k * SLOT + 2 * u, 2 * u, buf, qd0)
+            prescore(k * SLOT + 2 * u + 1, 2 * u + 1, buf, qd1)
+            return carry
+
+        lax.fori_loop(0, SLOT // 2, ahead, 0)
     side()
     net.settle(bbuf.at[pl.ds(0, group - 1)], 7)
     bscr[...] = bbuf[...].astype(f32).reshape(group * SLOT, size)
     for h in range(heads):
         bias[:, h * size:(h + 1) * size] = jnp.transpose(bscr[pl.ds(h, size, stride=SLOT), :] * LOG2E)
 
-    def one(s, qd):
+    def one(s, u, buf):
         cols = pl.ds(pl.multiple_of(s * size, size), size)
-        for h in range(heads):
-            qd[h * hd:(h + 1) * hd, h * size:(h + 1) * size] = qt[h * hd:(h + 1) * hd, cols]
         mrow = mask_ref[pl.ds(me * seqs + s, 1), :]
         keep = jnp.transpose(jnp.broadcast_to(mrow.astype(f32), (size, size))) != 0
         keep2 = jnp.concatenate([keep, keep], axis=1)
         for h in range(0, heads, 2):
             two = slice(h * size, (h + 2) * size)
-            t = mm(kk[cols, :], qd[:, two]) * c + bias[:, two]
+            rows = pl.ds(pl.multiple_of((2 * u + h // slab) * size, size), size)
+            t = buf[rows, h % slab * size:(h % slab + 2) * size] + bias[:, two]
             t = jnp.where(keep2, t, NEG)
             e = jnp.exp2(t - jnp.max(t, axis=0, keepdims=True))
             total = jnp.sum(e, axis=0, keepdims=True)
@@ -379,24 +399,21 @@
             gat[h * hd:(h + 1) * hd, cols] = (mixed[:hd, :size] * sig[h * hd:(h + 1) * hd, cols]).astype(bf16)
             gat[(h + 1) * hd:(h + 2) * hd, cols] = (mixed[hd:, size:] * sig[(h + 1) * hd:(h + 2) * hd, cols]).astype(bf16)
 
-    def chunk(k, carry):
-        def pair(u, carry):
-            one(k * SLOT + 2 * u, qd0)
-            one(k * SLOT + 2 * u + 1, qd1)
+    for k, buf in enumerate(stash):
+        def several(u, carry):
+            for j in range(4):
+                one(k * SLOT + 4 * u + j, 4 * u + j, buf)
             return carry
 
-        lax.fori_loop(0, SLOT // 2, pair, 0)
+        lax.fori_loop(0, SLOT // 4, several, 0)
         for b in range(SLOT * size // bp):
-            rows = pl.ds(pl.multiple_of((k * SLOT * size // bp + b) * bp, bp), bp)
+            rows = slice((k * SLOT * size // bp + b) * bp, (k * SLOT * size // bp + b + 1) * bp)
             y = (x_ref[rows, :].astype(f32) + mm(gat[:, rows], wout_ref[...], TN)).astype(bf16).astype(f32)
             for i in range(bp // size):
                 for half in range(width // 128):
                     ytr[half, pl.ds(b * (bp // size) + i, size, stride=SLOT), :] = (
                         y[i * size:(i + 1) * size, half * 128:(half + 1) * 128])
         ship(k, jnp.concatenate([ytr[half] for half in range(width // 128)], axis=1).astype(bf16))
-        return carry
-
-    lax.fori_loop(0, seqs // SLOT, chunk, 0)
 
 
 def block_kernel(group, dap, m_ref, z_ref, mask_ref, res_ref, wr_in, wr_bias, wr_out, wc_in, wc_out, wopm_in, wopm_out,
@@ -428,7 +445,7 @@
         xbuf[k, me] = msend[k, me]
         net.to_all(lambda t: (msend.at[k, t], xbuf.at[k, me]), 8 + k)
 
-    row_stage(net, m_ref, z_ref, mask_ref, wr_bias, wr_in, wr_out, ship, side,
+    row_stage(net, m_ref, z_ref, mask_ref, wr_bias, wr_in, wr_out, ship, side, (s0, s1),
               kk, qt, rvt, rsig, rgat, bias, rwt, qd0, qd1, rsend, rbuf, rscr, ytr)
 
     def arrive(b):

time: 130 us -> 122 us (0.938)
  Pallas kernels: 126 us -> 118 us
    pallas_call x1, Pallas kernels: 126 us -> 118 us  [block_update(): pl.pallas_call(functools.partial(block_kernel, group, dap), out_shape=(ja...]
where the time goes in v7:
time: 122 us
  Pallas kernels  118 us (97%)
  local copies, waits for them, and re-layouts  3.05 us (2%)
    pallas_call x1, Pallas kernels, block_update(): pl.pallas_call(functools.partial(block_kernel, group, dap), out_shape=(ja...  118 us

profile of v7, /device:TPU:1, one launch (start us, length us, event | category | flops | bytes accessed | tf_op | source)
XLA Modules:
  0.0 121.6 jit_solution(8134188475144213445)
XLA Ops:
  0.6 117.9 %block_update.1 = (bf16[2,128,8,256]{3,2,1,0:T(8,128)(2,1)}, bf16[128,128]{1,0:T(8,128)(2,1)}) custom-call(bf16[2048,256]{1,0:T(8,128)(2,1)} %bitcast.10, bf16[128,128]{1,0:T(8,128)(2,1)} %bitcast.13, s32[2048,128]{1,0:T(8,128)} %mask_ref.1, s32[1,128]{1,0:T(1,128)} %bitcast.19, bf16[256,1024]{1,0:T(8,128)(2,1)} %wr_in.1, bf16[8,128]{1,0:T(8,128)(2,1)} %bitcast.16, ...), custom_call_target="tpu_custom_call" | custom-call | tf_op jit(solution)/shard_map/block_update/pallas_call | solution.py:567
  118.5 0.0 copy-start
  118.5 2.4 %copy.19 = bf16[2,8,128,256]{3,2,1,0:T(8,128)(2,1)} copy(bf16[2,8,128,256]{3,1,2,0:T(8,128)(2,1)} %bitcast.12) | data formatting | bytes 2097152 | tf_op jit(solution)/shard_map/transpose | solution.py:594
  121.0 0.0 copy-done
  121.0 0.6 copy.21
Async XLA Ops:
  118.5 2.4 %copy-start = (bf16[128,128]{1,0:T(8,128)(2,1)S(1)}, bf16[128,128]{1,0:T(8,128)(2,1)}, u32[]{:S(2)}) copy-start(bf16[128,128]{1,0:T(8,128)(2,1)} %get-tuple-element.5) | copy-start | bytes 98308

commit v8 on v7

--- a/solution.py
+++ b/solution.py
@@ -253,7 +253,22 @@
     return jnp.concatenate([rows, jnp.zeros((spare, rows.shape[1]), bf16)], axis=0) if spare else rows
 
 
-def pair_stage(net, z_ref, norm, mask_ref, wopm_ref, ws_in, ws_bias, ws_out, we_in, we_bias, we_out, zout,
+def untile(block):
+    size = block.shape[0]
+    out = jnp.transpose(block)
+    row = lax.broadcasted_iota(jnp.int32, (size, size), 0)
+    lane = lax.broadcasted_iota(jnp.int32, (size, size), 1)
+    step = INNER // 2
+    while step:
+        low, high = lax.rem(lax.div(row, step), 2), lax.rem(lax.div(lane, step), 2)
+        down = pltpu.roll(pltpu.roll(out, size - step, 0), step, 1)
+        back = pltpu.roll(pltpu.roll(out, step, 0), size - step, 1)
+        out = jnp.where(low == high, out, jnp.where(low < high, down, back))
+        step //= 2
+    return out
+
+
+def pair_stage(net, z_ref, norm, tnorm, ztbuf, mask_ref, wopm_ref, ws_in, ws_bias, ws_out, we_in, we_bias, we_out, zout,
                abuf, cbuf, oscr, uscr, usend, ubuf, zrow, bsend, bbuf, bscr, esend, ebuf, zsend, zfin):
     me, lo, group, outer_n = net.me, net.lo, net.group, net.outer_n
     blocks, opm = abuf.shape[0], abuf.shape[2]
@@ -290,18 +305,22 @@
         usend[x] = uscr[pl.ds(x, outer_n, stride=INNER), :]
     ubuf[lo] = usend[lo]
     net.to_inner(lambda x: (usend.at[x], ubuf.at[lo]), 3)
+    net.settle(ztbuf.at[pl.ds(0, INNER - 1)], 14)
+    for x in range(INNER):
+        zrow[pl.ds(x, outer_n, stride=INNER), :] = ztbuf[x]
+    tile = (zrow[...] + up / (1e-3 + tnorm[...])).astype(bf16)
+    bsend[...] = bias_rows(tile, ws_bias)
+    bbuf[me] = bsend[...]
+    net.to_all(lambda t: (bsend, bbuf.at[me]), 4)
     net.settle(ubuf.at[pl.ds(0, INNER - 1)], 3)
     for x in range(INNER):
         zrow[pl.ds(x, outer_n, stride=INNER), :] = ubuf[x]
     z1 = (z_ref[...].astype(f32) + zrow[...] / (1e-3 + norm[...])).astype(bf16)
 
-    bsend[...] = bias_rows(z1, ws_bias)
-    bbuf[me] = bsend[...]
-    net.to_all(lambda t: (bsend, bbuf.at[me]), 4)
     parts = pair_project(z1, ws_in, fold)
     net.settle(bbuf.at[pl.ds(0, group - 1)], 4)
     bscr[...] = bbuf[...].astype(f32).reshape(group * SLOT, size)
-    biases = [jnp.transpose(bscr[pl.ds(h, size, stride=SLOT), :]) for h in range(heads)]
+    biases = [untile(bscr[pl.ds(h, size, stride=SLOT), :]) for h in range(heads)]
     z2 = pair_attend(z1, parts, biases, keep, ws_out)
 
     end_rows = bias_rows(z2, we_bias).astype(f32)
@@ -418,7 +437,7 @@
 
 def block_kernel(group, dap, m_ref, z_ref, mask_ref, res_ref, wr_in, wr_bias, wr_out, wc_in, wc_out, wopm_in, wopm_out,
                  ws_in, ws_bias, ws_out, we_in, we_bias, we_out, mout, zout,
-                 kk, qt, rvt, rsig, rgat, bias, rwt, qd0, qd1, rsend, rbuf, rscr, ytr, msend, xbuf, mrow, norm,
+                 kk, qt, rvt, rsig, rgat, bias, rwt, qd0, qd1, rsend, rbuf, rscr, ytr, msend, xbuf, mrow, norm, tnorm, zst, ztbuf,
                  kaug, qaug, vt, sig, gat, s0, s1, wt, wka, ycol, acs, abuf, cbuf,
                  oscr, uscr, usend, ubuf, zrow, bsend, bbuf, bscr, esend, ebuf, zsend, zfin, send, recv):
     net = Links(group, dap, send, recv)
@@ -431,7 +450,17 @@
     turns = group // per
 
     def side():
+        zrow[...] = z_ref[...].astype(f32)
+        for x in range(INNER):
+            zst[x] = zrow[pl.ds(x, group // INNER, stride=INNER), :]
+        ztbuf[lo] = zst[lo]
+        net.to_inner(lambda x: (zst.at[x], ztbuf.at[lo]), 14)
         flags = mask_ref[...].astype(bf16)
+        source = lax.broadcasted_iota(jnp.int32, (size, size), 0)
+        pair = lax.broadcasted_iota(jnp.int32, (size, size), 1)
+        rows_i = mm(flags, (source == hi * INNER + lax.rem(pair, INNER)).astype(bf16))
+        rows_j = mm(flags, (source == lax.div(pair, INNER) * INNER + lo).astype(bf16))
+        tnorm[...] = jnp.transpose(jnp.broadcast_to(jnp.sum(rows_i * rows_j, axis=0, keepdims=True), (size, size)))
         pick = (lax.broadcasted_iota(jnp.int32, (size, size), 0) == me).astype(bf16)
         norm[...] = mm(flags, mm(flags, pick).astype(bf16), TN)
         row = (lax.broadcasted_iota(jnp.int32, (SLOT, size), 1) == me).astype(bf16)
@@ -492,12 +521,12 @@
     pass_on(cbuf.shape[0] - 1)
     net.settle(cbuf.at[:, pl.ds(0, net.outer_n // 2)], 1)
     net.settle(abuf.at[:, pl.ds(0, INNER - 1)], 0)
-    pair_stage(net, z_ref, norm, res_ref, wopm_out, ws_in, ws_bias, ws_out, we_in, we_bias, we_out, zout,
+    pair_stage(net, z_ref, norm, tnorm, ztbuf, res_ref, wopm_out, ws_in, ws_bias, ws_out, we_in, we_bias, we_out, zout,
                abuf, cbuf, oscr, uscr, usend, ubuf, zrow, bsend, bbuf, bscr, esend, ebuf, zsend, zfin)
     net.settle(mout.at[:, pl.ds(0, group - 1)], 2)
 
 
-def row_scratch(tokens, size, width, heads, fold, group):
+def row_scratch(tokens, size, width, z_width, heads, fold, group):
     seqs = tokens // size
     return [
         pltpu.VMEM((tokens, fold), bf16),
@@ -517,6 +546,9 @@
         pltpu.VMEM((seqs // SLOT, group, SLOT, width), bf16),
         pltpu.VMEM((SLOT, seqs * group), f32),
         pltpu.VMEM((size, size), f32),
+        pltpu.VMEM((size, size), f32),
+        pltpu.VMEM((INNER, group // INNER, z_width), f32),
+        pltpu.VMEM((INNER, group // INNER, z_width), f32),
     ]
 
 
@@ -569,10 +601,10 @@
         out_shape=(jax.ShapeDtypeStruct((seqs // SLOT, group, SLOT, m_width), bf16), jax.ShapeDtypeStruct((size, width), bf16)),
         in_specs=[vm] * (4 + len(weights)),
         out_specs=(vm, vm),
-        scratch_shapes=row_scratch(tokens, size, m_width, heads, fold, group)
+        scratch_shapes=row_scratch(tokens, size, m_width, width, heads, fold, group)
         + col_scratch(seq, m_width, heads, fold // heads, bq)
         + pair_scratch(seq, size, width, opm, group, bq)
-        + [pltpu.SemaphoreType.DMA((14,)), pltpu.SemaphoreType.DMA((14,))],
+        + [pltpu.SemaphoreType.DMA((15,)), pltpu.SemaphoreType.DMA((15,))],
         compiler_params=pltpu.CompilerParams(collective_id=1, has_side_effects=True, vmem_limit_bytes=63 << 20),
         name='block_update',
     )(m, z, msa_mask, res_mask, *weights)

time: 122 us -> 120 us (0.984)
  Pallas kernels: 118 us -> 116 us
    pallas_call x1, Pallas kernels: 118 us -> 116 us  [block_update(): pl.pallas_call(functools.partial(block_kernel, group, dap), out_shape=(ja...]
where the time goes in v8:
time: 120 us
  Pallas kernels  116 us (97%)
  local copies, waits for them, and re-layouts  3.05 us (3%)
    pallas_call x1, Pallas kernels, block_update(): pl.pallas_call(functools.partial(block_kernel, group, dap), out_shape=(ja...  116 us
    transpose x1, local copies, waits for them, and re-layouts, per_device(): m_out = jnp.swapaxes(slots, 1, 2).reshape(seqs, res, width)  2.43 us

profile of v8, /device:TPU:1, one launch (start us, length us, event | category | flops | bytes accessed | tf_op | source)
XLA Modules:
  0.0 120.2 jit_solution(1346855159043557368)
XLA Ops:
  0.6 116.5 %block_update.1 = (bf16[2,128,8,256]{3,2,1,0:T(8,128)(2,1)}, bf16[128,128]{1,0:T(8,128)(2,1)}) custom-call(bf16[2048,256]{1,0:T(8,128)(2,1)} %bitcast.10, bf16[128,128]{1,0:T(8,128)(2,1)} %bitcast.13, s32[2048,128]{1,0:T(8,128)} %mask_ref.1, s32[1,128]{1,0:T(1,128)} %bitcast.19, bf16[256,1024]{1,0:T(8,128)(2,1)} %wr_in.1, bf16[8,128]{1,0:T(8,128)(2,1)} %bitcast.16, ...), custom_call_target="tpu_custom_call" | custom-call | tf_op jit(solution)/shard_map/block_update/pallas_call | solution.py:599
  117.1 0.0 copy-start
  117.1 2.4 %copy.19 = bf16[2,8,128,256]{3,2,1,0:T(8,128)(2,1)} copy(bf16[2,8,128,256]{3,1,2,0:T(8,128)(2,1)} %bitcast.12) | data formatting | bytes 2097152 | tf_op jit(solution)/shard_map/transpose | solution.py:626
  119.5 0.0 copy-done
  119.5 0.6 copy.21
Async XLA Ops:
  117.1 2.4 %copy-start = (bf16[128,128]{1,0:T(8,128)(2,1)S(1)}, bf16[128,128]{1,0:T(8,128)(2,1)}, u32[]{:S(2)}) copy-start(bf16[128,128]{1,0:T(8,128)(2,1)} %get-tuple-element.5) | copy-start | bytes 98308

commit v9 on v8

--- a/solution.py
+++ b/solution.py
@@ -268,7 +268,7 @@
     return out
 
 
-def pair_stage(net, z_ref, norm, tnorm, ztbuf, mask_ref, wopm_ref, ws_in, ws_bias, ws_out, we_in, we_bias, we_out, zout,
+def pair_stage(net, between, collect, z_ref, norm, tnorm, ztbuf, mask_ref, wopm_ref, ws_in, ws_bias, ws_out, we_in, we_bias, we_out, zout,
                abuf, cbuf, oscr, uscr, usend, ubuf, zrow, bsend, bbuf, bscr, esend, ebuf, zsend, zfin):
     me, lo, group, outer_n = net.me, net.lo, net.group, net.outer_n
     blocks, opm = abuf.shape[0], abuf.shape[2]
@@ -280,6 +280,8 @@
     per = 128 // opm
     outer = None
     for q in range(blocks):
+        net.settle(abuf.at[q, pl.ds(0, INNER - 1)], 15 + q)
+        net.settle(cbuf.at[q, pl.ds(0, outer_n // 2)], 19 + q)
         term = mm(abuf[q].reshape(INNER * opm, -1), cbuf[q].reshape(outer_n * opm, -1), NT)
         outer = term if outer is None else outer + term
     for g in range(outer_n // per):
@@ -312,6 +314,7 @@
     bsend[...] = bias_rows(tile, ws_bias)
     bbuf[me] = bsend[...]
     net.to_all(lambda t: (bsend, bbuf.at[me]), 4)
+    between()
     net.settle(ubuf.at[pl.ds(0, INNER - 1)], 3)
     for x in range(INNER):
         zrow[pl.ds(x, outer_n, stride=INNER), :] = ubuf[x]
@@ -339,6 +342,7 @@
     zsend[...] = z3.astype(f32)
     zfin[pl.ds(me, 1), :] = zsend[pl.ds(me, 1), :]
     net.to_all(lambda t: (zsend.at[pl.ds(t, 1)], zfin.at[pl.ds(me, 1)]), 6)
+    collect()
     net.settle(zfin.at[pl.ds(0, group - 1)], 6)
     zout[...] = zfin[...].astype(bf16)
 
@@ -437,7 +441,7 @@
 
 def block_kernel(group, dap, m_ref, z_ref, mask_ref, res_ref, wr_in, wr_bias, wr_out, wc_in, wc_out, wopm_in, wopm_out,
                  ws_in, ws_bias, ws_out, we_in, we_bias, we_out, mout, zout,
-                 kk, qt, rvt, rsig, rgat, bias, rwt, qd0, qd1, rsend, rbuf, rscr, ytr, msend, xbuf, mrow, norm, tnorm, zst, ztbuf,
+                 kk, qt, rvt, rsig, rgat, bias, rwt, qd0, qd1, rsend, rbuf, rscr, ytr, msend, xbuf, mrow, norm, tnorm, zst, ztbuf, mslot,
                  kaug, qaug, vt, sig, gat, s0, s1, wt, wka, ycol, acs, abuf, cbuf,
                  oscr, uscr, usend, ubuf, zrow, bsend, bbuf, bscr, esend, ebuf, zsend, zfin, send, recv):
     net = Links(group, dap, send, recv)
@@ -455,6 +459,13 @@
             zst[x] = zrow[pl.ds(x, group // INNER, stride=INNER), :]
         ztbuf[lo] = zst[lo]
         net.to_inner(lambda x: (zst.at[x], ztbuf.at[lo]), 14)
+        row = (lax.broadcasted_iota(jnp.int32, (SLOT, size), 1) == me).astype(bf16)
+        split = mask_ref[...].reshape(group, chunks, SLOT, size)
+        for k in range(chunks):
+            mrow[:, k * group * SLOT:(k + 1) * group * SLOT] = mm(
+                row, split[:, k].astype(f32).reshape(group * SLOT, size).astype(bf16), NT)
+
+    def normalisers():
         flags = mask_ref[...].astype(bf16)
         source = lax.broadcasted_iota(jnp.int32, (size, size), 0)
         pair = lax.broadcasted_iota(jnp.int32, (size, size), 1)
@@ -463,11 +474,6 @@
         tnorm[...] = jnp.transpose(jnp.broadcast_to(jnp.sum(rows_i * rows_j, axis=0, keepdims=True), (size, size)))
         pick = (lax.broadcasted_iota(jnp.int32, (size, size), 0) == me).astype(bf16)
         norm[...] = mm(flags, mm(flags, pick).astype(bf16), TN)
-        row = (lax.broadcasted_iota(jnp.int32, (SLOT, size), 1) == me).astype(bf16)
-        split = mask_ref[...].reshape(group, chunks, SLOT, size)
-        for k in range(chunks):
-            mrow[:, k * group * SLOT:(k + 1) * group * SLOT] = mm(
-                row, split[:, k].astype(f32).reshape(group * SLOT, size).astype(bf16), NT)
 
     def ship(k, y):
         msend[k] = y.astype(f32).reshape(group, SLOT, -1).astype(bf16)
@@ -491,7 +497,31 @@
 
     def pass_on(qb):
         net.settle(cbuf.at[qb, pl.ds(0, net.outer_n // 2 - 1)], 10 + qb)
-        net.to_partner(cbuf.at[qb, half], 1)
+        net.to_partner(cbuf.at[qb, half], 19 + qb)
+
+    last = cbuf.shape[0] - 1
+
+    def give_back(qb):
+        def share_m(o):
+            i = lax.rem(me + o, per)
+            t = lax.rem(qb, turns) * per + i
+
+            @pl.when(t != me)
+            def _():
+                net.copy(ycol.at[qb, i], mslot.at[lax.div(qb, turns), me], 2, t).start()
+
+        each(0, per, share_m)
+
+    def collect():
+        net.settle(mslot.at[:, pl.ds(0, group - 1)], 2)
+        for k in range(chunks):
+            y = mslot[k].astype(f32).reshape(group * SLOT, -1)
+            for side_half in range(ytr.shape[0]):
+                lanes = slice(side_half * 128, (side_half + 1) * 128)
+                ytr[side_half] = y[:, lanes]
+                for r in range(SLOT):
+                    at = (k * SLOT + r) * size
+                    mout[at:at + size, lanes] = ytr[side_half, pl.ds(r, size, stride=SLOT), :].astype(bf16)
 
     def emit(qb, y, ac):
         ycol[qb] = y.astype(f32).reshape(per, SLOT, -1).astype(bf16)
@@ -499,31 +529,23 @@
         abuf[qb, lo] = ac[:opm]
         cbuf[qb, hi] = ac[opm:]
         net.to_half(acs.at[qb, pl.ds(opm, opm)], cbuf.at[qb, hi], 10 + qb)
-        net.to_inner(lambda x: (acs.at[qb, pl.ds(0, opm)], abuf.at[qb, lo]), 0)
+        net.to_inner(lambda x: (acs.at[qb, pl.ds(0, opm)], abuf.at[qb, lo]), 15 + qb)
 
         @pl.when(qb > 0)
         def _():
             pass_on(qb - 1)
 
-        def share_m(o):
-            i = lax.rem(me + o, per)
-            t = lax.rem(qb, turns) * per + i
-
-            @pl.when(t != me)
-            def _():
-                net.copy(ycol.at[qb, i], mout.at[lax.div(qb, turns), me], 2, t).start()
-
-        each(0, per, share_m)
+        @pl.when(qb < last)
+        def _():
+            give_back(qb)
 
     col_stage(arrive, load, seq, mrow, wc_in, wc_out, wopm_in, emit, kaug, qaug, vt, sig, gat, s0, s1, wt, wka)
     for k in range(chunks):
-        mout[k, me] = ycol[k * turns + lax.div(me, per), lax.rem(me, per)]
-    pass_on(cbuf.shape[0] - 1)
-    net.settle(cbuf.at[:, pl.ds(0, net.outer_n // 2)], 1)
-    net.settle(abuf.at[:, pl.ds(0, INNER - 1)], 0)
-    pair_stage(net, z_ref, norm, tnorm, ztbuf, res_ref, wopm_out, ws_in, ws_bias, ws_out, we_in, we_bias, we_out, zout,
+        mslot[k, me] = ycol[k * turns + lax.div(me, per), lax.rem(me, per)]
+    normalisers()
+    pass_on(last)
+    pair_stage(net, lambda: give_back(last), collect, z_ref, norm, tnorm, ztbuf, res_ref, wopm_out, ws_in, ws_bias, ws_out, we_in, we_bias, we_out, zout,
                abuf, cbuf, oscr, uscr, usend, ubuf, zrow, bsend, bbuf, bscr, esend, ebuf, zsend, zfin)
-    net.settle(mout.at[:, pl.ds(0, group - 1)], 2)
 
 
 def row_scratch(tokens, size, width, z_width, heads, fold, group):
@@ -549,6 +571,7 @@
         pltpu.VMEM((size, size), f32),
         pltpu.VMEM((INNER, group // INNER, z_width), f32),
         pltpu.VMEM((INNER, group // INNER, z_width), f32),
+        pltpu.VMEM((seqs // SLOT, group, SLOT, width), bf16),
     ]
 
 
@@ -598,13 +621,13 @@
     opm = weights[5].shape[0] // 2
     return pl.pallas_call(
         functools.partial(block_kernel, group, dap),
-        out_shape=(jax.ShapeDtypeStruct((seqs // SLOT, group, SLOT, m_width), bf16), jax.ShapeDtypeStruct((size, width), bf16)),
+        out_shape=(jax.ShapeDtypeStruct((tokens, m_width), bf16), jax.ShapeDtypeStruct((size, width), bf16)),
         in_specs=[vm] * (4 + len(weights)),
         out_specs=(vm, vm),
         scratch_shapes=row_scratch(tokens, size, m_width, width, heads, fold, group)
         + col_scratch(seq, m_width, heads, fold // heads, bq)
         + pair_scratch(seq, size, width, opm, group, bq)
-        + [pltpu.SemaphoreType.DMA((15,)), pltpu.SemaphoreType.DMA((15,))],
+        + [pltpu.SemaphoreType.DMA((23,)), pltpu.SemaphoreType.DMA((23,))],
         compiler_params=pltpu.CompilerParams(collective_id=1, has_side_effects=True, vmem_limit_bytes=63 << 20),
         name='block_update',
     )(m, z, msa_mask, res_mask, *weights)
@@ -621,9 +644,8 @@
         seqs, res, width = m_blk.shape
         weights = (w_row_in, w_row_bias.T, w_row_out, w_col_in, w_col_out, w_opm_in.T, w_opm_out,
                    w_start_in, w_start_bias.T, w_start_out, w_end_in, w_end_bias.T, w_end_out)
-        slots, z_out = block_update(m_blk.reshape(seqs * res, width), z_blk[0], msa_mask, res_mask[None, :], weights,
+        m_out, z_out = block_update(m_blk.reshape(seqs * res, width), z_blk[0], msa_mask, res_mask[None, :], weights,
                                     w_row_bias.shape[1], group_size, dap_size)
-        m_out = jnp.swapaxes(slots, 1, 2).reshape(seqs, res, width)
-        return m_out, z_out[None]
+        return m_out.reshape(seqs, res, width), z_out[None]
 
     return jax.shard_map(per_device, mesh=mesh, in_specs=in_specs, out_specs=(rows, rows), check_vma=False)

time: 120 us -> 116 us (0.967)
  Pallas kernels: 116 us -> 112 us
    pallas_call x1, Pallas kernels: 116 us -> 112 us  [block_update(): pl.pallas_call(functools.partial(block_kernel, group, dap), out_shape=(ja...]
    transpose x1 -> x0, local copies, waits for them, and re-layouts: 2.43 us -> none  [per_device(): m_out = jnp.swapaxes(slots, 1, 2).reshape(seqs, res, width)]
    unnamed x3 -> x4, local copies, waits for them, and re-layouts: 0.62 us -> 2.91 us
where the time goes in v9:
time: 116 us
  Pallas kernels  112 us (97%)
  local copies, waits for them, and re-layouts  2.91 us (3%)
    pallas_call x1, Pallas kernels, block_update(): pl.pallas_call(functools.partial(block_kernel, group, dap), out_shape=(ja...  112 us
    unnamed x4, local copies, waits for them, and re-layouts  2.91 us

profile of v9, /device:TPU:1, one launch (start us, length us, event | category | flops | bytes accessed | tf_op | source)
XLA Modules:
  0.0 116.0 jit_solution(4219905419485794111)
XLA Ops:
  0.6 112.5 %block_update.1 = (bf16[2048,256]{1,0:T(8,128)(2,1)}, bf16[128,128]{1,0:T(8,128)(2,1)}) custom-call(bf16[2048,256]{1,0:T(8,128)(2,1)} %bitcast.9, bf16[128,128]{1,0:T(8,128)(2,1)} %bitcast.11, s32[2048,128]{1,0:T(8,128)} %mask_ref.1, s32[1,128]{1,0:T(1,128)} %bitcast.17, bf16[256,1024]{1,0:T(8,128)(2,1)} %wr_in.1, bf16[8,128]{1,0:T(8,128)(2,1)} %bitcast.14, ...), custom_call_target="tpu_custom_call" | custom-call | tf_op jit(solution)/shard_map/block_update/pallas_call | solution.py:622
  113.1 0.0 copy-start
  113.1 2.3 %copy.21 = bf16[16,128,256]{2,1,0:T(8,128)(2,1)} copy(bf16[16,128,256]{2,1,0:T(8,128)(2,1)} %bitcast.10) | data formatting | bytes 2097152
  115.4 0.0 copy-done
  115.4 0.6 copy.22
Async XLA Ops:
  113.1 2.3 %copy-start = (bf16[128,128]{1,0:T(8,128)(2,1)S(1)}, bf16[128,128]{1,0:T(8,128)(2,1)}, u32[]{:S(2)}) copy-start(bf16[128,128]{1,0:T(8,128)(2,1)} %get-tuple-element.5) | copy-start | bytes 98308

commit v10 on v9

--- a/solution.py
+++ b/solution.py
@@ -181,7 +181,7 @@
     lax.fori_loop(0, nq, block, m)
 
 
-def each(start, stop, one, step=8):
+def each(start, stop, one, step=32):
     whole = (stop - start) // step
 
     def some(i, carry):
@@ -423,12 +423,8 @@
             gat[(h + 1) * hd:(h + 2) * hd, cols] = (mixed[hd:, size:] * sig[(h + 1) * hd:(h + 2) * hd, cols]).astype(bf16)
 
     for k, buf in enumerate(stash):
-        def several(u, carry):
-            for j in range(4):
-                one(k * SLOT + 4 * u + j, 4 * u + j, buf)
-            return carry
-
-        lax.fori_loop(0, SLOT // 4, several, 0)
+        for j in range(SLOT):
+            one(k * SLOT + j, j, buf)
         for b in range(SLOT * size // bp):
             rows = slice((k * SLOT * size // bp + b) * bp, (k * SLOT * size // bp + b + 1) * bp)
             y = (x_ref[rows, :].astype(f32) + mm(gat[:, rows], wout_ref[...], TN)).astype(bf16).astype(f32)
@@ -535,7 +531,7 @@
         def _():
             pass_on(qb - 1)
 
-        @pl.when(qb < last)
+        @pl.when(qb < last - 1)
         def _():
             give_back(qb)
 
@@ -544,7 +540,7 @@
         mslot[k, me] = ycol[k * turns + lax.div(me, per), lax.rem(me, per)]
     normalisers()
     pass_on(last)
-    pair_stage(net, lambda: give_back(last), collect, z_ref, norm, tnorm, ztbuf, res_ref, wopm_out, ws_in, ws_bias, ws_out, we_in, we_bias, we_out, zout,
+    pair_stage(net, lambda: (give_back(last - 1), give_back(last)), collect, z_ref, norm, tnorm, ztbuf, res_ref, wopm_out, ws_in, ws_bias, ws_out, we_in, we_bias, we_out, zout,
                abuf, cbuf, oscr, uscr, usend, ubuf, zrow, bsend, bbuf, bscr, esend, ebuf, zsend, zfin)
 
 

time: 116 us -> 115 us (level)
    pallas_call x1, Pallas kernels: 112 us -> 111 us  [block_update(): pl.pallas_call(functools.partial(block_kernel, group, dap), out_shape=(ja...]
where the time goes in v10:
time: 115 us
  Pallas kernels  111 us (97%)
  local copies, waits for them, and re-layouts  2.91 us (3%)
    pallas_call x1, Pallas kernels, block_update(): pl.pallas_call(functools.partial(block_kernel, group, dap), out_shape=(ja...  111 us
    unnamed x4, local copies, waits for them, and re-layouts  2.91 us

profile of v10, /device:TPU:1, one launch (start us, length us, event | category | flops | bytes accessed | tf_op | source)
XLA Modules:
  0.0 114.8 jit_solution(16068206442085703084)
XLA Ops:
  0.6 111.2 %block_update.1 = (bf16[2048,256]{1,0:T(8,128)(2,1)}, bf16[128,128]{1,0:T(8,128)(2,1)}) custom-call(bf16[2048,256]{1,0:T(8,128)(2,1)} %bitcast.9, bf16[128,128]{1,0:T(8,128)(2,1)} %bitcast.11, s32[2048,128]{1,0:T(8,128)} %mask_ref.1, s32[1,128]{1,0:T(1,128)} %bitcast.17, bf16[256,1024]{1,0:T(8,128)(2,1)} %wr_in.1, bf16[8,128]{1,0:T(8,128)(2,1)} %bitcast.14, ...), custom_call_target="tpu_custom_call" | custom-call | tf_op jit(solution)/shard_map/block_update/pallas_call | solution.py:618
  111.9 0.0 copy-start
  111.9 2.3 %copy.21 = bf16[16,128,256]{2,1,0:T(8,128)(2,1)} copy(bf16[16,128,256]{2,1,0:T(8,128)(2,1)} %bitcast.10) | data formatting | bytes 2097152
  114.2 0.0 copy-done
  114.2 0.6 copy.22
Async XLA Ops:
  111.9 2.3 %copy-start = (bf16[128,128]{1,0:T(8,128)(2,1)S(1)}, bf16[128,128]{1,0:T(8,128)(2,1)}, u32[]{:S(2)}) copy-start(bf16[128,128]{1,0:T(8,128)(2,1)} %get-tuple-element.5) | copy-start | bytes 98308

commit v11 on v10

--- a/solution.py
+++ b/solution.py
@@ -394,12 +394,9 @@
             buf[out, :] = mm(kk[cols, :], qd[:, g * slab * size:(g + 1) * slab * size]) * c
 
     for k, buf in enumerate(stash):
-        def ahead(u, carry):
-            prescore(k * SLOT + 2 * u, 2 * u, buf, qd0)
-            prescore(k * SLOT + 2 * u + 1, 2 * u + 1, buf, qd1)
-            return carry
-
-        lax.fori_loop(0, SLOT // 2, ahead, 0)
+        for j in range(SLOT):
+            prescore(k * SLOT + j, j, buf, (qd0, qd1)[j % 2])
+
     side()
     net.settle(bbuf.at[pl.ds(0, group - 1)], 7)
     bscr[...] = bbuf[...].astype(f32).reshape(group * SLOT, size)

time: 115 us -> 115 us (level)
  no operation moved by 1% of the time
where the time goes in v11:
time: 115 us
  Pallas kernels  111 us (97%)
  local copies, waits for them, and re-layouts  2.91 us (3%)
    pallas_call x1, Pallas kernels, block_update(): pl.pallas_call(functools.partial(block_kernel, group, dap), out_shape=(ja...  111 us
    unnamed x4, local copies, waits for them, and re-layouts  2.91 us

profile of v11, /device:TPU:1, one launch (start us, length us, event | category | flops | bytes accessed | tf_op | source)
XLA Modules:
  0.0 114.8 jit_solution(7871043198405908138)
XLA Ops:
  0.6 111.3 %block_update.1 = (bf16[2048,256]{1,0:T(8,128)(2,1)}, bf16[128,128]{1,0:T(8,128)(2,1)}) custom-call(bf16[2048,256]{1,0:T(8,128)(2,1)} %bitcast.9, bf16[128,128]{1,0:T(8,128)(2,1)} %bitcast.11, s32[2048,128]{1,0:T(8,128)} %mask_ref.1, s32[1,128]{1,0:T(1,128)} %bitcast.17, bf16[256,1024]{1,0:T(8,128)(2,1)} %wr_in.1, bf16[8,128]{1,0:T(8,128)(2,1)} %bitcast.14, ...), custom_call_target="tpu_custom_call" | custom-call | tf_op jit(solution)/shard_map/block_update/pallas_call | solution.py:615
  111.9 0.0 copy-start
  111.9 2.3 %copy.21 = bf16[16,128,256]{2,1,0:T(8,128)(2,1)} copy(bf16[16,128,256]{2,1,0:T(8,128)(2,1)} %bitcast.10) | data formatting | bytes 2097152
  114.2 0.0 copy-done
  114.2 0.6 copy.22
Async XLA Ops:
  111.9 2.3 %copy-start = (bf16[128,128]{1,0:T(8,128)(2,1)S(1)}, bf16[128,128]{1,0:T(8,128)(2,1)}, u32[]{:S(2)}) copy-start(bf16[128,128]{1,0:T(8,128)(2,1)} %get-tuple-element.5) | copy-start | bytes 98308
